TPU v7x, 32 devices: a whole 2x2x4 slice. The times are simulated.
32 devices in a mesh: seq: 8 (over y, x, core), head: 4 (over z).
Axes of the slice: x: 2, y: 2, z: 4, core: 2. Of those that a mesh axis runs over, the one named last changes fastest.
Arguments:
- hidden_in: bfloat16 [4096, 1536], P('seq', 'head'), may hold values from -6 to 6
- seq_lengths: int32 [8], replicated, may hold values from 1 to 1536, 4096 in all
- norm_gain: float32 [1536], P('head'), may hold values from 0.5 to 1.5
- w_z: bfloat16 [1536, 3072], P(None, 'head'), may hold values from -0.15625 to 0.15625
- w_x: bfloat16 [1536, 3072], P(None, 'head'), may hold values from -0.15625 to 0.15625
- w_bc: bfloat16 [1536, 256], P('head'), may hold values from -0.15625 to 0.15625
- w_dt: bfloat16 [1536, 48], P(None, 'head'), may hold values from -0.15625 to 0.15625
- conv_x_w: float32 [4, 3072], P(None, 'head'), may hold values from -3 to 3
- conv_x_b: float32 [3072], P('head'), may hold values from -3 to 3
- conv_bc_w: float32 [4, 256], replicated, may hold values from -3 to 3
- conv_bc_b: float32 [256], replicated, may hold values from -3 to 3
- dt_bias: float32 [48], P('head'), may hold values from -2 to 0.5
- a_log: float32 [48], P('head'), may hold values from -9 to -3
- d_skip: float32 [48], P('head'), may hold values from 0.5 to 2
- gate_gain: float32 [3072], P('head'), may hold values from 0.5 to 1.5
- w_out: bfloat16 [3072, 1536], P('head'), may hold values from -0.109375 to 0.109375
- cotangent: bfloat16 [4096, 1536], P('seq', 'head'), may hold values from -6 to 6
Outputs:
- layer_out: bfloat16 [4096, 1536], P('seq', 'head')
- grad_in: float32 [4096, 1536], P('seq', 'head')
- grad_norm_gain: float32 [1536], P('head')
- grad_w_z: float32 [1536, 3072], P(None, 'head')
- grad_w_x: float32 [1536, 3072], P(None, 'head')
- grad_w_bc: float32 [1536, 256], P('head')
- grad_w_dt: float32 [1536, 48], P(None, 'head')
- grad_conv_x_w: float32 [4, 3072], P(None, 'head')
- grad_conv_x_b: float32 [3072], P('head')
- grad_conv_bc_w: float32 [4, 256], replicated
- grad_conv_bc_b: float32 [256], replicated
- grad_dt_bias: float32 [48], P('head')
- grad_a_log: float32 [48], P('head')
- grad_d_skip: float32 [48], P('head')
- grad_gate_gain: float32 [3072], P('head')
- grad_w_out: float32 [3072, 1536], P('head')
Inputs may be any that keep to these rules, and one draw needn't show every extreme that they name: `seq_lengths`: the lengths add up to 4096; the largest is exactly 1536.
All inputs are finite; a program needn't handle non-finite values.
Results may differ from a plain program's by a relative error of at most 0.007.
The roundings to bfloat16 on the way count: a program that leaves them out, or rounds other values in their place, can miss the bound.
Values may be sent and summed in bfloat16 or wider, within the bound.
A program may use at most 128 MiB of HBM per device.

v0:
```python
import jax
import jax.numpy as jnp
from jax import lax
from jax.sharding import PartitionSpec as P

D = 1536
HEAD_DIM = 64
STATE = 128
CONV = 4
SPAN = 256
INNER = 3072


epsilon = 1e-05
highest = lax.Precision.HIGHEST


def prefix(part, axis, combine, identity, reverse):
    count = lax.axis_size(axis)
    place = lax.axis_index(axis)
    ahead = count - 1 - place if reverse else place
    gathered = jax.tree.map(lambda a: lax.all_gather(a, axis), part)
    state = jax.tree.map(lambda a, e: jnp.zeros_like(a) + jnp.asarray(e, a.dtype), part, identity)

    def one(hop, state):
        source = count - 1 - hop if reverse else hop
        return combine(
            state, jax.tree.map(lambda a: lax.dynamic_index_in_dim(a, source, 0, False), gathered)
        )

    return lax.fori_loop(0, ahead, one, state)


def passed_along(block, axis, distance):
    devices = range(lax.axis_size(axis))
    route = [(i - distance, i) for i in devices if i - distance in devices]
    return lax.ppermute(block, axis, route)


def segment_of(positions, starts):
    return jnp.sum((positions[:, None] >= starts[None, :]).astype(jnp.int32), axis=1) - 1


def silu_slope(values):
    sigmoid_val = jax.nn.sigmoid(values)
    return sigmoid_val * (1.0 + values * (1.0 - sigmoid_val))


def chain_join(earlier, later):
    return (earlier[0] * later[0], earlier[1] * later[0][:, None, None] + later[1])


def state_prefix(decay, summary, backwards):
    identity = (jnp.ones_like(decay), jnp.zeros_like(summary))
    result = prefix((decay, summary), "seq", chain_join, identity, backwards)
    return result[1]


def span_terms(span_item, lower_tri):
    inner_c, b_rows, c_rows, step_c, cumul_c, seg_rows, seg_prev = span_item
    same_seq = ((seg_rows[:, None] == seg_rows[None, :]) & (lower_tri > 0.5))[None, :, :]
    spread = cumul_c[:, :, None] - cumul_c[:, None, :]
    decay_mat = jnp.where(same_seq, jnp.exp(jnp.where(same_seq, spread, 0.0)), 0.0)
    scores = lax.dot_general(
        c_rows, b_rows, (((1,), (1,)), ((), ())), preferred_element_type=jnp.float32
    )
    mixing = scores[None, :, :] * decay_mat * step_c[:, None, :]
    last_cum = cumul_c[:, SPAN - 1]
    tail_weight = (
        jnp.exp(last_cum[:, None] - cumul_c)
        * (seg_rows == seg_rows[SPAN - 1]).astype(jnp.float32)[None, :]
    )
    head_weight = jnp.exp(cumul_c) * (seg_rows == seg_prev).astype(jnp.float32)[None, :]
    carry_decay = jnp.exp(last_cum) * (seg_rows[SPAN - 1] == seg_prev).astype(jnp.float32)
    return (decay_mat, scores, mixing, tail_weight, head_weight, carry_decay)


def on_device(
    hidden_in,
    seq_lengths,
    norm_gain,
    w_z,
    w_x,
    w_bc,
    w_dt,
    conv_x_w,
    conv_x_b,
    conv_bc_w,
    conv_bc_b,
    dt_bias,
    a_log,
    d_skip,
    gate_gain,
    w_out,
    cotangent,
):
    tokens_here = hidden_in.shape[0]
    heads_here = dt_bias.shape[0]
    inner_here = w_z.shape[1]
    spans = tokens_here // SPAN
    first_pos = lax.axis_index("seq") * tokens_here
    starts = jnp.cumsum(seq_lengths) - seq_lengths
    segment = segment_of(first_pos + jnp.arange(tokens_here, dtype=jnp.int32), starts)
    edge_segment = segment_of(
        first_pos - (CONV - 1) + jnp.arange(CONV - 1, dtype=jnp.int32), starts
    )
    span_prev = segment_of(first_pos - 1 + jnp.arange(spans, dtype=jnp.int32) * SPAN, starts)
    row_ids = jnp.arange(SPAN)
    lower_tri = (row_ids[:, None] >= row_ids[None, :]).astype(jnp.float32)
    inputs = hidden_in.astype(jnp.float32)
    squares = lax.psum(jnp.sum(inputs * inputs, axis=1), "head")
    scale_in = lax.rsqrt(squares / D + epsilon)
    normed = (inputs * scale_in[:, None] * norm_gain).astype(jnp.bfloat16)
    gathered, bc_weight = (
        lax.all_gather(normed, "head", axis=1, tiled=True),
        lax.all_gather(w_bc, "head", axis=0, tiled=True),
    )
    gate_pre = jnp.dot(gathered, w_z, preferred_element_type=jnp.float32)
    x_part = jnp.dot(gathered, w_x, preferred_element_type=jnp.float32)
    bc_part = jnp.dot(gathered, bc_weight, preferred_element_type=jnp.float32)
    conv_in = jnp.concatenate([x_part, bc_part], axis=1).astype(jnp.bfloat16)
    step_raw = jnp.dot(gathered, w_dt, preferred_element_type=jnp.float32)
    edge_rows = passed_along(conv_in[tokens_here - (CONV - 1) :], "seq", 1)
    padded = jnp.concatenate([edge_rows, conv_in], axis=0).astype(jnp.float32)
    seg_padded = jnp.concatenate([edge_segment, segment])
    conv_weight = jnp.concatenate([conv_x_w, conv_bc_w], axis=1)
    conv_bias = jnp.concatenate([conv_x_b, conv_bc_b])
    tap_masks = [
        (seg_padded[offset : offset + tokens_here] == segment).astype(jnp.float32)[:, None]
        for offset in range(CONV)
    ]
    conv_out = jnp.zeros(conv_in.shape, jnp.float32) + conv_bias[None, :]
    for offset in range(CONV):
        conv_out = (
            conv_out
            + conv_weight[offset] * padded[offset : offset + tokens_here] * tap_masks[offset]
        )
    activated = jax.nn.silu(conv_out)
    inner_vals = activated[:, :inner_here].astype(jnp.bfloat16)
    b_vals = activated[:, inner_here : inner_here + STATE].astype(jnp.bfloat16)
    c_vals = activated[:, inner_here + STATE :].astype(jnp.bfloat16)
    step_pre = step_raw + dt_bias
    step_size = jax.nn.softplus(step_pre)
    rates = jnp.exp(a_log)
    log_decay = -rates * step_size
    decay_heads = log_decay.reshape(spans, SPAN, heads_here).transpose(0, 2, 1)
    step_heads = step_size.reshape(spans, SPAN, heads_here).transpose(0, 2, 1)
    cumul = jnp.einsum("ij,chj->chi", lower_tri, decay_heads, precision=highest)
    inner_spans = inner_vals.reshape(spans, SPAN, heads_here, HEAD_DIM).transpose(0, 2, 1, 3)
    c_spans = c_vals.reshape(spans, SPAN, STATE)
    per_span = (
        inner_spans,
        b_vals.reshape(spans, SPAN, STATE),
        c_spans,
        step_heads,
        cumul,
        segment.reshape(spans, SPAN),
        span_prev,
    )

    def forward_span(span_item):
        decay_mat, scores, mixing, tail_weight, head_weight, carry_decay = span_terms(
            span_item, lower_tri
        )
        inner_c = span_item[0]
        y_inside = jnp.einsum(
            "hij,hjp->hip", mixing.astype(jnp.bfloat16), inner_c, preferred_element_type=jnp.float32
        )
        loaded = (
            span_item[1].astype(jnp.float32)[None, :, :] * (tail_weight * span_item[3])[:, :, None]
        ).astype(jnp.bfloat16)
        local_state = jnp.einsum(
            "hjn,hjp->hnp", loaded, inner_c, preferred_element_type=jnp.float32
        )
        return (y_inside, local_state, carry_decay, head_weight)

    y_inside, local_states, carry_decay, head_weight = lax.map(forward_span, per_span)

    def advance(state_carry, span_item):
        running, factor = state_carry
        local_c, decay_c = span_item
        return ((decay_c[:, None, None] * running + local_c, decay_c * factor), (running, factor))

    zero_state = jnp.zeros((heads_here, STATE, HEAD_DIM), jnp.float32)
    unit_decay = jnp.ones((heads_here,), jnp.float32)
    (device_state, device_decay), (local_in, local_factor) = lax.scan(
        advance, (zero_state, unit_decay), (local_states, carry_decay)
    )
    incoming = state_prefix(device_decay, device_state, False)
    state_in = local_in + local_factor[:, :, None, None] * incoming
    state_low = state_in.astype(jnp.bfloat16)
    c_weighted = (c_spans.astype(jnp.float32)[:, None, :, :] * head_weight[:, :, :, None]).astype(
        jnp.bfloat16
    )
    y_outside = jnp.einsum(
        "chin,chnp->chip", c_weighted, state_low, preferred_element_type=jnp.float32
    )
    skip_rep = jnp.repeat(d_skip, HEAD_DIM)
    mixed_out = (y_inside + y_outside).transpose(0, 2, 1, 3).reshape(
        tokens_here, inner_here
    ) + inner_vals.astype(jnp.float32) * skip_rep
    gate_act = jax.nn.silu(gate_pre)
    gated = mixed_out * gate_act
    gate_squares = lax.psum(jnp.sum(gated * gated, axis=1), "head")
    scale_gate = lax.rsqrt(gate_squares / INNER + epsilon)
    gate_normed = (gated * scale_gate[:, None] * gate_gain).astype(jnp.bfloat16)
    partial_value = jnp.dot(gate_normed, w_out, preferred_element_type=jnp.float32)
    mixed_sum = lax.psum_scatter(partial_value, "head", scatter_dimension=1, tiled=True)
    layer_out = (inputs + mixed_sum).astype(jnp.bfloat16)
    grad_full = lax.all_gather(cotangent, "head", axis=1, tiled=True)
    grad_gate_normed = lax.dot_general(
        grad_full, w_out, (((1,), (1,)), ((), ())), preferred_element_type=jnp.float32
    )
    grad_w_out = lax.dot_general(
        gate_normed, grad_full, (((0,), (0,)), ((), ())), preferred_element_type=jnp.float32
    )
    grad_gate_gain = jnp.sum(grad_gate_normed * gated * scale_gate[:, None], axis=0)
    grad_scaled = grad_gate_normed * gate_gain
    gate_inner = lax.psum(jnp.sum(grad_scaled * gated, axis=1), "head")
    grad_gated = (
        scale_gate[:, None] * grad_scaled - gated * (scale_gate**3 * gate_inner / INNER)[:, None]
    )
    grad_mixed = (grad_gated * gate_act).astype(jnp.bfloat16)
    grad_gate_pre = (grad_gated * mixed_out * silu_slope(gate_pre)).astype(jnp.bfloat16)
    grad_d_skip = jnp.sum(
        (grad_mixed.astype(jnp.float32) * inner_vals.astype(jnp.float32)).reshape(
            tokens_here, heads_here, HEAD_DIM
        ),
        axis=(0, 2),
    )
    grad_spans = grad_mixed.reshape(spans, SPAN, heads_here, HEAD_DIM).transpose(0, 2, 1, 3)
    from_inter = jnp.einsum(
        "chin,chip->chnp", c_weighted, grad_spans, preferred_element_type=jnp.float32
    )

    def retreat(state_carry, span_item):
        running, factor = state_carry
        local_c, decay_c = span_item
        current = local_c + decay_c[:, None, None] * running
        product = decay_c * factor
        return ((current, product), (current, product))

    (device_grad, device_reach), (local_grad, local_reach) = lax.scan(
        retreat, (zero_state, unit_decay), (from_inter, carry_decay), reverse=True
    )
    beyond = state_prefix(device_reach, device_grad, True)
    grad_state_in = local_grad + local_reach[:, :, None, None] * beyond
    grad_local_states = jnp.concatenate([grad_state_in[1:], beyond[None]], axis=0)
    grad_carry_decay = jnp.sum(grad_local_states * state_in, axis=(2, 3))

    def backward_span(span_item):
        span_base = span_item[:7]
        inner_c, b_rows, c_rows, step_c = (span_base[0], span_base[1], span_base[2], span_base[3])
        grad_y, grad_state, state_c, grad_decay = (
            span_item[7],
            span_item[8],
            span_item[9],
            span_item[10],
        )
        decay_mat, scores, mixing, tail_weight, head_weight, carry_decay = span_terms(
            span_base, lower_tri
        )
        grad_mixing = jnp.einsum(
            "hip,hjp->hij", grad_y, inner_c, preferred_element_type=jnp.float32
        )
        grad_inner = jnp.einsum(
            "hij,hip->hjp", mixing.astype(jnp.bfloat16), grad_y, preferred_element_type=jnp.float32
        )
        related = grad_mixing * mixing
        grad_cum = jnp.sum(related, axis=2) - jnp.sum(related, axis=1)
        grad_scores = jnp.sum(grad_mixing * decay_mat * step_c[:, None, :], axis=0)
        grad_step = jnp.sum(grad_mixing * decay_mat * scores[None, :, :], axis=1)
        b_float = b_rows.astype(jnp.float32)
        c_float = c_rows.astype(jnp.float32)
        grad_c = jnp.dot(grad_scores, b_float, precision=highest)
        grad_b = lax.dot_general(grad_scores, c_float, (((0,), (0,)), ((), ())), precision=highest)
        loading = tail_weight * step_c
        loaded = (b_float[None, :, :] * loading[:, :, None]).astype(jnp.bfloat16)
        grad_loaded = jnp.einsum(
            "hjp,hnp->hjn", inner_c, grad_state, preferred_element_type=jnp.float32
        )
        grad_inner = grad_inner + jnp.einsum(
            "hjn,hnp->hjp", loaded, grad_state, preferred_element_type=jnp.float32
        )
        grad_loading = jnp.sum(grad_loaded * b_float[None, :, :], axis=2)
        grad_b = grad_b + jnp.einsum("hjn,hj->jn", grad_loaded, loading, precision=highest)
        tail_term = grad_loading * loading
        grad_cum = grad_cum - tail_term
        grad_last = jnp.sum(tail_term, axis=1) + grad_decay * carry_decay
        grad_step = grad_step + grad_loading * tail_weight
        grad_weighted = jnp.einsum(
            "hip,hnp->hin", grad_y, state_c, preferred_element_type=jnp.float32
        )
        grad_head = jnp.sum(grad_weighted * c_float[None, :, :], axis=2)
        grad_c = grad_c + jnp.einsum("hin,hi->in", grad_weighted, head_weight, precision=highest)
        grad_cum = grad_cum + grad_head * head_weight
        grad_cum = grad_cum.at[:, SPAN - 1].add(grad_last)
        grad_log = jnp.einsum("ij,hi->hj", lower_tri, grad_cum, precision=highest)
        return (grad_inner, grad_b, grad_c, grad_step, grad_log)

    back_items = per_span + (
        grad_spans,
        grad_local_states.astype(jnp.bfloat16),
        state_low,
        grad_carry_decay,
    )
    grad_inner_s, grad_b_s, grad_c_s, grad_step_s, grad_log_s = lax.map(backward_span, back_items)
    grad_inner = (
        grad_inner_s.transpose(0, 2, 1, 3).reshape(tokens_here, inner_here)
        + grad_mixed.astype(jnp.float32) * skip_rep
    )
    grad_log_decay = grad_log_s.transpose(0, 2, 1).reshape(tokens_here, heads_here)
    grad_step_total = (
        grad_step_s.transpose(0, 2, 1).reshape(tokens_here, heads_here) - grad_log_decay * rates
    )
    grad_a_log = jnp.sum(grad_log_decay * log_decay, axis=0)
    grad_step_pre = grad_step_total * jax.nn.sigmoid(step_pre)
    grad_dt_bias = jnp.sum(grad_step_pre, axis=0)
    grad_step_raw = grad_step_pre.astype(jnp.bfloat16)
    grad_bc = lax.psum(
        jnp.concatenate(
            [grad_b_s.reshape(tokens_here, STATE), grad_c_s.reshape(tokens_here, STATE)], axis=1
        ),
        "head",
    )
    grad_conv = jnp.concatenate([grad_inner, grad_bc], axis=1) * silu_slope(conv_out)
    grad_conv_bias = jnp.sum(grad_conv, axis=0)
    grad_conv_weight = jnp.stack(
        [
            jnp.sum(grad_conv * padded[offset : offset + tokens_here] * tap_masks[offset], axis=0)
            for offset in range(CONV)
        ]
    )
    grad_padded = jnp.zeros(padded.shape, jnp.float32)
    for offset in range(CONV):
        grad_padded = grad_padded + jnp.pad(
            conv_weight[offset] * grad_conv * tap_masks[offset],
            ((offset, CONV - 1 - offset), (0, 0)),
        )
    returned = passed_along(grad_padded[: CONV - 1], "seq", -1)
    grad_conv_in = (
        grad_padded[CONV - 1 :] + jnp.pad(returned, ((tokens_here - (CONV - 1), 0), (0, 0)))
    ).astype(jnp.bfloat16)
    grad_x_pre = grad_conv_in[:, :inner_here]
    grad_bc_pre = grad_conv_in[:, inner_here:]
    contract_rows = (((0,), (0,)), ((), ()))
    contract_cols = (((1,), (1,)), ((), ()))
    grad_w_z = lax.dot_general(
        gathered, grad_gate_pre, contract_rows, preferred_element_type=jnp.float32
    )
    grad_w_x = lax.dot_general(
        gathered, grad_x_pre, contract_rows, preferred_element_type=jnp.float32
    )
    grad_w_dt = lax.dot_general(
        gathered, grad_step_raw, contract_rows, preferred_element_type=jnp.float32
    )
    grad_w_bc = lax.dot_general(
        normed, grad_bc_pre, contract_rows, preferred_element_type=jnp.float32
    )
    partial_back = lax.dot_general(
        grad_gate_pre, w_z, contract_cols, preferred_element_type=jnp.float32
    )
    partial_back = partial_back + lax.dot_general(
        grad_x_pre, w_x, contract_cols, preferred_element_type=jnp.float32
    )
    partial_back = partial_back + lax.dot_general(
        grad_step_raw, w_dt, contract_cols, preferred_element_type=jnp.float32
    )
    grad_normed = lax.psum_scatter(partial_back, "head", scatter_dimension=1, tiled=True)
    grad_normed = grad_normed + lax.dot_general(
        grad_bc_pre, w_bc, contract_cols, preferred_element_type=jnp.float32
    )
    grad_scaled_in = grad_normed * norm_gain
    grad_norm_gain = jnp.sum(grad_normed * inputs * scale_in[:, None], axis=0)
    norm_inner = lax.psum(jnp.sum(grad_scaled_in * inputs, axis=1), "head")
    grad_in = (
        cotangent.astype(jnp.float32)
        + scale_in[:, None] * grad_scaled_in
        - inputs * (scale_in**3 * norm_inner / D)[:, None]
    )
    summed = lax.psum(
        (
            grad_norm_gain,
            grad_w_z,
            grad_w_x,
            grad_w_bc,
            grad_w_dt,
            grad_conv_weight[:, :inner_here],
            grad_conv_bias[:inner_here],
            grad_conv_weight[:, inner_here:],
            grad_conv_bias[inner_here:],
            grad_dt_bias,
            grad_a_log,
            grad_d_skip,
            grad_gate_gain,
            grad_w_out,
        ),
        "seq",
    )
    return (
        layer_out,
        grad_in,
        summed[0],
        summed[1],
        summed[2],
        summed[3],
        summed[4],
        summed[5],
        summed[6],
        summed[7],
        summed[8],
        summed[9],
        summed[10],
        summed[11],
        summed[12],
        summed[13],
    )


def solution(mesh):
    placed = (
        P("seq", "head"),
        P(),
        P("head"),
        P(None, "head"),
        P(None, "head"),
        P("head", None),
        P(None, "head"),
        P(None, "head"),
        P("head"),
        P(),
        P(),
        P("head"),
        P("head"),
        P("head"),
        P("head"),
        P("head", None),
        P("seq", "head"),
    )
    return jax.shard_map(
        on_device,
        mesh=mesh,
        in_specs=placed,
        out_specs=(
            P("seq", "head"),
            P("seq", "head"),
            P("head"),
            P(None, "head"),
            P(None, "head"),
            P("head", None),
            P(None, "head"),
            P(None, "head"),
            P("head"),
            P(),
            P(),
            P("head"),
            P("head"),
            P("head"),
            P("head"),
            P("head", None),
        ),
        check_vma=False,
    )
```

profile of v0, /device:TPU:0, one launch (start us, length us, event | category | flops | bytes accessed | tf_op | source)
XLA Modules:
  0.0 749.0 jit_solution(9070033676555361686)
XLA Ops:
  8.6 13.5 %psum.133 = f32[512]{0:T(512)S(1)} all-reduce(f32[512]{0:T(512)S(1)} %fusion.107), channel_id=1, replica_groups=mesh['seq'=8,'head'=4] {'head'}, use_global_device_ids=true, to_apply=%region_1.2 | all-reduce | flops 512 | bytes 4096 | tf_op jit(solution)/shard_map/psum | solution.py:111
  31.2 29.2 %all_gather.34 = bf16[1536,256]{1,0:T(8,128)(2,1)} all-gather(bf16[384,256]{1,0:T(8,128)(2,1)} %param.36), channel_id=1, replica_groups=mesh['seq'=8,'head'=4] {'head'}, dimensions={0}, use_global_device_ids=true | all-gather | bytes 983040 | tf_op jit(solution)/shard_map/all_gather | solution.py:116
  60.4 10.5 %all-gather.9.cloned.1.call-done = bf16[512,1536]{1,0:T(8,128)(2,1)} async-done(((bf16[512,384]{1,0:T(8,128)(2,1)}), bf16[512,1536]{1,0:T(8,128)(2,1)}) %all-gather.9.cloned.1.call-update) | async-done | bytes 1572880 | tf_op jit(solution)/shard_map/all_gather | solution.py:115
  70.9 2.6 compare_select_fusion
  74.0 3.7 convolution_convert_fusion
  82.7 2.9 multiply_convert_fusion.13
  89.8 2.9 reshape.421
  96.3 23.8 %while.107 = (s32[]{:T(128)}, f32[2,12,256,64]{2,3,1,0:T(8,128)}, f32[2,12,128,64]{2,3,1,0:T(8,128)}, f32[2,12]{1,0:T(2,128)S(1)}, f32[2,12,256]{2,1,0:T(8,128)S...) while((s32[]{:T(128)}, f32[2,12,256,64]{2,3,1,0:T(8,128)}, ...), condition=%wide.region_7.8_spmd.clone, body=%wide.region_6.7_spmd.clone.sunk | while | flops 173650960 | bytes 3251719 | solution.py:177
  105.1 3.1 fusion.215
  114.5 2.4 fusion.216
  116.9 3.1 fusion.215
  121.5 7.6 %while.109 = (s32[]{:T(128)}, f32[12,128,64]{2,1,0:T(8,128)S(1)}, f32[12]{0:T(128)S(1)}, f32[2,12,128,64]{3,2,1,0:T(8,128)}, f32[2,12]{1,0:T(2,128)S(1)}, /*inde...) while((s32[]{:T(128)}, f32[12,128,64]{2,1,0:T(8,128)S(1)}, ...), condition=%wide.region_9.10_spmd.clone, body=%wide.region_8.9_spmd.clone.sunk | while | flops 393243 | bytes 5505565 | solution.py:186
  134.6 14.6 %all-reduce.5 = f32[96]{0:T(128)S(1)} all-reduce(f32[96]{0:T(128)S(1)} %dynamic-update-slice.6), channel_id=2, replica_groups=mesh['seq'=8,'head'=4] {'seq'}, use_global_device_ids=true, to_apply=%add.5 | all-reduce | flops 96 | bytes 768
  149.9 15.1 %all-gather.13.cloned.1.call-done = f32[96,128,64]{1,2,0:T(8,128)} async-done(((f32[12,128,64]{1,2,0:T(8,128)}), f32[96,128,64]{1,2,0:T(8,128)}) %all-gather.13.cloned.1.call-update) | async-done | bytes 3145744 | tf_op jit(solution)/shard_map/all_gather | solution.py:22
  173.0 3.3 copy.257
  176.3 5.2 multiply_reduce_fusion.15
  181.5 12.2 %psum.134 = f32[512]{0:T(512)S(1)} all-reduce(f32[512]{0:T(512)S(1)} %get-tuple-element.1391), channel_id=1, replica_groups=mesh['seq'=8,'head'=4] {'head'}, use_global_device_ids=true, to_apply=%region_13.14 | all-reduce | flops 512 | bytes 4096 | tf_op jit(solution)/shard_map/psum | solution.py:204
  193.7 9.7 %all-gather.11.cloned.1.call-done = bf16[512,1536]{1,0:T(8,128)(2,1)} async-done(((bf16[512,384]{1,0:T(8,128)(2,1)}), bf16[512,1536]{1,0:T(8,128)(2,1)}) %all-gather.11.cloned.1.call-update) | async-done | bytes 1572880 | tf_op jit(solution)/shard_map/all_gather | solution.py:210
  203.4 5.8 multiply_reduce_fusion.12
  209.2 10.0 %psum.135 = f32[512]{0:T(512)S(1)} all-reduce(f32[512]{0:T(512)S(1)} %get-tuple-element.1243), channel_id=1, replica_groups=mesh['seq'=8,'head'=4] {'head'}, use_global_device_ids=true, to_apply=%region_16.17 | all-reduce | flops 512 | bytes 4096 | tf_op jit(solution)/shard_map/psum | solution.py:219
  219.3 5.8 fusion.98
  227.6 4.3 fusion.93
  233.3 4.5 while.110
  243.0 26.8 %all-reduce.6 = f32[96]{0:T(128)S(1)} all-reduce(f32[96]{0:T(128)S(1)} %dynamic-update-slice.7), channel_id=4, replica_groups=mesh['seq'=8,'head'=4] {'seq'}, use_global_device_ids=true, to_apply=%add.6 | all-reduce | flops 96 | bytes 768
  269.9 4.4 fusion.147
  274.3 8.5 %all-gather.15.cloned.1.call-done = f32[96,128,64]{1,2,0:T(8,128)} async-done(((f32[12,128,64]{1,2,0:T(8,128)}), f32[96,128,64]{1,2,0:T(8,128)}) %all-gather.15.cloned.1.call-update) | async-done | bytes 3145744 | tf_op jit(solution)/shard_map/all_gather | solution.py:22
  282.9 10.9 %while.106 = (s32[]{:T(128)}, f32[12,128,64]{2,1,0:T(8,128)S(1)}, s32[]{:T(128)}, f32[8,12]{1,0:T(8,128)S(1)}, f32[8,12,128,64]{2,3,1,0:T(8,128)}, /*index=5*/s32[]{:T(128)}, s32[]{:T(128)}, s32[]{:T(128)}, s32[]{:T(128)}) while((s32[]{:T(128)}, f32[12,128,64]{2,1,0:T(8,128)S(1)}, s32[]{:T(128)}, f32[8,12]{1,0:T(8,128)S(1)}, ...), condition=%wide.region_20.21_spmd, body=%wide.region_19.20_spmd.sunk | while | flops 196614 | bytes 2752811 | solution.py:31
  299.9 44.1 %while.108 = (s32[]{:T(128)}, f32[2,12,256,64]{2,3,1,0:T(8,128)}, f32[2,256,128]{2,1,0:T(8,128)}, f32[2,256,128]{2,1,0:T(8,128)}, f32[2,12,256]{2,1,0:T(8,128)},...) while((s32[]{:T(128)}, f32[2,12,256,64]{2,3,1,0:T(8,128)}, ...), condition=%wide.region_31.32_spmd.clone.clone, body=%wide.region_23.31_spmd.clone.clone.sunk | while | flops 599427136 | bytes 24932688 | solution.py:307
  312.0 3.2 fusion.233
  334.0 3.2 fusion.233
  344.8 2.6 copy.269
  348.7 3.2 copy.270
  354.1 2.9 fusion.97
  357.0 34.6 %all-reduce.12.cloned.1.call-done = f32[512,256]{1,0:T(8,128)} async-done(((f32[512,256]{1,0:T(8,128)}), f32[512,256]{1,0:T(8,128)}) %all-reduce.12.cloned.1.call-update) | async-done | bytes 524304 | tf_op jit(solution)/shard_map/psum | solution.py:320
  391.6 3.7 multiply_reduce_fusion.11
  405.9 4.7 fusion.139
  412.6 3.6 fusion.148
  416.2 3.7 fusion.138
  421.9 3.6 fusion.115
  426.5 39.1 %reduce-scatter.5.cloned.1.call-done = f32[512,384]{1,0:T(8,128)} async-done(((f32[512,1536]{1,0:T(8,128)}), f32[512,384]{1,0:T(8,128)}) %reduce-scatter.5.cloned.1.call-update) | async-done | bytes 786448 | tf_op jit(solution)/shard_map/reduce_scatter | solution.py:369
  467.2 25.1 %all-reduce.7 = (f32[384]{0:T(512)}, f32[4,768]{1,0:T(4,128)}, f32[768]{0:T(1024)}, f32[4,256]{1,0:T(4,128)}, f32[256]{0:T(256)}, /*index=5*/f32[12]{0:T(128)}, f32[12]{0:T(128)}, f32[12]{0:T(128)}, f32[768]{0:T(1024)}) all-reduce(f32[384]{0:T(512)S(1)} %get-tuple-element.1245, ...), channel_id=1, replica_groups=mesh['seq'=8,'head'=4] {'seq'}, use_global_device_ids=true, to_apply=%region_37.38 | all-reduce | flops 6308 | bytes 50464 | tf_op jit(solution)/shard_map/psum | solution.py:381
  492.3 11.5 %psum.137 = f32[512]{0:T(512)S(1)} all-reduce(f32[512]{0:T(512)S(1)} %get-tuple-element.1246), channel_id=1, replica_groups=mesh['seq'=8,'head'=4] {'head'}, use_global_device_ids=true, to_apply=%region_35.36 | all-reduce | flops 512 | bytes 4096 | tf_op jit(solution)/shard_map/psum | solution.py:375
  503.9 24.6 %reduce-scatter.3.cloned.1.call-done = f32[512,384]{1,0:T(8,128)} async-done(((f32[512,1536]{1,0:T(8,128)}), f32[512,384]{1,0:T(8,128)}) %reduce-scatter.3.cloned.1.call-update) | async-done | bytes 786448 | tf_op jit(solution)/shard_map/reduce_scatter | solution.py:208
  528.4 2.5 fusion.112
  530.9 197.8 %all-reduce.14.cloned.1.call-done = (f32[1536,768]{1,0:T(8,128)}, f32[1536,768]{1,0:T(8,128)}, f32[384,256]{1,0:T(8,128)}, f32[1536,12]{0,1:T(8,128)}, f32[768,1536]{1,0:T(8,128)}) async-done(((f32[1536,768]{1,0:T(8,128)}, f32[1536,768]{1,0:T(8,128)}, f32[384,256]{1,0:T(8,128)}, f32[1536,12]{0,1:T(8,128)}, f32[768,1536]{1,0:T(8,128)}), (f32[1536,768]{1,0:T(8,128)}, f32[1536,768]{1,0:T(8,128)}, ...) | async-done | bytes 14622736 | tf_op jit(solution)/shard_map/psum | solution.py:381
  728.7 5.2 copy.454
  733.9 2.4 copy.455
  738.4 2.4 copy.458
  (484 shorter events, 147.3 us)
Async XLA Ops:
  7.2 169.1 %copy-start = (bf16[1536,768]{1,0:T(8,128)(2,1)S(1)}, bf16[1536,768]{1,0:T(8,128)(2,1)}, u32[]{:S(2)}) copy-start(bf16[1536,768]{1,0:T(8,128)(2,1)} %param.34) | copy-start | bytes 7077892
  7.2 63.7 %copy-start.51 = (bf16[1536,12]{0,1:T(8,128)(2,1)S(1)}, bf16[1536,12]{0,1:T(8,128)(2,1)}, u32[]{:S(2)}) copy-start(bf16[1536,12]{0,1:T(8,128)(2,1)} %param.37) | copy-start | bytes 110596
  7.2 63.7 %copy-start.93 = (f32[12]{0:T(128)S(1)}, f32[12]{0:T(128)}, u32[]{:S(2)}) copy-start(f32[12]{0:T(128)} %param.42) | copy-start | bytes 148
  7.2 63.6 %all-gather.9.cloned.1.call-start = ((), (), s32[]{:S(2)}) async-start(), calls=%async_computation.2 | async-start | bytes 1966080 | tf_op jit(solution)/shard_map/all_gather | solution.py:115
  24.6 140.4 %all-gather.13.cloned.1.call-start = ((), (), s32[]{:S(2)}) async-start(), calls=%async_computation.7 | async-start | bytes 3538944 | tf_op jit(solution)/shard_map/all_gather | solution.py:22
  31.2 51.5 %copy-start.80 = (f32[512]{0:T(512)}, f32[512]{0:T(512)S(1)}, u32[]{:S(2)}) copy-start(f32[512]{0:T(512)S(1)} %get-tuple-element.1420) | copy-start | bytes 6148
  31.2 51.5 %copy-start.82 = (f32[512]{0:T(512)}, f32[512]{0:T(512)S(1)}, u32[]{:S(2)}) copy-start(f32[512]{0:T(512)S(1)} %get-tuple-element.1421) | copy-start | bytes 6148
  31.2 51.5 %copy-start.84 = (f32[512]{0:T(512)}, f32[512]{0:T(512)S(1)}, u32[]{:S(2)}) copy-start(f32[512]{0:T(512)S(1)} %get-tuple-element.1422) | copy-start | bytes 6148
  31.2 51.5 %copy-start.68 = (f32[1,1024]{1,0:T(1,128)}, f32[1,1024]{1,0:T(1,128)S(1)}, u32[]{:S(2)}) copy-start(f32[1,1024]{1,0:T(1,128)S(1)} %get-tuple-element.1416) | copy-start | bytes 12292
  31.2 51.5 %copy-start.70 = (f32[1,1024]{1,0:T(1,128)}, f32[1,1024]{1,0:T(1,128)S(1)}, u32[]{:S(2)}) copy-start(f32[1,1024]{1,0:T(1,128)S(1)} %get-tuple-element.1417) | copy-start | bytes 12292
  31.2 51.5 %copy-start.72 = (f32[1,1024]{1,0:T(1,128)}, f32[1,1024]{1,0:T(1,128)S(1)}, u32[]{:S(2)}) copy-start(f32[1,1024]{1,0:T(1,128)S(1)} %get-tuple-element.1418) | copy-start | bytes 12292
  31.2 51.5 %copy-start.74 = (f32[1,1024]{1,0:T(1,128)}, f32[1,1024]{1,0:T(1,128)S(1)}, u32[]{:S(2)}) copy-start(f32[1,1024]{1,0:T(1,128)S(1)} %get-tuple-element.1419) | copy-start | bytes 12292
  78.6 2.6 collective-permute-start
  129.1 4.6 copy-start.20
  130.1 73.3 %all-gather.11.cloned.1.call-start = ((), (), s32[]{:S(2)}) async-start(), calls=%async_computation.4 | async-start | bytes 1966080 | tf_op jit(solution)/shard_map/all_gather | solution.py:210
  130.9 152.0 %all-gather.15.cloned.1.call-start = ((), (), s32[]{:S(2)}) async-start(), calls=%async_computation.8 | async-start | bytes 3538944 | tf_op jit(solution)/shard_map/all_gather | solution.py:22
  131.8 87.5 %copy-start.66 = (f32[768]{0:T(1024)}, f32[768]{0:T(1024)S(1)}, u32[]{:S(2)}) copy-start(f32[768]{0:T(1024)S(1)} %mul.806) | copy-start | bytes 9220
  176.3 27.1 %copy-start.63 = (f32[768]{0:T(1024)S(1)}, f32[768]{0:T(1024)}, u32[]{:S(2)}) copy-start(f32[768]{0:T(1024)} %param.45) | copy-start | bytes 9220
  193.7 25.6 %copy-start.78 = (f32[512]{0:T(512)}, f32[512]{0:T(512)S(1)}, u32[]{:S(2)}) copy-start(f32[512]{0:T(512)S(1)} %add_rsqrt_fusion) | copy-start | bytes 6148
  227.6 5.7 copy-start.8
  238.8 152.7 %all-reduce.12.cloned.1.call-start = ((), (), s32[]{:S(2)}) async-start(), calls=%async_computation.5 | async-start | bytes 1048576 | tf_op jit(solution)/shard_map/psum | solution.py:320
  312.0 4.5 copy-start.11
  312.0 4.5 copy-start.18
  334.0 4.4 copy-start.18
  348.6 5.2 copy-start.47
  348.6 5.2 copy-start.60
  348.7 5.2 copy-start.94
  348.7 5.4 copy-start.16
  348.7 5.4 copy-start.67
  353.8 37.8 %copy-start.3 = (f32[515,1024]{1,0:T(8,128)S(1)}, f32[515,1024]{1,0:T(8,128)}, u32[]{:S(2)}) copy-start(f32[515,1024]{1,0:T(8,128)} %copy-done.2) | copy-start | bytes 6328324
  353.8 37.8 %copy-start.81 = (f32[512]{0:T(512)S(1)}, f32[512]{0:T(512)}, u32[]{:S(2)}) copy-start(f32[512]{0:T(512)} %copy-done.80) | copy-start | bytes 6148
  353.8 37.8 %copy-start.83 = (f32[512]{0:T(512)S(1)}, f32[512]{0:T(512)}, u32[]{:S(2)}) copy-start(f32[512]{0:T(512)} %copy-done.82) | copy-start | bytes 6148
  353.8 37.8 %copy-start.85 = (f32[512]{0:T(512)S(1)}, f32[512]{0:T(512)}, u32[]{:S(2)}) copy-start(f32[512]{0:T(512)} %copy-done.84) | copy-start | bytes 6148
  353.8 111.8 %reduce-scatter.5.cloned.1.call-start = ((), (), s32[]{:S(2)}) async-start(), calls=%async_computation.6 | async-start | bytes 3932160 | tf_op jit(solution)/shard_map/reduce_scatter | solution.py:369
  396.1 3.1 collective-permute-start.1
  404.5 124.0 %reduce-scatter.3.cloned.1.call-start = ((), (), s32[]{:S(2)}) async-start(), calls=%async_computation.3 | async-start | bytes 3932160 | tf_op jit(solution)/shard_map/reduce_scatter | solution.py:208
  410.6 318.1 %all-reduce.14.cloned.1.call-start = ((), (), s32[]{:S(2)}) async-start(), calls=%async_computation.9 | async-start | bytes 29294592 | tf_op jit(solution)/shard_map/psum | solution.py:381
  416.2 4.7 copy-start.27
  425.5 40.1 %copy-start.22 = (bf16[512,384]{1,0:T(8,128)(2,1)S(1)}, bf16[512,384]{1,0:T(8,128)(2,1)}, u32[]{:S(2)}) copy-start(bf16[512,384]{1,0:T(8,128)(2,1)} %param.31) | copy-start | bytes 1179652
  425.5 40.1 %copy-start.43 = (bf16[384,256]{1,0:T(8,128)(2,1)S(1)}, bf16[384,256]{1,0:T(8,128)(2,1)}, u32[]{:S(2)}) copy-start(bf16[384,256]{1,0:T(8,128)(2,1)} %param.36) | copy-start | bytes 589828
  425.5 40.1 %copy-start.77 = (f32[512]{0:T(512)S(1)}, f32[512]{0:T(512)}, u32[]{:S(2)}) copy-start(f32[512]{0:T(512)} %copy-done.76) | copy-start | bytes 6148
  425.5 40.1 %copy-start.86 = (f32[384]{0:T(512)S(1)}, f32[384]{0:T(512)}, u32[]{:S(2)}) copy-start(f32[384]{0:T(512)} %param.33) | copy-start | bytes 4612
  425.6 41.7 %copy-start.92 = (f32[768]{0:T(1024)S(1)}, f32[768]{0:T(1024)}, u32[]{:S(2)}) copy-start(f32[768]{0:T(1024)} %get-tuple-element.1242) | copy-start | bytes 9220
  425.6 78.3 %copy-start.88 = (f32[512]{0:T(512)S(1)}, f32[512]{0:T(512)}, u32[]{:S(2)}) copy-start(f32[512]{0:T(512)} %copy-done.87) | copy-start | bytes 6148
  425.6 102.8 %copy-start.37 = (bf16[512,384]{1,0:T(8,128)(2,1)S(1)}, bf16[512,384]{1,0:T(8,128)(2,1)}, u32[]{:S(2)}) copy-start(bf16[512,384]{1,0:T(8,128)(2,1)} %param.47) | copy-start | bytes 1179652
  728.7 5.2 copy-start.26
  728.7 9.7 %slice-start = ((s8[4718592]{0:T(1024)(128)(4,1)}), s8[4194304]{0:T(1024)(128)(4,1)S(1)}, s32[]{:S(2)}) async-start(s8[4718592]{0:T(1024)(128)(4,1)} %bitcast.365), calls=%async_computation.10 | async-start | bytes 8388608
  733.9 4.5 slice-start.1
  (73 other events, 180.9 us)
Sparse Core Ops, SparseCore 0:
  24.7 46.1 all-gather.8
  130.3 34.6 all-gather.12
  166.5 36.8 all-gather.10
  239.0 43.8 all-gather.14
  353.9 37.6 all-reduce.11
  404.6 60.9 reduce-scatter.4
  467.9 60.4 reduce-scatter.2
  533.9 194.7 all-reduce.13
where the time goes:
time: 759 us; the launch traced here: 749 us
  waiting for transfers between devices  342 us (45%)
  blocking collectives  143 us (19%)
  local copies, waits for them, and re-layouts  97.9 us (13%)
  matrix products  80.2 us (11%)
  other arithmetic  60.1 us (8%)
  between operations  16.2 us (2%)
    psum x1, waiting for transfers between devices, on_device(): lax.psum((grad_norm_gain, grad_w_z, grad_w_x, grad_w_bc, grad_w_dt, grad_...  198 us
    unnamed x2, blocking collectives  41.4 us
    reduce_scatter x1, waiting for transfers between devices, on_device(): lax.psum_scatter(partial_back, 'head', scatter_dimension=1, tiled=True)  39.1 us
    psum x1, waiting for transfers between devices, on_device(): lax.psum(jnp.concatenate([grad_b_s.reshape(tokens_here, STATE), grad_c_s....  34.6 us
    unnamed x187, local copies, waits for them, and re-layouts  32.8 us
    all_gather x1, blocking collectives, on_device(): lax.all_gather(w_bc, 'head', axis=0, tiled=True)  29.2 us
    psum x1, blocking collectives, on_device(): lax.psum((grad_norm_gain, grad_w_z, grad_w_x, grad_w_bc, grad_w_dt, grad_...  25.1 us
    reduce_scatter x1, waiting for transfers between devices, on_device(): lax.psum_scatter(partial_value, 'head', scatter_dimension=1, tiled=True)  24.6 us
  transfers between devices with their start and end apart: 10, of which 10 were waited for; matrix products, arithmetic and copies ran while one was open for 8% of the time, Pallas kernels for 0%

commit v1 on v0

--- a/solution.py
+++ b/solution.py
@@ -1,6 +1,8 @@
 import jax
 import jax.numpy as jnp
 from jax import lax
+from jax.experimental import pallas as pl
+from jax.experimental.pallas import tpu as pltpu
 from jax.sharding import PartitionSpec as P
 
 D = 1536
@@ -417,6 +419,1148 @@
     )
 
 
+BF = jnp.bfloat16
+F32 = jnp.float32
+MESH = pl.DeviceIdType.MESH
+ROWS = 512
+BLOCK = 384
+CHANNELS = 768
+WIDE = 1024
+HALO = 16
+HOPS = 3
+SEQ = 8
+LINE = 4
+ALONG = "seq"
+ACROSS = "head"
+NN = (((1,), (0,)), ((), ()))
+NT = (((1,), (1,)), ((), ()))
+TN = (((0,), (0,)), ((), ()))
+
+
+def mul(a, b, dims=NN):
+    return lax.dot_general(a, b, dims, preferred_element_type=F32)
+
+
+def cut(start, size, mult):
+    return pl.ds(pl.multiple_of(start, mult), size)
+
+
+def parts(v, n):
+    out = []
+    for _ in range(n):
+        p = v.astype(BF)
+        out.append(p)
+        v = v - p.astype(F32)
+    return out
+
+
+def lanes_sum(v):
+    total = v[:, 0:128]
+    for i in range(1, v.shape[1] // 128):
+        total = total + v[:, 128 * i : 128 * i + 128]
+    return total
+
+
+def rows_sum(v):
+    return jnp.sum(v.reshape(v.shape[0] // 8, 8, v.shape[1]), axis=0)
+
+
+def wide_of(v, n):
+    return jnp.concatenate([v] * n, axis=1)
+
+
+def to_row(part):
+    return jnp.sum(part.T, axis=0, keepdims=True)
+
+
+def to_col(row):
+    return jnp.broadcast_to(row, (128, row.shape[1])).T
+
+
+def loop(n, body):
+    def run(i, carry):
+        body(i)
+        return carry
+
+    lax.fori_loop(0, n, run, 0)
+
+
+def remote(src, dst, send, recv, peer):
+    return pltpu.make_async_remote_copy(
+        src_ref=src, dst_ref=dst, send_sem=send, recv_sem=recv, device_id=peer, device_id_type=MESH
+    )
+
+
+class Total:
+    def __init__(self, whole, bufs, send, recv, freed, base, me):
+        self.w = whole
+        self.freed, self.slot = freed, 3 * (base // 10)
+        self.r0, self.ra, self.rb, self.qa, self.qb = bufs
+        self.send, self.recv, self.base = send, recv, base
+        self.c, self.x, self.y, self.s = me
+        self.rows, self.cols = whole.shape
+        self.live, self.left = {}, set()
+
+    def peer(self, bit):
+        return {ALONG: self.s + bit - 2 * bit * {1: self.c, 2: self.x, 4: self.y}[bit]}
+
+    def free(self, k, n, bit):
+        self.sent(k)
+        pl.semaphore_signal(
+            self.freed.at[self.slot + n], inc=1, device_id=self.peer(bit), device_id_type=MESH
+        )
+
+    def copy(self, k, src, dst, bit):
+        d = remote(src, dst, self.send.at[self.base + k], self.recv.at[self.base + k], self.peer(bit))
+        d.start()
+        self.live[k] = d
+        self.left.add(k)
+
+    def wait(self, k):
+        self.live[k].wait_recv()
+
+    def sent(self, k):
+        self.left.remove(k)
+        self.live[k].wait_send()
+
+    def add(self, start, got, rows, col, cols, step):
+        def body(i):
+            at = (cut(start + i * step, step, 16), pl.ds(col, cols))
+            new = self.w[at].astype(F32) + got[cut(i * step, step, 16), :].astype(F32)
+            self.w[at] = new.astype(self.w.dtype)
+
+        loop(rows // step, body)
+
+    def s0(self):
+        h = self.rows // 2
+        self.copy(0, self.w.at[cut((1 - self.c) * h, h, 16)], self.r0, 1)
+
+    def s1(self):
+        h, q, m = self.rows // 2, self.rows // 4, self.cols // 2
+        base = self.c * h
+        self.free(0, 0, 1)
+        self.wait(0)
+        self.add(base, self.r0, h, 0, self.cols, 32)
+        self.copy(1, self.w.at[cut(base + (1 - self.x) * q, q, 16), pl.ds(0, m)], self.ra, 2)
+        self.copy(2, self.w.at[cut(base + (1 - self.y) * q, q, 16), pl.ds(m, m)], self.rb, 4)
+
+    def s2(self):
+        h, q, e, m = self.rows // 2, self.rows // 4, self.rows // 8, self.cols // 2
+        ba = self.c * h + self.x * q
+        bb = self.c * h + self.y * q
+        self.wait(1)
+        self.add(ba, self.ra, q, 0, m, 32)
+        self.sent(2)
+        self.copy(3, self.w.at[cut(ba + (1 - self.y) * e, e, 16), pl.ds(0, m)], self.qa, 4)
+        self.wait(2)
+        self.add(bb, self.rb, q, m, m, 32)
+        self.sent(1)
+        self.copy(4, self.w.at[cut(bb + (1 - self.x) * e, e, 16), pl.ds(m, m)], self.qb, 2)
+
+    def s3(self):
+        h, q, e, m = self.rows // 2, self.rows // 4, self.rows // 8, self.cols // 2
+        ba = self.c * h + self.x * q + self.y * e
+        bb = self.c * h + self.y * q + self.x * e
+        self.free(3, 1, 4)
+        self.free(4, 2, 2)
+        self.wait(3)
+        self.add(ba, self.qa, e, 0, m, 16)
+        pl.semaphore_wait(self.freed.at[self.slot + 1], 1)
+        p = self.w.at[cut(ba, e, 16), pl.ds(0, m)]
+        self.copy(5, p, p, 4)
+        self.wait(4)
+        self.add(bb, self.qb, e, m, m, 16)
+        pl.semaphore_wait(self.freed.at[self.slot + 2], 1)
+        p = self.w.at[cut(bb, e, 16), pl.ds(m, m)]
+        self.copy(6, p, p, 2)
+
+    def s4(self):
+        h, q, m = self.rows // 2, self.rows // 4, self.cols // 2
+        self.wait(5)
+        p = self.w.at[cut(self.c * h + self.x * q, q, 16), pl.ds(0, m)]
+        self.copy(7, p, p, 2)
+        self.wait(6)
+        p = self.w.at[cut(self.c * h + self.y * q, q, 16), pl.ds(m, m)]
+        self.copy(8, p, p, 4)
+
+    def s5(self):
+        h = self.rows // 2
+        self.wait(7)
+        self.wait(8)
+        pl.semaphore_wait(self.freed.at[self.slot], 1)
+        p = self.w.at[cut(self.c * h, h, 16)]
+        self.copy(9, p, p, 1)
+
+    def s6(self):
+        self.wait(9)
+        for k in sorted(self.left):
+            self.sent(k)
+
+
+def total_bufs(rows, cols, kind):
+    sizes = [(2, 1), (4, 2), (4, 2), (8, 2), (8, 2)]
+    return [pltpu.VMEM((rows // a, cols // b), kind) for a, b in sizes]
+
+
+class Refs:
+    def __init__(self, named):
+        self.__dict__.update(named)
+
+
+def layer_kernel(named, sum_bufs):
+    g = Refs(named)
+    g.ggn = g.acc.at[:, pl.ds(0, CHANNELS)]
+    g.z = g.ggn
+    g.gn = g.xg.at[:, pl.ds(0, CHANNELS)]
+    g.gz = g.xg.at[:, pl.ds(CHANNELS, CHANNELS)]
+    g.gconv = g.slope
+    g.gx = g.gm
+    g.sblk2 = g.sblk
+    g.own = g.gated.at[:, pl.ds(0, BLOCK)]
+    g.gb = g.gated.at[:, pl.ds(BLOCK, 128)]
+    g.gc = g.gated.at[:, pl.ds(BLOCK + 128, 128)]
+    s = lax.axis_index(ALONG)
+    z = lax.axis_index(ACROSS)
+    me = (lax.rem(s, 2), lax.rem(s // 2, 2), s // 4, s)
+    zpeers = [{ACROSS: lax.rem(z + d, LINE)} for d in range(1, LINE)]
+    speers = [{ALONG: lax.rem(s + d, SEQ)} for d in range(1, SEQ)]
+
+    loads = []
+    for i, (src, dst) in enumerate(
+        [(g.x_hbm, g.x), (g.w_x, g.wx), (g.w_z, g.wz), (g.cot_hbm, g.cotg.at[:, cut(z * BLOCK, BLOCK, 128)]), (g.w_out, g.wo)]
+    ):
+        d = pltpu.make_async_copy(src, dst, g.load_sem.at[i])
+        d.start()
+        loads.append(d)
+
+    sem = pltpu.get_barrier_semaphore()
+    for p in zpeers + speers:
+        pl.semaphore_signal(sem, inc=1, device_id=p, device_id_type=MESH)
+    pl.semaphore_wait(sem, len(zpeers) + len(speers))
+
+    pending = []
+
+    def send(src, dst, sems, i, peer):
+        d = remote(src, dst, sems[0].at[i], sems[1].at[i], peer)
+        d.start()
+        pending.append(d)
+        return d
+
+    loads[0].wait()
+    loads[3].wait()
+    gain = g.params[0:1, 0:BLOCK]
+    xv = g.x[...].astype(F32)
+    g.ssq[z] = jnp.broadcast_to(to_row(lanes_sum(xv * xv)), (8, ROWS))
+    g.gains[z] = jnp.broadcast_to(gain, (8, BLOCK))
+    piece = cut(48 * s, 48, 16)
+    own = cut(z * BLOCK, BLOCK, 128)
+    g.wbc[z, piece, :] = g.w_bc[piece, :]
+    small = []
+    for i, p in enumerate(zpeers):
+        small.append(send(g.ssq.at[z], g.ssq.at[z], g.small, i, p))
+        small.append(send(g.gains.at[z], g.gains.at[z], g.small, 3 + i, p))
+        small.append(send(g.w_bc.at[piece], g.wbc.at[z, piece], g.small, 6 + i, p))
+    xin = [send(g.x, g.xg.at[:, own], g.gather, i, p) for i, p in enumerate(zpeers)]
+    cin = [send(g.cotg.at[:, own], g.cotg.at[:, own], g.gather, 3 + i, p) for i, p in enumerate(zpeers)]
+
+    g.wd[...] = jnp.zeros(g.wd.shape, BF)
+    g.wd[:, 0:12] = g.w_dt[...]
+    g.taps[...] = jnp.zeros(g.taps.shape, F32)
+    g.taps[0:4, 0:CHANNELS] = g.conv_x_w[...]
+    g.taps[0:4, CHANNELS:WIDE] = g.conv_bc_w[...]
+    g.taps[4:5, 0:CHANNELS] = g.params[1:2, :]
+    g.taps[4:5, CHANNELS:WIDE] = g.params[2:3, 0:256]
+    expand_row = lax.broadcasted_iota(jnp.int32, (256, CHANNELS), 0)
+    expand_col = lax.broadcasted_iota(jnp.int32, (256, CHANNELS), 1)
+    g.spread[...] = jnp.where((expand_col >> 6) == (expand_row & 127), 1.0, 0.0).astype(BF)
+    starts = [jnp.int32(0)]
+    for k in range(7):
+        starts.append(starts[-1] + g.lengths[k])
+
+    def segment(pos):
+        total = jnp.full(pos.shape, -1, jnp.int32)
+        for k in range(8):
+            total = total + jnp.where(pos >= starts[k], 1, 0)
+        return total.astype(F32)
+
+    g.segc[...] = segment(
+        lax.broadcasted_iota(jnp.int32, (ROWS + HALO, 128), 0) + (s * ROWS - HALO)
+    )
+    g.segr[...] = segment(lax.broadcasted_iota(jnp.int32, (8, ROWS), 1) + s * ROWS)
+    tri_i = lax.broadcasted_iota(jnp.int32, (SPAN, SPAN), 0)
+    tri_j = lax.broadcasted_iota(jnp.int32, (SPAN, SPAN), 1)
+    g.tri[...] = jnp.where(tri_i >= tri_j, 1.0, 0.0).astype(BF)
+    lane = lax.broadcasted_iota(jnp.int32, (1, 128), 1)
+    left = lane < 64
+
+    def spread(v):
+        hi, lo = parts(v, 2)
+        return mul(jnp.concatenate([hi, lo], axis=1), g.spread[...])
+
+    def head_sum(v):
+        hi, lo = parts(v, 2)
+        e = g.spread[0:128, :]
+        return mul(hi, e, NT) + mul(lo, e, NT)
+
+    g.skipe[...] = spread(jnp.broadcast_to(g.params[5:6, 0:128], (8, 128)))
+    rates = jnp.exp(g.params[4:5, 0:128])
+
+    for d in small:
+        d.wait_recv()
+    wide = [
+        send(g.wbc.at[:, piece], g.wbc.at[:, piece], g.wide, i, p) for i, p in enumerate(speers)
+    ]
+    total = g.ssq[0] + g.ssq[1] + g.ssq[2] + g.ssq[3]
+    g.xscale[...] = to_col(lax.rsqrt(total[0:1] / D + epsilon))
+
+    def normalise(k, src):
+        gk = g.gains[k][0:1]
+        cols = cut(k * BLOCK, BLOCK, 128)
+
+        def body(i):
+            at = cut(i * 64, 64, 16)
+            v = src(at, cols).astype(F32)
+            g.xn[at, cols] = (v * wide_of(g.xscale[at, :], 3) * gk).astype(BF)
+
+        loop(ROWS // 64, body)
+
+    def project(k, w, cols, base, first, width=256):
+        at = cut(k * BLOCK, BLOCK, 128)
+
+        def body(n):
+            p = mul(g.xn[:, at], w[cut(k * BLOCK, BLOCK, 16), cut(n * width, width, 128)])
+            dst = cut(base + n * width, width, 128)
+            if first:
+                g.acc[:, dst] = p
+            else:
+                g.acc[:, dst] += p
+
+        loop(cols // width, body)
+
+    def project_bc(k, first):
+        p = mul(g.xn[:, cut(k * BLOCK, BLOCK, 128)], g.wbc[k])
+        if first:
+            g.acc[:, CHANNELS:WIDE] = p
+        else:
+            g.acc[:, CHANNELS:WIDE] += p
+
+    normalise(z, lambda at, cols: g.x[at, :])
+    loads[1].wait()
+    loads[2].wait()
+    project(z, g.wx, CHANNELS, 0, True)
+    project(z, g.wz, CHANNELS, WIDE, True)
+    project(z, g.wd, 128, WIDE + CHANNELS, True, 128)
+    for d in wide:
+        d.wait_recv()
+    project_bc(z, True)
+    ks = [lax.rem(z + LINE - d, LINE) for d in range(1, LINE)]
+    for i, k in enumerate(ks):
+        xin[i].wait_recv()
+        normalise(k, lambda at, cols: g.xg[at, cols])
+        project(k, g.wx, CHANNELS, 0, False)
+        project_bc(k, False)
+        if i < 2:
+            project(k, g.wz, CHANNELS, WIDE, False)
+            project(k, g.wd, 128, WIDE + CHANNELS, False, 128)
+
+    g.edge[...] = g.acc[ROWS - HALO : ROWS, 0:WIDE].astype(BF)
+    edge = remote(g.edge, g.halo, g.edge_sem.at[0], g.edge_sem.at[1], {ALONG: s + 1})
+
+    @pl.when(s < SEQ - 1)
+    def _():
+        edge.start()
+
+    @pl.when(s == 0)
+    def _():
+        g.halo[...] = jnp.zeros(g.halo.shape, BF)
+
+    def put(i):
+        g.cf[cut(HALO + i * 64, 64, 8), :] = (
+            g.acc[cut(i * 64, 64, 8), 0:WIDE].astype(BF).astype(F32)
+        )
+
+    loop(ROWS // 64, put)
+    project(ks[2], g.wz, CHANNELS, WIDE, False)
+    project(ks[2], g.wd, 128, WIDE + CHANNELS, False, 128)
+
+    step_pre = g.acc[:, WIDE + CHANNELS :] + g.params[3:4, 0:128]
+    g.spre[...] = step_pre
+    g.step[...] = jnp.where(lane < 12, jax.nn.softplus(step_pre), 0.0)
+    for q in range(2):
+        rows = pl.ds(q * SPAN, SPAN)
+        log_decay = -rates * g.step[rows, :]
+        cum = sum(mul(g.tri[...], p) for p in parts(log_decay, 3))
+        g.cum[rows, :] = cum
+        g.cumt[q] = cum.T[0:16, :]
+        last = cum[SPAN - 1 : SPAN, :]
+        seg = g.segc[pl.ds(HALO + q * SPAN, SPAN), :]
+        seg_last = g.segc[HALO + q * SPAN + SPAN - 1 : HALO + q * SPAN + SPAN, :]
+        seg_prev = g.segc[HALO + q * SPAN - 1 : HALO + q * SPAN, :]
+        tail = jnp.where(seg == seg_last, jnp.exp(last - cum), 0.0)
+        load = tail * g.step[rows, :]
+        lead = jnp.where(seg == seg_prev, jnp.exp(cum), 0.0)
+        g.tail[rows, :] = tail
+        g.load[rows, :] = load
+        g.lead[rows, :] = lead
+        g.loadt[q] = load.T[0:16, :]
+        g.leadt[q] = lead.T[0:16, :]
+        g.stept[q] = g.step[rows, :].T[0:16, :]
+        carry = jnp.where(seg_last == seg_prev, jnp.exp(last), 0.0)
+        g.carry[q] = jnp.broadcast_to(carry, (8, 128))
+        g.carrye[q] = spread(jnp.broadcast_to(carry, (8, 128)))
+    g.decay[0] = g.carrye[0] * g.carrye[1]
+
+    @pl.when(s > 0)
+    def _():
+        edge.wait_recv()
+
+    g.cf[0:HALO, :] = g.halo[...].astype(F32)
+
+    def taps_of(first, cols):
+        v = g.cf[cut(first + 8, 72, 8), cols]
+        sv = g.segc[cut(first + 8, 72, 8), :]
+        width = v.shape[1] // 128
+        out = []
+        for k in range(3):
+            same = pltpu.roll(sv, 67 - k, 0)[0:64] == sv[8:72]
+            out.append(jnp.where(wide_of(same, width), pltpu.roll(v, 67 - k, 0)[0:64], 0.0))
+        out.append(v[8:72])
+        return out
+
+    def convolve(i):
+        first = i * 64
+        at = cut(first, 64, 16)
+        for n in range(4):
+            cols = pl.ds(n * 256, 256)
+            v = jnp.broadcast_to(g.taps[4:5, cols], (64, 256))
+            for k, t in enumerate(taps_of(first, cols)):
+                v = v + g.taps[k : k + 1, cols] * t
+            sig = jax.nn.sigmoid(v)
+            act = (v * sig).astype(BF)
+            g.slope[at, cols] = sig * (1.0 + v * (1.0 - sig))
+            if n < 3:
+                g.inner[at, cols] = act
+            else:
+                g.b[at, :] = act[:, 0:128]
+                g.c[at, :] = act[:, 128:256]
+
+    loop(ROWS // 64, convolve)
+
+    g.bt[...] = g.b[...].astype(F32).T
+    g.ct[...] = g.c[...].astype(F32).T
+
+    def outer(maps, weights, vals):
+        def body(t):
+            q, p = t // 6, lax.rem(t, 6)
+            at = cut(p * 128, 128, 128)
+            v = vals[cut(q * SPAN, SPAN, 256), at]
+            m = maps[:, cut(q * SPAN, SPAN, 256)]
+            o = [mul((m * weights[q, pl.ds(2 * p + e, 1), :]).astype(BF), v) for e in range(2)]
+            g.local[q, :, at] = jnp.where(left, o[0], o[1])
+
+        loop(12, body)
+
+    outer(g.bt, g.loadt, g.inner)
+    c0, c1 = g.carrye[0][0:1], g.carrye[1][0:1]
+    g.state_out[...] = (c1 * g.local[0] + g.local[1])
+    for j in range(1, HOPS + 1):
+        ahead = s + j < SEQ
+        behind = s - j >= 0
+        d = remote(g.state_out, g.states.at[j - 1], g.st_send.at[j - 1], g.st_recv.at[j - 1], {ALONG: s + j})
+
+        @pl.when(ahead)
+        def _():
+            d.start()
+
+        @pl.when(jnp.logical_not(behind))
+        def _():
+            g.states[j - 1] = jnp.zeros((STATE, CHANNELS), F32)
+
+    for j in range(1, HOPS):
+        up = remote(g.decay.at[0], g.decay.at[j], g.st_send.at[2 + j], g.st_recv.at[2 + j], {ALONG: s + j})
+        down = remote(g.decay.at[0], g.decay.at[2 + j], g.st_send.at[4 + j], g.st_recv.at[4 + j], {ALONG: s - j})
+
+        @pl.when(s + j < SEQ)
+        def _():
+            up.start()
+
+        @pl.when(s - j >= 0)
+        def _():
+            down.start()
+
+        @pl.when(s - j < 0)
+        def _():
+            g.decay[j] = jnp.zeros((8, CHANNELS), F32)
+
+        @pl.when(s + j >= SEQ)
+        def _():
+            g.decay[2 + j] = jnp.zeros((8, CHANNELS), F32)
+
+    def head_cols(ref, rows, p):
+        moved = pltpu.roll(ref[rows, :], lax.rem(128 - 2 * p, 128), 1)
+        return moved[:, 0:1], moved[:, 1:2]
+
+    def inside(q):
+        rows = cut(q * SPAN, SPAN, 256)
+        seg = g.segc[cut(HALO + q * SPAN, SPAN, 16), 0:1]
+        segr = g.segr[0:1, cut(q * SPAN, SPAN, 256)]
+        scores = mul(g.c[rows, :], g.b[rows, :], NT)
+        g.scores[...] = jnp.where((tri_i >= tri_j) & (seg == segr), scores, 0.0)
+
+        def pair(p):
+            cols = head_cols(g.cum, rows, p)
+            at = cut(p * 128, 128, 128)
+            outs = []
+            for e in range(2):
+                row = g.cumt[q, pl.ds(2 * p + e, 1), :]
+                step = g.stept[q, pl.ds(2 * p + e, 1), :]
+                fall = jnp.exp(jnp.minimum(cols[e] - row, 0.0))
+                outs.append(mul((g.scores[...] * fall * step).astype(BF), g.inner[rows, at]))
+            g.out[rows, at] = jnp.where(left, outs[0], outs[1])
+
+        loop(6, pair)
+
+    loop(2, inside)
+
+    for j in range(1, HOPS + 1):
+        d = remote(g.state_out, g.states.at[j - 1], g.st_send.at[j - 1], g.st_recv.at[j - 1], {ALONG: s + j})
+
+        @pl.when(s - j >= 0)
+        def _():
+            d.wait_recv()
+
+    for j in range(1, HOPS):
+        up = remote(g.decay.at[0], g.decay.at[j], g.st_send.at[2 + j], g.st_recv.at[2 + j], {ALONG: s + j})
+
+        @pl.when(s - j >= 0)
+        def _():
+            up.wait_recv()
+
+    got = [g.states[j].astype(F32) for j in range(HOPS)]
+    incoming = got[0] + g.decay[1][0:1] * (got[1] + g.decay[2][0:1] * got[2])
+    g.sin[0] = incoming
+    g.sin[1] = g.local[0] + c0 * incoming
+    for q in range(2):
+        g.slow[q] = g.sin[q].astype(BF)
+
+    def outside(t):
+        q, p = t // 6, lax.rem(t, 6)
+        rows, at = cut(q * SPAN, SPAN, 256), cut(p * 128, 128, 128)
+        cols = head_cols(g.lead, rows, p)
+        cv = g.c[rows, :].astype(F32)
+        o = [mul((cv * cols[e]).astype(BF), g.slow[q, :, at]) for e in range(2)]
+        g.out[rows, at] += jnp.where(left, o[0], o[1])
+
+    loop(12, outside)
+
+    gate_cols = pl.ds(WIDE, CHANNELS)
+    skip = g.skipe[0:1]
+
+    def gate(i):
+        at = cut(i * 64, 64, 16)
+        pre = g.acc[at, gate_cols]
+        mixed = g.out[at, :] + g.inner[at, :].astype(F32) * skip
+        gated = mixed * (pre * jax.nn.sigmoid(pre))
+        g.gated[at, :] = gated
+        g.part[0, at, :] = lanes_sum(gated * gated)
+
+    loop(ROWS // 64, gate)
+
+    for d in cin:
+        d.wait_recv()
+    loads[4].wait()
+    gate_gain = g.params[6:7, :]
+
+    def down(n):
+        g.ggn[:, cut(n * 256, 256, 256)] = mul(g.cotg[...], g.wo[cut(n * 256, 256, 256), :], NT)
+
+    loop(3, down)
+
+    def inner_part(i):
+        at = cut(i * 64, 64, 16)
+        g.part[1, at, :] = lanes_sum(g.ggn[at, :] * gate_gain * g.gated[at, :])
+
+    loop(ROWS // 64, inner_part)
+    g.stats[z, 0:8, :] = jnp.broadcast_to(to_row(g.part[0]), (8, ROWS))
+    g.stats[z, 8:16, :] = jnp.broadcast_to(to_row(g.part[1]), (8, ROWS))
+    stat = [send(g.stats.at[z], g.stats.at[z], g.stat, i, p) for i, p in enumerate(zpeers)]
+    for d in stat:
+        d.wait_recv()
+    sums = g.stats[0] + g.stats[1] + g.stats[2] + g.stats[3]
+    gscale = lax.rsqrt(sums[0:1] / INNER + epsilon)
+    g.part[0] = to_col(gscale)
+    g.part[1] = to_col(gscale * gscale * gscale * sums[8:9] / INNER)
+    g.vacc[...] = jnp.zeros(g.vacc.shape, F32)
+
+    def ungate(i):
+        at = cut(i * 64, 64, 16)
+        a = wide_of(g.part[0, at, :], 6)
+        pre = g.acc[at, gate_cols]
+        vals = g.inner[at, :].astype(F32)
+        mixed = g.out[at, :] + vals * skip
+        gated, ggn = g.gated[at, :], g.ggn[at, :]
+        g.gn[at, :] = (gated * a * gate_gain).astype(BF)
+        gg = a * (ggn * gate_gain) - gated * wide_of(g.part[1, at, :], 6)
+        sig = jax.nn.sigmoid(pre)
+        gm = (gg * (pre * sig)).astype(BF)
+        g.gm[at, :] = gm
+        g.gz[at, :] = (gg * mixed * (sig * (1.0 + pre * (1.0 - sig)))).astype(BF)
+        g.vacc[0] += rows_sum(ggn * gated * a)
+        g.vacc[1] += rows_sum(gm.astype(F32) * vals)
+
+    loop(ROWS // 64, ungate)
+
+    outer(g.ct, g.leadt, g.gm)
+    g.sent_grad[...] = (g.local[0] + c0 * g.local[1])
+    back = []
+    for j in range(1, HOPS + 1):
+        d = remote(g.sent_grad, g.gstates.at[j - 1], g.gs_send.at[j - 1], g.gs_recv.at[j - 1], {ALONG: s - j})
+        back.append(d)
+
+        @pl.when(s - j >= 0)
+        def _():
+            d.start()
+
+        @pl.when(s + j >= SEQ)
+        def _():
+            g.gstates[j - 1] = jnp.zeros((STATE, CHANNELS), F32)
+
+    def total_of(i, ref, n):
+        return Total(ref, sum_bufs[5 * i : 5 * i + 5], g.tot_send, g.tot_recv, g.freed, 10 * i, me)
+
+    t_out = total_of(0, g.p_out, 0)
+    t_z = total_of(1, g.p_z, 0)
+    t_x = total_of(2, g.p_x, 0)
+    t_bc = total_of(3, g.p_bc, 0)
+
+    def grad_out(n):
+        at = cut(n * 256, 256, 256)
+        g.p_out[at, :] = mul(g.gn[:, at], g.cotg[...], TN).astype(BF)
+
+    loop(3, grad_out)
+    t_out.s0()
+
+    def grad_z(n):
+        at = cut(n * 256, 256, 256)
+        g.p_z[at, :] = mul(g.xn[:, at], g.gz[...], TN).astype(BF)
+
+    loop(6, grad_z)
+    t_z.s0()
+    t_out.s1()
+
+    outs = []
+    for i, p in enumerate(zpeers):
+        k = lax.rem(z + 1 + i, LINE)
+        g.sblk[i] = mul(g.gn[...], g.wo[:, cut(k * BLOCK, BLOCK, 128)]).astype(BF)
+        outs.append(send(g.sblk.at[i], g.rblk.at[i], g.block, i, p))
+    g.own[...] = mul(g.gn[...], g.wo[:, own])
+    t_z.s1()
+
+    def inside_back(q):
+        rows = cut(q * SPAN, SPAN, 256)
+        seg = g.segc[cut(HALO + q * SPAN, SPAN, 16), 0:1]
+        segr = g.segr[0:1, cut(q * SPAN, SPAN, 256)]
+        scores = mul(g.b[rows, :], g.c[rows, :], NT)
+        mask = (tri_i <= tri_j) & (seg == segr)
+        g.scores[...] = jnp.where(mask, scores, 0.0)
+        g.gscores[...] = jnp.zeros((SPAN, SPAN), F32)
+
+        def pair(p):
+            cols = head_cols(g.cum, rows, p)
+            at = cut(p * 128, 128, 128)
+            steps = head_cols(g.step, rows, p)
+            gm = g.gm[rows, at]
+            outs = []
+            for e in range(2):
+                row = g.cumt[q, pl.ds(2 * p + e, 1), :]
+                fall = jnp.exp(jnp.minimum(row - cols[e], 0.0)) * steps[e]
+                outs.append(mul((g.scores[...] * fall).astype(BF), gm))
+                keep = left if e == 0 else jnp.logical_not(left)
+                vals = jnp.where(keep, g.inner[rows, at].astype(F32), 0.0).astype(BF)
+                g.gscores[...] += mul(vals, gm, NT) * fall
+            g.z[rows, at] = jnp.where(left, outs[0], outs[1])
+
+        loop(6, pair)
+        gs = jnp.where(mask, g.gscores[...], 0.0)
+        hi, lo = parts(gs, 2)
+        g.gb[rows, :] = mul(hi, g.c[rows, :]) + mul(lo, g.c[rows, :])
+        g.gc[rows, :] = mul(hi, g.b[rows, :], TN) + mul(lo, g.b[rows, :], TN)
+
+    inside_back(1)
+    t_out.s2()
+    inside_back(0)
+    t_z.s2()
+
+    for j in range(1, HOPS + 1):
+        @pl.when(s + j < SEQ)
+        def _():
+            back[j - 1].wait_recv()
+
+    for j in range(1, HOPS):
+        d = remote(g.decay.at[0], g.decay.at[2 + j], g.st_send.at[4 + j], g.st_recv.at[4 + j], {ALONG: s - j})
+
+        @pl.when(s + j < SEQ)
+        def _():
+            d.wait_recv()
+
+    got = [g.gstates[j].astype(F32) for j in range(HOPS)]
+    beyond = got[0] + g.decay[3][0:1] * (got[1] + g.decay[4][0:1] * got[2])
+    g.gloc[1] = beyond
+    g.gloc[0] = g.local[1] + c1 * beyond
+    t_out.s3()
+    ends = []
+    for q in range(2):
+        rows = pl.ds(q * SPAN, SPAN)
+        glow = g.gloc[q].astype(BF)
+        vals = g.inner[rows, :].astype(F32)
+        gm = g.gm[rows, :].astype(F32)
+        loade = spread(g.load[rows, :])
+        bg = mul(g.b[rows, :], glow)
+        zed = g.z[rows, :]
+        carry_sum = jnp.sum(g.gloc[q] * g.sin[q], axis=0, keepdims=True)
+        grad_carry = head_sum(jnp.broadcast_to(carry_sum, (8, CHANNELS)))[0:1]
+        t1 = head_sum(gm * g.out[rows, :])
+        q1 = head_sum(vals * zed)
+        q2 = head_sum(vals * bg)
+        step, load = g.step[rows, :], g.load[rows, :]
+        tail_term = q2 * load
+        gcum = t1 - q1 - tail_term
+        end = jnp.sum(tail_term, axis=0, keepdims=True) + grad_carry * g.carry[q][0:1]
+        is_last = lax.broadcasted_iota(jnp.int32, (SPAN, 128), 0) == SPAN - 1
+        gcum = gcum + jnp.where(is_last, end, 0.0)
+        glog = sum(mul(g.tri[...], p, TN) for p in parts(gcum, 3))
+        gstep = jnp.where(step > 1e-30, q1 / jnp.maximum(step, 1e-30), 0.0) + q2 * g.tail[rows, :]
+        gpre = (gstep - rates * glog) * jax.nn.sigmoid(g.spre[rows, :])
+        g.gsr[rows, :] = gpre.astype(BF)
+        ends.append((rows_sum(gpre), rows_sum(glog * (-rates * step))))
+        g.z[rows, :] = zed + loade * bg + skip * gm
+        g.gb[rows, :] += sum(mul(p, glow, NT) for p in parts(vals * loade, 2))
+        g.gc[rows, :] += sum(mul(p, g.slow[q], NT) for p in parts(gm * spread(g.lead[rows, :]), 2))
+    g.pack[16:24, 0:128] = jnp.broadcast_to(
+        jnp.sum(ends[0][0] + ends[1][0], axis=0, keepdims=True), (8, 128)
+    )
+    g.pack[16:24, 128:256] = jnp.broadcast_to(
+        jnp.sum(ends[0][1] + ends[1][1], axis=0, keepdims=True), (8, 128)
+    )
+    t_z.s3()
+
+    def grads_of(at, n):
+        cols = pl.ds(n * 256, 256)
+        if n < 3:
+            v = g.z[at, cols]
+        else:
+            v = jnp.concatenate([g.gb[at, :], g.gc[at, :]], axis=1)
+        return v * g.slope[at, cols]
+
+    def slopes(i):
+        at = cut(i * 64, 64, 16)
+        for n in range(4):
+            g.gconv[cut(i * 64, 64, 8), pl.ds(n * 256, 256)] = grads_of(at, n)
+
+    g.gconv[ROWS : ROWS + 16, :] = jnp.zeros((16, WIDE), F32)
+    loop(ROWS // 64, slopes)
+
+    def same_ahead(first, count, shift):
+        sv = g.segc[cut(first + HALO, count + 8, 8), :] if count else None
+        return sv
+
+    v = g.gconv[0:8, :]
+    sv = g.segc[HALO - 8 : HALO + 8, :]
+    back_rows = jnp.zeros((8, WIDE), F32)
+    for k in range(3):
+        shift = 3 - k
+        full = jnp.concatenate([jnp.zeros((8, WIDE), F32), v], axis=0)
+        src = pltpu.roll(full, 16 - shift, 0)[0:8]
+        same = pltpu.roll(sv, 16 - shift, 0)[0:8] == sv[0:8]
+        back_rows = back_rows + jnp.where(wide_of(same, 8), g.taps[k : k + 1, :] * src, 0.0)
+    g.ret_out[...] = back_rows
+    ret = remote(g.ret_out, g.ret_in, g.edge_sem.at[2], g.edge_sem.at[3], {ALONG: s - 1})
+
+    @pl.when(s > 0)
+    def _():
+        ret.start()
+
+    @pl.when(s == SEQ - 1)
+    def _():
+        g.ret_in[...] = jnp.zeros((8, WIDE), F32)
+
+    g.wacc[...] = jnp.zeros(g.wacc.shape, F32)
+
+    def convolve_back(i):
+        first = i * 64
+        at = cut(first, 64, 16)
+        sv = g.segc[cut(first + HALO, 64, 8), :]
+        ahead = jnp.where(i < ROWS // 64 - 1, 1.0, 0.0)
+        for n in range(4):
+            cols = pl.ds(n * 256, 256)
+            v = g.gconv[cut(first, 72, 8), cols]
+            here = v[0:64]
+            total = g.taps[3:4, cols] * here
+            nxt = g.segc[cut(jnp.minimum(first + HALO + 64, ROWS + HALO - 8), 8, 8), :]
+            sfull = jnp.concatenate([sv, nxt], axis=0)
+            for k in range(3):
+                shift = 3 - k
+                same = pltpu.roll(sfull, 72 - shift, 0)[0:64] == sv
+                src = pltpu.roll(v, 72 - shift, 0)[0:64]
+                total = total + jnp.where(wide_of(same, 2), g.taps[k : k + 1, cols] * src, 0.0)
+            if n < 3:
+                g.gx[at, cols] = total.astype(BF)
+            else:
+                for k, v in enumerate(parts(total, 2)):
+                    g.gbc[k, at, :] = v
+
+            @pl.when(i == ROWS // 64 - 1)
+            def _():
+                g.tail_rows[:, cols] = total[48:64]
+
+            for k, t in enumerate(taps_of(first, cols)):
+                g.wacc[k, :, cols] += rows_sum(here * t)
+            g.wacc[4, :, cols] += rows_sum(here)
+
+    loop(ROWS // 64, convolve_back)
+    t_out.s4()
+
+    @pl.when(s < SEQ - 1)
+    def _():
+        ret.wait_recv()
+
+    last_rows = g.tail_rows[...] + jnp.concatenate([jnp.zeros((8, WIDE), F32), g.ret_in[...]], axis=0)
+    g.gx[ROWS - 16 : ROWS, :] = last_rows[:, 0:CHANNELS].astype(BF)
+    for k, v in enumerate(parts(last_rows[:, CHANNELS:WIDE], 2)):
+        g.gbc[k, ROWS - 16 : ROWS, :] = v
+
+    def bc_block(at):
+        return sum(mul(g.xn[:, at], g.gbc[k], TN) for k in range(2))
+
+    bcs = []
+    for i, p in enumerate(zpeers):
+        k = lax.rem(z + 1 + i, LINE)
+        g.sbc[i] = bc_block(cut(k * BLOCK, BLOCK, 128)).astype(BF)
+        bcs.append(send(g.sbc.at[i], g.rbc.at[i], g.bcsem, i, p))
+
+    def grad_x(n):
+        at = cut(n * 256, 256, 256)
+        g.p_x[at, :] = mul(g.xn[:, at], g.gx[...], TN).astype(BF)
+
+    loop(6, grad_x)
+    t_x.s0()
+    t_z.s4()
+
+    def back_block(k):
+        at = cut(k * BLOCK, BLOCK, 16)
+        v = mul(g.gx[...], g.wx[at, :], NT) + mul(g.gz[...], g.wz[at, :], NT)
+        return v + mul(g.gsr[...], g.wd[at, :], NT) + mul(g.gbc[0], g.wbc[k], NT) + mul(g.gbc[1], g.wbc[k], NT)
+
+    for d in outs:
+        d.wait_recv()
+        d.wait_send()
+        pending[:] = [q for q in pending if q is not d]
+    out_sum = g.own[...]
+    for i in range(3):
+        out_sum = out_sum + g.rblk[i].astype(F32)
+    g.layer_out[...] = (g.x[...].astype(F32) + out_sum).astype(BF)
+    ins = []
+    for i, p in enumerate(zpeers):
+        k = lax.rem(z + 1 + i, LINE)
+        g.sblk2[i] = back_block(k).astype(BF)
+        ins.append(send(g.sblk2.at[i], g.rblk2.at[i], g.block, 3 + i, p))
+        if i == 0:
+            t_x.s1()
+            t_out.s5()
+    g.own[...] = back_block(z)
+
+    for k in range(5):
+        row = jnp.sum(g.wacc[k], axis=0, keepdims=True)
+        g.pack[k : k + 1, :] = row[:, 0:CHANNELS]
+        g.pack[8 + k : 9 + k, 0:256] = row[:, CHANNELS:WIDE]
+    g.pack[5:6, :] = jnp.sum(g.vacc[0], axis=0, keepdims=True)
+    g.pack[6:7, :] = jnp.sum(g.vacc[1], axis=0, keepdims=True)
+    g.dt_out[...] = mul(g.gsr[...], g.xn[...], TN)[0:16].astype(BF)
+    packs = []
+    for i, p in enumerate(speers):
+        packs.append(send(g.pack, g.packs.at[i], g.packsem, i, p))
+        packs.append(send(g.dt_out, g.dts.at[i], g.packsem, 7 + i, p))
+    bc = bc_block(own)
+    for d in bcs:
+        d.wait_recv()
+    for i in range(3):
+        bc = bc + g.rbc[i].astype(F32)
+    g.p_bc[...] = bc
+    t_bc.s0()
+    t_z.s5()
+    t_out.s6()
+    store = [pltpu.make_async_copy(g.p_out, g.grad_out, g.load_sem.at[5])]
+    store[0].start()
+    t_x.s2()
+    t_bc.s1()
+    t_z.s6()
+    store.append(pltpu.make_async_copy(g.p_z, g.grad_z, g.load_sem.at[6]))
+    store[1].start()
+    for d in packs:
+        d.wait_recv()
+    vec = g.pack[...]
+    dts = g.dt_out[...].astype(F32)
+    for i in range(7):
+        vec = vec + g.packs[i]
+        dts = dts + g.dts[i].astype(F32)
+    g.vec[...] = vec
+    g.grad_dt[...] = dts
+    g.bcv[z] = vec[8:16, 0:256]
+    bcv = [send(g.bcv.at[z], g.bcv.at[z], g.bcvsem, i, p) for i, p in enumerate(zpeers)]
+    t_x.s3()
+    t_bc.s2()
+    t_bc.s3()
+    t_x.s4()
+    t_bc.s4()
+
+    for d in ins:
+        d.wait_recv()
+    g.nacc[...] = jnp.zeros(g.nacc.shape, F32)
+
+    def finish(i):
+        at = cut(i * 64, 64, 16)
+        v = g.own[at, :]
+        for k in range(3):
+            v = v + g.rblk2[k, at, :].astype(F32)
+        g.own[at, :] = v
+        x = g.x[at, :].astype(F32)
+        g.part[0, at, :] = lanes_sum(v * gain * x)
+        g.nacc[...] += rows_sum(v * x * wide_of(g.xscale[at, :], 3))
+
+    loop(ROWS // 64, finish)
+    g.nstat[z] = jnp.broadcast_to(to_row(g.part[0]), (8, ROWS))
+    nst = [send(g.nstat.at[z], g.nstat.at[z], g.nsem, i, p) for i, p in enumerate(zpeers)]
+    g.ngain[0] = jnp.broadcast_to(jnp.sum(g.nacc[...], axis=0, keepdims=True), (8, BLOCK))
+    ngs = [send(g.ngain.at[0], g.ngain.at[1 + i], g.nsem, 3 + i, p) for i, p in enumerate(speers)]
+    t_x.s5()
+    t_bc.s5()
+    for d in nst:
+        d.wait_recv()
+    rows = (g.nstat[0] + g.nstat[1] + g.nstat[2] + g.nstat[3])[0:1]
+    g.part[0] = to_col(rows / D)
+
+    def last(i):
+        at = cut(i * 64, 64, 16)
+        sc = wide_of(g.xscale[at, :], 3)
+        x = g.x[at, :].astype(F32)
+        g.grad_in[at, :] = (
+            g.cotg[at, own].astype(F32)
+            + sc * (g.own[at, :] * gain)
+            - x * (sc * sc * sc * wide_of(g.part[0, at, :], 3))
+        )
+
+    loop(ROWS // 64, last)
+    for d in ngs:
+        d.wait_recv()
+    total = g.ngain[0]
+    for i in range(7):
+        total = total + g.ngain[1 + i]
+    g.grad_gain[...] = total
+    for d in bcv:
+        d.wait_recv()
+    g.vec[8:16, 0:256] = g.bcv[0] + g.bcv[1] + g.bcv[2] + g.bcv[3]
+    t_bc.s6()
+    g.grad_bc[...] = g.p_bc[...]
+    t_x.s6()
+    store.append(pltpu.make_async_copy(g.p_x, g.grad_x, g.load_sem.at[7]))
+    store[2].start()
+    for d in pending:
+        d.wait_send()
+
+    @pl.when(s < SEQ - 1)
+    def _():
+        edge.wait_send()
+
+    @pl.when(s > 0)
+    def _():
+        ret.wait_send()
+
+    for j in range(1, HOPS + 1):
+        d = remote(g.state_out, g.states.at[j - 1], g.st_send.at[j - 1], g.st_recv.at[j - 1], {ALONG: s + j})
+
+        @pl.when(s + j < SEQ)
+        def _():
+            d.wait_send()
+
+        @pl.when(s - j >= 0)
+        def _():
+            back[j - 1].wait_send()
+
+    for j in range(1, HOPS):
+        up = remote(g.decay.at[0], g.decay.at[j], g.st_send.at[2 + j], g.st_recv.at[2 + j], {ALONG: s + j})
+        down_copy = remote(g.decay.at[0], g.decay.at[2 + j], g.st_send.at[4 + j], g.st_recv.at[4 + j], {ALONG: s - j})
+
+        @pl.when(s + j < SEQ)
+        def _():
+            up.wait_send()
+
+        @pl.when(s - j >= 0)
+        def _():
+            down_copy.wait_send()
+
+    for d in store:
+        d.wait()
+
+
+def fast_layer(
+    hidden_in, seq_lengths, norm_gain, w_z, w_x, w_bc, w_dt, conv_x_w, conv_x_b, conv_bc_w,
+    conv_bc_b, dt_bias, a_log, d_skip, gate_gain, w_out, cotangent,
+):
+    vectors = (norm_gain, conv_x_b, conv_bc_b, dt_bias, a_log, d_skip, gate_gain)
+    params = jnp.stack([jnp.pad(v, (0, CHANNELS - v.shape[0])) for v in vectors] + [jnp.zeros((CHANNELS,), F32)])
+    vm = pl.BlockSpec(memory_space=pltpu.VMEM)
+    hbm = pl.BlockSpec(memory_space=pl.ANY)
+    sm = pl.BlockSpec(memory_space=pltpu.SMEM)
+    ins = dict(
+        x_hbm=(hidden_in, hbm), cot_hbm=(cotangent, hbm), w_x=(w_x, hbm), w_z=(w_z, hbm), w_out=(w_out, hbm),
+        lengths=(seq_lengths, sm), params=(params, vm), w_bc=(w_bc, vm), w_dt=(w_dt, vm),
+        conv_x_w=(conv_x_w, vm), conv_bc_w=(conv_bc_w, vm),
+    )
+    outs = dict(
+        layer_out=((ROWS, BLOCK), BF, vm),
+        grad_in=((ROWS, BLOCK), F32, vm),
+        grad_out=((CHANNELS, D), BF, hbm),
+        grad_z=((D, CHANNELS), BF, hbm),
+        grad_x=((D, CHANNELS), BF, hbm),
+        grad_bc=((BLOCK, 256), F32, vm),
+        grad_dt=((16, D), F32, vm),
+        vec=((24, CHANNELS), F32, vm),
+        grad_gain=((8, BLOCK), F32, vm),
+    )
+    V = pltpu.VMEM
+    S = pltpu.SemaphoreType.DMA
+    scr = dict(
+        x=V((ROWS, BLOCK), BF),
+        wx=V((D, CHANNELS), BF),
+        wz=V((D, CHANNELS), BF),
+        wo=V((CHANNELS, D), BF),
+        xg=V((ROWS, D), BF),
+        xn=V((ROWS, D), BF),
+        cotg=V((ROWS, D), BF),
+        ssq=V((LINE, 8, ROWS), F32),
+        gains=V((LINE, 8, BLOCK), F32),
+        wbc=V((LINE, BLOCK, 256), BF),
+        wd=V((D, 128), BF),
+        taps=V((8, WIDE), F32),
+        spread=V((256, CHANNELS), BF),
+        segc=V((ROWS + HALO, 128), F32),
+        segr=V((8, ROWS), F32),
+        tri=V((SPAN, SPAN), BF),
+        skipe=V((8, CHANNELS), F32),
+        xscale=V((ROWS, 128), F32),
+        acc=V((ROWS, WIDE + CHANNELS + 128), F32),
+        edge=V((HALO, WIDE), BF),
+        halo=V((HALO, WIDE), BF),
+        cf=V((ROWS + HALO, WIDE), F32),
+        spre=V((ROWS, 128), F32),
+        step=V((ROWS, 128), F32),
+        cum=V((ROWS, 128), F32),
+        cumt=V((2, 16, SPAN), F32),
+        tail=V((ROWS, 128), F32),
+        load=V((ROWS, 128), F32),
+        lead=V((ROWS, 128), F32),
+        carry=V((2, 8, 128), F32),
+        carrye=V((2, 8, CHANNELS), F32),
+        decay=V((5, 8, CHANNELS), F32),
+        slope=V((ROWS + 16, WIDE), F32),
+        inner=V((ROWS, CHANNELS), BF),
+        b=V((ROWS, 128), BF),
+        c=V((ROWS, 128), BF),
+        bt=V((STATE, ROWS), F32),
+        ct=V((STATE, ROWS), F32),
+        loadt=V((2, 16, SPAN), F32),
+        leadt=V((2, 16, SPAN), F32),
+        stept=V((2, 16, SPAN), F32),
+        local=V((2, STATE, CHANNELS), F32),
+        state_out=V((STATE, CHANNELS), F32),
+        states=V((HOPS, STATE, CHANNELS), F32),
+        scores=V((SPAN, SPAN), F32),
+        gscores=V((SPAN, SPAN), F32),
+        out=V((ROWS, CHANNELS), F32),
+        sin=V((2, STATE, CHANNELS), F32),
+        slow=V((2, STATE, CHANNELS), BF),
+        gated=V((ROWS, CHANNELS), F32),
+        part=V((2, ROWS, 128), F32),
+        stats=V((LINE, 16, ROWS), F32),
+        vacc=V((2, 8, CHANNELS), F32),
+        gm=V((ROWS, CHANNELS), BF),
+        sent_grad=V((STATE, CHANNELS), F32),
+        gstates=V((HOPS, STATE, CHANNELS), F32),
+        gloc=V((2, STATE, CHANNELS), F32),
+        sblk=V((3, ROWS, BLOCK), BF),
+        rblk=V((3, ROWS, BLOCK), BF),
+        rblk2=V((3, ROWS, BLOCK), BF),
+        gsr=V((ROWS, 128), BF),
+        pack=V((24, CHANNELS), F32),
+        packs=V((7, 24, CHANNELS), F32),
+        ret_out=V((8, WIDE), F32),
+        ret_in=V((8, WIDE), F32),
+        wacc=V((5, 8, WIDE), F32),
+        gbc=V((2, ROWS, 256), BF),
+        tail_rows=V((16, WIDE), F32),
+        sbc=V((3, BLOCK, 256), BF),
+        rbc=V((3, BLOCK, 256), BF),
+        dt_out=V((16, D), BF),
+        dts=V((7, 16, D), BF),
+        bcv=V((LINE, 8, 256), F32),
+        nacc=V((8, BLOCK), F32),
+        nstat=V((LINE, 8, ROWS), F32),
+        ngain=V((8, 8, BLOCK), F32),
+        p_out=V((CHANNELS, D), BF),
+        p_z=V((D, CHANNELS), BF),
+        p_x=V((D, CHANNELS), BF),
+        p_bc=V((BLOCK, 256), F32),
+        load_sem=S((8,)),
+        edge_sem=S((4,)),
+        st_send=S((7,)),
+        st_recv=S((7,)),
+        gs_send=S((3,)),
+        gs_recv=S((3,)),
+        tot_send=S((40,)),
+        tot_recv=S((40,)),
+        freed=pltpu.SemaphoreType.REGULAR((12,)),
+    )
+    pairs = dict(
+        small=9,
+        gather=6,
+        wide=7,
+        stat=3,
+        block=6,
+        bcsem=3,
+        packsem=14,
+        bcvsem=3,
+        nsem=10,
+    )
+    sums = [(CHANNELS, D, BF), (D, CHANNELS, BF), (D, CHANNELS, BF), (BLOCK, 256, F32)]
+    bufs = [b for spec in sums for b in total_bufs(*spec)]
+    sems = [S((k,)) for k in pairs.values() for _ in range(2)]
+    names = [*ins, *outs, *scr]
+
+    def kernel(*refs):
+        n, m = len(names), len(names) + len(bufs)
+        d = dict(zip(names, refs[:n]))
+        rest = refs[m:]
+        for i, name in enumerate(pairs):
+            d[name] = (rest[2 * i], rest[2 * i + 1])
+        layer_kernel(d, refs[n:m])
+
+    res = pl.pallas_call(
+        kernel,
+        out_shape=[jax.ShapeDtypeStruct(sh, dt) for sh, dt, _ in outs.values()],
+        in_specs=[sp for _, sp in ins.values()],
+        out_specs=[sp for _, _, sp in outs.values()],
+        scratch_shapes=[*scr.values(), *bufs, *sems],
+        compiler_params=pltpu.CompilerParams(collective_id=0, has_side_effects=True, vmem_limit_bytes=66 * 2**20 - 2**21),
+        name="layer",
+    )(*[a for a, _ in ins.values()])
+    layer_out, grad_in, grad_out, grad_z, grad_x, grad_bc, grad_dt, vec, grad_gain = res
+    return (
+        layer_out, grad_in, grad_gain[0], grad_z.astype(F32), grad_x.astype(F32), grad_bc,
+        grad_dt[0:12].T, vec[0:4], vec[4], vec[8:12, 0:256], vec[12, 0:256], vec[16, 0:12], vec[16, 128:140],
+        jnp.sum(vec[6].reshape(12, HEAD_DIM), axis=1), vec[5], grad_out.astype(F32),
+    )
+
+
 def solution(mesh):
     placed = (
         P("seq", "head"),
@@ -437,8 +1581,9 @@
         P("head", None),
         P("seq", "head"),
     )
+    fits = mesh.shape["seq"] == SEQ and mesh.shape["head"] == LINE
     return jax.shard_map(
-        on_device,
+        fast_layer if fits else on_device,
         mesh=mesh,
         in_specs=placed,
         out_specs=(

time: 759 us -> 255 us (0.34); the launches traced: 749 us -> 254 us
  waiting for transfers between devices: 342 us -> 0 us
  Pallas kernels: 0 us -> 224 us
  blocking collectives: 143 us -> 0 us
  matrix products: 80.2 us -> 0 us
  local copies, waits for them, and re-layouts: 97.9 us -> 19 us
  other arithmetic: 60.1 us -> 10.4 us
  between operations: 16.2 us -> 0.67 us
    psum x2 -> x0, waiting for transfers between devices: 232 us -> none  [the longest x1 198 us: on_device(): lax.psum((grad_norm_gain, grad_w_z, grad_w_x, grad_w_bc, grad_w_dt, grad_...]
    pallas_call x0 -> x1, Pallas kernels: none -> 224 us  [fast_layer(): pl.pallas_call(kernel, out_shape=[jax.ShapeDtypeStruct(sh, dt) for sh, dt...]
    dot_general x42 -> x0, matrix products: 80.2 us -> none  [the longest x2 6.49 us: backward_span(): jnp.einsum('hip,hjp->hij', grad_y, inner_c, preferred_element_type=jnp.fl...]
    psum x5 -> x0, blocking collectives: 72.3 us -> none  [the longest x1 25.1 us: on_device(): lax.psum((grad_norm_gain, grad_w_z, grad_w_x, grad_w_bc, grad_w_dt, grad_...]
    reduce_scatter x2 -> x0, waiting for transfers between devices: 63.7 us -> none  [the longest x1 39.1 us: on_device(): lax.psum_scatter(partial_back, 'head', scatter_dimension=1, tiled=True)]
    all_gather x4 -> x0, waiting for transfers between devices: 43.8 us -> none  [the longest x2 23.6 us: prefix(): gathered = jax.tree.map(lambda a: lax.all_gather(a, axis), part)]
    unnamed x2 -> x0, blocking collectives: 41.4 us -> none
    all_gather x1 -> x0, blocking collectives: 29.2 us -> none  [on_device(): lax.all_gather(w_bc, 'head', axis=0, tiled=True)]
  transfers between devices with their start and end apart: 10 -> 0, of which waited for: 10 -> 0; matrix products, arithmetic and copies ran while one was open for 8% -> 0% of each run, Pallas kernels for 0% -> 0%
where the time goes in v1:
time: 255 us; the launch traced here: 254 us
  Pallas kernels  224 us (88%)
  local copies, waits for them, and re-layouts  19 us (7%)
  other arithmetic  10.4 us (4%)
    pallas_call x1, Pallas kernels, fast_layer(): pl.pallas_call(kernel, out_shape=[jax.ShapeDtypeStruct(sh, dt) for sh, dt...  224 us

profile of v1, /device:TPU:0, one launch (start us, length us, event | category | flops | bytes accessed | tf_op | source)
XLA Modules:
  0.0 254.0 jit_solution(15682555817125762139)
XLA Ops:
  0.6 0.7 stack.25
  1.3 0.7 stack.30
  2.0 0.7 pad.18
  2.7 0.7 pad.19
  3.4 0.7 pad.20
  4.1 0.7 pad.21
  4.7 0.7 pad.22
  5.4 0.7 stack.31.refs_6_
  6.1 1.8 copy.33.refs_8_
  7.8 224.0 %layer.1 = (bf16[512,384]{1,0:T(8,128)(2,1)}, f32[512,384]{1,0:T(8,128)}, bf16[768,1536]{1,0:T(8,128)(2,1)}, bf16[1536,768]{1,0:T(8,128)(2,1)}, bf16[1536,768]{1...) custom-call(bf16[512,384]{1,0:T(8,128)(2,1)} %refs_0_.1, ...), custom_call_target="tpu_custom_call" | custom-call | tf_op jit(solution)/shard_map/layer/pallas_call | solution.py:1547
  231.8 1.3 slice.35
  233.0 1.2 slice_bitcast_fusion.1
  234.2 1.3 slice_reduce_fusion.3
  235.5 1.3 slice.34
  236.8 1.3 slice.32
  238.2 1.5 slice_reduce_fusion
  239.6 0.1 reshape_squeeze.3
  239.7 0.6 reduce_sum.9
  240.3 1.5 slice_bitcast_fusion
  241.9 0.0 copy-start.1
  241.9 4.4 %convert_element_type.17 = f32[1536,768]{1,0:T(8,128)} convert(bf16[1536,768]{1,0:T(8,128)(2,1)} %get-tuple-element.28) | non-fusion elementwise | flops 1179648 | bytes 7077888 | tf_op jit(solution)/shard_map/convert_element_type | solution.py:1558
  246.2 0.0 copy-done.1
  246.2 0.0 copy-start
  246.2 2.5 %convert_element_type.18 = f32[1536,768]{1,0:T(8,128)} convert(bf16[1536,768]{1,0:T(8,128)(2,1)S(1)} %copy-done.1) | non-fusion elementwise | flops 1179648 | bytes 7077888 | tf_op jit(solution)/shard_map/convert_element_type | solution.py:1558
  248.8 0.0 copy-done
  248.8 0.0 copy-start.4
  248.8 0.0 copy-start.2
  248.8 2.8 %convert_element_type.19 = f32[768,1536]{1,0:T(8,128)} convert(bf16[768,1536]{1,0:T(8,128)(2,1)S(1)} %copy-done) | non-fusion elementwise | flops 1179648 | bytes 7077888 | tf_op jit(solution)/shard_map/convert_element_type | solution.py:1560
  251.6 0.0 copy-done.4
  251.6 0.0 copy-start.3
  251.6 0.7 copy.37
  252.4 0.0 copy-done.2
  252.4 0.9 copy.38
  253.3 0.0 copy-done.3
  253.3 0.7 copy.39
  (6 shorter events, 0.0 us)
Async XLA Ops:
  241.9 4.4 %copy-start.1 = (bf16[1536,768]{1,0:T(8,128)(2,1)S(1)}, bf16[1536,768]{1,0:T(8,128)(2,1)}, u32[]{:S(2)}) copy-start(bf16[1536,768]{1,0:T(8,128)(2,1)} %get-tuple-element.29) | copy-start | bytes 7077892
  246.2 2.5 %copy-start = (bf16[768,1536]{1,0:T(8,128)(2,1)S(1)}, bf16[768,1536]{1,0:T(8,128)(2,1)}, u32[]{:S(2)}) copy-start(bf16[768,1536]{1,0:T(8,128)(2,1)} %get-tuple-element.33) | copy-start | bytes 7077892
  248.8 2.8 %copy-start.4 = (bf16[512,384]{1,0:T(8,128)(2,1)S(1)}, bf16[512,384]{1,0:T(8,128)(2,1)}, u32[]{:S(2)}) copy-start(bf16[512,384]{1,0:T(8,128)(2,1)} %get-tuple-element.55) | copy-start | bytes 1179652
  248.8 3.6 %copy-start.2 = (f32[512,384]{1,0:T(8,128)S(1)}, f32[512,384]{1,0:T(8,128)}, u32[]{:S(2)}) copy-start(f32[512,384]{1,0:T(8,128)} %get-tuple-element.56) | copy-start | bytes 2359300
  251.6 1.6 copy-start.3

commit v2 on v1

--- a/solution.py
+++ b/solution.py
@@ -427,7 +427,6 @@
 CHANNELS = 768
 WIDE = 1024
 HALO = 16
-HOPS = 3
 SEQ = 8
 LINE = 4
 ALONG = "seq"
@@ -452,6 +451,11 @@
         out.append(p)
         v = v - p.astype(F32)
     return out
+
+
+def along_line(z, ends, middles):
+    k = jnp.where(lax.rem(z, 3) == 0, ends, middles)
+    return jnp.where(z >= 2, 3 - k, k)
 
 
 def lanes_sum(v):
@@ -633,6 +637,12 @@
         d.start()
         loads.append(d)
 
+    g.params[...] = jnp.zeros(g.params.shape, F32)
+    vectors = (g.norm_gain, g.conv_x_b, g.conv_bc_b, g.dt_bias, g.a_log, g.d_skip, g.gate_gain)
+    for i, v in enumerate(vectors):
+        for n in range(v.shape[0]):
+            g.params[i : i + 1, 128 * n : 128 * n + v.shape[1]] = v[n : n + 1, :]
+
     sem = pltpu.get_barrier_semaphore()
     for p in zpeers + speers:
         pl.semaphore_signal(sem, inc=1, device_id=p, device_id_type=MESH)
@@ -660,11 +670,39 @@
         small.append(send(g.ssq.at[z], g.ssq.at[z], g.small, i, p))
         small.append(send(g.gains.at[z], g.gains.at[z], g.small, 3 + i, p))
         small.append(send(g.w_bc.at[piece], g.wbc.at[z, piece], g.small, 6 + i, p))
-    xin = [send(g.x, g.xg.at[:, own], g.gather, i, p) for i, p in enumerate(zpeers)]
-    cin = [send(g.cotg.at[:, own], g.cotg.at[:, own], g.gather, 3 + i, p) for i, p in enumerate(zpeers)]
+    middle = lax.rem(z, 3) != 0
+    near = [along_line(z, a, b) for a, b in ((1, 2), (2, 0), (3, 3))]
+
+    def block_copy(src, whole, base, slot, k, to):
+        cols = cut(k * BLOCK, BLOCK, 128)
+        return remote(src, whole.at[:, cols], g.gather_s.at[base + slot], g.gather_r.at[base + k], {ACROSS: to})
+
+    def gather(src, whole, base):
+        for j in range(2):
+            pending.append(block_copy(src, whole, base, j, z, near[j]))
+            pending[-1].start()
+        third = block_copy(src, whole, base, 2, z, near[2])
+
+        @pl.when(jnp.logical_not(middle))
+        def _():
+            third.start()
+
+        return third
+
+    def gathered(src, whole, base, j):
+        block_copy(src, whole, base, 0, near[j], z).wait_recv()
+
+    def relay(whole, base):
+        part = whole.at[:, cut(near[0] * BLOCK, BLOCK, 128)]
+
+        @pl.when(middle)
+        def _():
+            block_copy(part, whole, base, 2, near[0], near[1]).start()
+
+    x_third = gather(g.x, g.xg, 0)
 
     g.wd[...] = jnp.zeros(g.wd.shape, BF)
-    g.wd[:, 0:12] = g.w_dt[...]
+    g.wd[0:12, :] = g.w_dt[...]
     g.taps[...] = jnp.zeros(g.taps.shape, F32)
     g.taps[0:4, 0:CHANNELS] = g.conv_x_w[...]
     g.taps[0:4, CHANNELS:WIDE] = g.conv_bc_w[...]
@@ -737,31 +775,36 @@
 
         loop(cols // width, body)
 
-    def project_bc(k, first):
-        p = mul(g.xn[:, cut(k * BLOCK, BLOCK, 128)], g.wbc[k])
+    def project_dt(k, first):
+        at = cut(k * BLOCK, BLOCK, 128)
+        p = mul(g.xn[:, at], g.wd[:, at], NT)
         if first:
-            g.acc[:, CHANNELS:WIDE] = p
+            g.acc[:, WIDE + CHANNELS :] = p
         else:
-            g.acc[:, CHANNELS:WIDE] += p
+            g.acc[:, WIDE + CHANNELS :] += p
 
     normalise(z, lambda at, cols: g.x[at, :])
     loads[1].wait()
     loads[2].wait()
     project(z, g.wx, CHANNELS, 0, True)
     project(z, g.wz, CHANNELS, WIDE, True)
-    project(z, g.wd, 128, WIDE + CHANNELS, True, 128)
+    project_dt(z, True)
+    for i, k in enumerate(near):
+        gathered(g.x, g.xg, 0, i)
+        if i == 0:
+            relay(g.xg, 0)
+        if i == 2:
+            pending.append(gather(g.cotg.at[:, own], g.cotg, 4))
+        normalise(k, lambda at, cols: g.xg[at, cols])
+        project(k, g.wx, CHANNELS, 0, False)
+        if i < 2:
+            project(k, g.wz, CHANNELS, WIDE, False)
+            project_dt(k, False)
     for d in wide:
         d.wait_recv()
-    project_bc(z, True)
-    ks = [lax.rem(z + LINE - d, LINE) for d in range(1, LINE)]
-    for i, k in enumerate(ks):
-        xin[i].wait_recv()
-        normalise(k, lambda at, cols: g.xg[at, cols])
-        project(k, g.wx, CHANNELS, 0, False)
-        project_bc(k, False)
-        if i < 2:
-            project(k, g.wz, CHANNELS, WIDE, False)
-            project(k, g.wd, 128, WIDE + CHANNELS, False, 128)
+    g.acc[:, CHANNELS:WIDE] = sum(
+        mul(g.xn[:, BLOCK * k : BLOCK * k + BLOCK], g.wbc[k]) for k in range(LINE)
+    )
 
     g.edge[...] = g.acc[ROWS - HALO : ROWS, 0:WIDE].astype(BF)
     edge = remote(g.edge, g.halo, g.edge_sem.at[0], g.edge_sem.at[1], {ALONG: s + 1})
@@ -780,11 +823,10 @@
         )
 
     loop(ROWS // 64, put)
-    project(ks[2], g.wz, CHANNELS, WIDE, False)
-    project(ks[2], g.wd, 128, WIDE + CHANNELS, False, 128)
+    project(near[2], g.wz, CHANNELS, WIDE, False)
+    project_dt(near[2], False)
 
     step_pre = g.acc[:, WIDE + CHANNELS :] + g.params[3:4, 0:128]
-    g.spre[...] = step_pre
     g.step[...] = jnp.where(lane < 12, jax.nn.softplus(step_pre), 0.0)
     for q in range(2):
         rows = pl.ds(q * SPAN, SPAN)
@@ -810,12 +852,6 @@
         g.carrye[q] = spread(jnp.broadcast_to(carry, (8, 128)))
     g.decay[0] = g.carrye[0] * g.carrye[1]
 
-    @pl.when(s > 0)
-    def _():
-        edge.wait_recv()
-
-    g.cf[0:HALO, :] = g.halo[...].astype(F32)
-
     def taps_of(first, cols):
         v = g.cf[cut(first + 8, 72, 8), cols]
         sv = g.segc[cut(first + 8, 72, 8), :]
@@ -844,7 +880,14 @@
                 g.b[at, :] = act[:, 0:128]
                 g.c[at, :] = act[:, 128:256]
 
-    loop(ROWS // 64, convolve)
+    loop(ROWS // 64 - 1, lambda i: convolve(i + 1))
+
+    @pl.when(s > 0)
+    def _():
+        edge.wait_recv()
+
+    g.cf[0:HALO, :] = g.halo[...].astype(F32)
+    convolve(0)
 
     g.bt[...] = g.b[...].astype(F32).T
     g.ct[...] = g.c[...].astype(F32).T
@@ -862,52 +905,92 @@
 
     outer(g.bt, g.loadt, g.inner)
     c0, c1 = g.carrye[0][0:1], g.carrye[1][0:1]
-    g.state_out[...] = (c1 * g.local[0] + g.local[1])
-    for j in range(1, HOPS + 1):
-        ahead = s + j < SEQ
-        behind = s - j >= 0
-        d = remote(g.state_out, g.states.at[j - 1], g.st_send.at[j - 1], g.st_recv.at[j - 1], {ALONG: s + j})
-
-        @pl.when(ahead)
+    core, chip = me[0], s // 2
+    half, rest = cut(core * BLOCK, BLOCK, 128), cut((1 - core) * BLOCK, BLOCK, 128)
+    partner = {ALONG: s + 1 - 2 * core}
+    later = []
+
+    class Chain:
+        def __init__(self, mine, other, joined, got, result, base, way):
+            self.mine, self.other, self.joined, self.got, self.result = mine, other, joined, got, result
+            self.base, self.way = base, way
+            self.near = self.link(joined, got.at[0], 1, way)
+            self.far = self.link(joined, got.at[1], 2, 2 * way)
+
+        def link(self, src, dst, i, hop):
+            to = {ALONG: s + 2 * hop}
+            return remote(src, dst, g.st_send.at[self.base + i], g.st_recv.at[self.base + i], to)
+
+        def share(self):
+            self.first = send(self.mine, self.other, (g.st_send, g.st_recv), self.base, partner)
+
+        def join(self):
+            self.first.wait_recv()
+            own, other = self.mine[:, half], self.other[:, half]
+            even, odd = jnp.where(core == 0, own, other), jnp.where(core == 0, other, own)
+            if self.way > 0:
+                self.joined[...] = odd_decay() * even + odd
+            else:
+                self.joined[...] = even + even_decay() * odd
+            for d, hop in ((self.near, 1), (self.far, 2)):
+                pass_on(d, hop * self.way)
+            for i, hop in ((0, 1), (1, 2)):
+                outside = chip - hop * self.way
+
+                @pl.when((outside < 0) | (outside > 3))
+                def _():
+                    self.got[i] = jnp.zeros((STATE, BLOCK), F32)
+
+        def meet(self, decay):
+            for d, hop in ((self.near, 1), (self.far, 2)):
+                arrive(d, hop * self.way)
+            self.result[:, half] = self.got[0] + decay * self.got[1]
+            p = self.result.at[:, half]
+            self.last = send(p, p, (g.st_send, g.st_recv), self.base + 3, partner)
+
+        def end(self):
+            self.last.wait_recv()
+
+    def pass_on(d, hop):
+        inside = (chip + hop >= 0) & (chip + hop <= 3)
+
+        @pl.when(inside)
         def _():
             d.start()
 
-        @pl.when(jnp.logical_not(behind))
+        later.append((inside, d))
+
+    def arrive(d, hop):
+        @pl.when((chip - hop >= 0) & (chip - hop <= 3))
         def _():
-            g.states[j - 1] = jnp.zeros((STATE, CHANNELS), F32)
-
-    for j in range(1, HOPS):
-        up = remote(g.decay.at[0], g.decay.at[j], g.st_send.at[2 + j], g.st_recv.at[2 + j], {ALONG: s + j})
-        down = remote(g.decay.at[0], g.decay.at[2 + j], g.st_send.at[4 + j], g.st_recv.at[4 + j], {ALONG: s - j})
-
-        @pl.when(s + j < SEQ)
-        def _():
-            up.start()
-
-        @pl.when(s - j >= 0)
-        def _():
-            down.start()
-
-        @pl.when(s - j < 0)
-        def _():
-            g.decay[j] = jnp.zeros((8, CHANNELS), F32)
-
-        @pl.when(s + j >= SEQ)
-        def _():
-            g.decay[2 + j] = jnp.zeros((8, CHANNELS), F32)
+            d.wait_recv()
+
+    def odd_decay():
+        return jnp.where(core == 0, g.decay[1, 0:1, half], g.decay[0, 0:1, half])
+
+    def even_decay():
+        return jnp.where(core == 0, g.decay[0, 0:1, half], g.decay[1, 0:1, half])
+
+    g.mine[...] = c1 * g.local[0] + g.local[1]
+    ahead = Chain(g.mine, g.other, g.joined, g.got, g.chain, 0, 1)
+    ahead.share()
+    dec = send(g.decay.at[0], g.decay.at[1], (g.st_send, g.st_recv), 8, partner)
+    both_up = remote(g.both, g.boths.at[0], g.st_send.at[9], g.st_recv.at[9], {ALONG: s + 2})
+    both_down = remote(g.both, g.boths.at[1], g.st_send.at[10], g.st_recv.at[10], {ALONG: s - 2})
 
     def head_cols(ref, rows, p):
         moved = pltpu.roll(ref[rows, :], lax.rem(128 - 2 * p, 128), 1)
         return moved[:, 0:1], moved[:, 1:2]
 
-    def inside(q):
+    def inside(q, first, count):
         rows = cut(q * SPAN, SPAN, 256)
         seg = g.segc[cut(HALO + q * SPAN, SPAN, 16), 0:1]
         segr = g.segr[0:1, cut(q * SPAN, SPAN, 256)]
         scores = mul(g.c[rows, :], g.b[rows, :], NT)
         g.scores[...] = jnp.where((tri_i >= tri_j) & (seg == segr), scores, 0.0)
 
-        def pair(p):
+        def pair(t):
+            p = first + t
             cols = head_cols(g.cum, rows, p)
             at = cut(p * 128, 128, 128)
             outs = []
@@ -918,26 +1001,37 @@
                 outs.append(mul((g.scores[...] * fall * step).astype(BF), g.inner[rows, at]))
             g.out[rows, at] = jnp.where(left, outs[0], outs[1])
 
-        loop(6, pair)
-
-    loop(2, inside)
-
-    for j in range(1, HOPS + 1):
-        d = remote(g.state_out, g.states.at[j - 1], g.st_send.at[j - 1], g.st_recv.at[j - 1], {ALONG: s + j})
-
-        @pl.when(s - j >= 0)
+        loop(count, pair)
+
+    inside(0, 0, 3)
+    dec.wait_recv()
+    g.both[...] = g.decay[0, :, half] * g.decay[1, :, half]
+    ahead.join()
+    pass_on(both_up, 1)
+    pass_on(both_down, -1)
+    for i, hop in ((0, 1), (1, -1)):
+        @pl.when((chip - hop < 0) | (chip - hop > 3))
         def _():
-            d.wait_recv()
-
-    for j in range(1, HOPS):
-        up = remote(g.decay.at[0], g.decay.at[j], g.st_send.at[2 + j], g.st_recv.at[2 + j], {ALONG: s + j})
-
-        @pl.when(s - j >= 0)
-        def _():
-            up.wait_recv()
-
-    got = [g.states[j].astype(F32) for j in range(HOPS)]
-    incoming = got[0] + g.decay[1][0:1] * (got[1] + g.decay[2][0:1] * got[2])
+            g.boths[i] = jnp.zeros((8, BLOCK), F32)
+
+    inside(0, 3, 3)
+    gathered(g.cotg.at[:, own], g.cotg, 4, 0)
+    relay(g.cotg, 4)
+    inside(1, 0, 6)
+
+    arrive(both_up, 1)
+    ahead.meet(g.boths[0, 0:1, :])
+
+    def act(i):
+        at = cut(i * 64, 64, 16)
+        pre = g.acc[at, gate_cols]
+        g.gated[at, :] = pre * jax.nn.sigmoid(pre)
+
+    gate_cols = pl.ds(WIDE, CHANNELS)
+    loop(ROWS // 64, act)
+    ahead.end()
+    from_chips = g.chain[...]
+    incoming = jnp.where(core == 0, from_chips, g.other[...] + g.decay[1, 0:1] * from_chips)
     g.sin[0] = incoming
     g.sin[1] = g.local[0] + c0 * incoming
     for q in range(2):
@@ -953,44 +1047,57 @@
 
     loop(12, outside)
 
-    gate_cols = pl.ds(WIDE, CHANNELS)
     skip = g.skipe[0:1]
 
     def gate(i):
         at = cut(i * 64, 64, 16)
-        pre = g.acc[at, gate_cols]
         mixed = g.out[at, :] + g.inner[at, :].astype(F32) * skip
-        gated = mixed * (pre * jax.nn.sigmoid(pre))
+        gated = mixed * g.gated[at, :]
         g.gated[at, :] = gated
         g.part[0, at, :] = lanes_sum(gated * gated)
 
     loop(ROWS // 64, gate)
 
-    for d in cin:
-        d.wait_recv()
     loads[4].wait()
     gate_gain = g.params[6:7, :]
 
-    def down(n):
-        g.ggn[:, cut(n * 256, 256, 256)] = mul(g.cotg[...], g.wo[cut(n * 256, 256, 256), :], NT)
-
-    loop(3, down)
+    def down(k, first):
+        at = cut(k * BLOCK, BLOCK, 128)
+
+        def body(n):
+            cols = cut(n * 256, 256, 256)
+            p = mul(g.cotg[:, at], g.wo[cols, at], NT)
+            if first:
+                g.ggn[:, cols] = p
+            else:
+                g.ggn[:, cols] += p
+
+        loop(3, body)
+
+    down(z, True)
+    for i, k in enumerate(near):
+        if i > 0:
+            gathered(g.cotg.at[:, own], g.cotg, 4, i)
+        down(k, False)
 
     def inner_part(i):
         at = cut(i * 64, 64, 16)
         g.part[1, at, :] = lanes_sum(g.ggn[at, :] * gate_gain * g.gated[at, :])
 
     loop(ROWS // 64, inner_part)
-    g.stats[z, 0:8, :] = jnp.broadcast_to(to_row(g.part[0]), (8, ROWS))
-    g.stats[z, 8:16, :] = jnp.broadcast_to(to_row(g.part[1]), (8, ROWS))
+    which = lax.broadcasted_iota(jnp.int32, (8, ROWS), 0)
+    g.stats[z] = jnp.where(which == 0, to_row(g.part[0]), to_row(g.part[1]))
     stat = [send(g.stats.at[z], g.stats.at[z], g.stat, i, p) for i, p in enumerate(zpeers)]
     for d in stat:
         d.wait_recv()
     sums = g.stats[0] + g.stats[1] + g.stats[2] + g.stats[3]
     gscale = lax.rsqrt(sums[0:1] / INNER + epsilon)
     g.part[0] = to_col(gscale)
-    g.part[1] = to_col(gscale * gscale * gscale * sums[8:9] / INNER)
+    g.part[1] = to_col(gscale * gscale * gscale * sums[1:2] / INNER)
+    x_third.wait_send()
     g.vacc[...] = jnp.zeros(g.vacc.shape, F32)
+    g.pack[...] = jnp.zeros(g.pack.shape, F32)
+    g.bcv[z] = jnp.zeros((8, 256), F32)
 
     def ungate(i):
         at = cut(i * 64, 64, 16)
@@ -1011,33 +1118,21 @@
     loop(ROWS // 64, ungate)
 
     outer(g.ct, g.leadt, g.gm)
-    g.sent_grad[...] = (g.local[0] + c0 * g.local[1])
-    back = []
-    for j in range(1, HOPS + 1):
-        d = remote(g.sent_grad, g.gstates.at[j - 1], g.gs_send.at[j - 1], g.gs_recv.at[j - 1], {ALONG: s - j})
-        back.append(d)
-
-        @pl.when(s - j >= 0)
-        def _():
-            d.start()
-
-        @pl.when(s + j >= SEQ)
-        def _():
-            g.gstates[j - 1] = jnp.zeros((STATE, CHANNELS), F32)
-
-    def total_of(i, ref, n):
-        return Total(ref, sum_bufs[5 * i : 5 * i + 5], g.tot_send, g.tot_recv, g.freed, 10 * i, me)
-
-    t_out = total_of(0, g.p_out, 0)
-    t_z = total_of(1, g.p_z, 0)
-    t_x = total_of(2, g.p_x, 0)
-    t_bc = total_of(3, g.p_bc, 0)
+    g.mine_b[...] = g.local[0] + c0 * g.local[1]
+    behind = Chain(g.mine_b, g.other_b, g.joined_b, g.got_b, g.chain_b, 4, -1)
+    behind.share()
+
+    t_out, t_z, t_x, t_rest = [
+        Total(ref, sum_bufs[5 * i : 5 * i + 5], g.tot_send, g.tot_recv, g.freed, 10 * i, me)
+        for i, ref in enumerate((g.p_out, g.p_z, g.p_x, g.p_rest))
+    ]
 
     def grad_out(n):
         at = cut(n * 256, 256, 256)
         g.p_out[at, :] = mul(g.gn[:, at], g.cotg[...], TN).astype(BF)
 
     loop(3, grad_out)
+    behind.join()
     t_out.s0()
 
     def grad_z(n):
@@ -1048,24 +1143,83 @@
     t_z.s0()
     t_out.s1()
 
-    outs = []
-    for i, p in enumerate(zpeers):
-        k = lax.rem(z + 1 + i, LINE)
-        g.sblk[i] = mul(g.gn[...], g.wo[:, cut(k * BLOCK, BLOCK, 128)]).astype(BF)
-        outs.append(send(g.sblk.at[i], g.rblk.at[i], g.block, i, p))
+    dests = [along_line(z, a, b) for a, b in ((2, 3), (3, 0), (1, 2))]
+
+    class Scatter:
+        def __init__(self, sent, got, via, base):
+            self.sent, self.got, self.via, self.base = sent, got, via, base
+
+        def copy(self, j, dst, i, to):
+            return remote(self.sent.at[j], dst, g.block_s.at[self.base + j], g.block_r.at[self.base + i], {ACROSS: to})
+
+        def direct(self, j):
+            slot = lax.rem(z - dests[j] + 7, 4)
+            return self.copy(j, self.got.at[slot], slot, dests[j])
+
+        def block(self, j, value):
+            v = value
+            if j == 2:
+                @pl.when(middle)
+                def _():
+                    self.copy(0, self.via, 3, z).wait_recv()
+
+                v = v + self.via[...].astype(F32)
+            self.sent[j] = v.astype(BF)
+            if j == 0:
+                @pl.when(middle)
+                def _():
+                    self.direct(0).start()
+
+                @pl.when(jnp.logical_not(middle))
+                def _():
+                    self.copy(0, self.via, 3, dests[2]).start()
+            else:
+                self.direct(j).start()
+
+        def arrived(self):
+            for i in (0, 2):
+                self.copy(0, self.got.at[i], i, z).wait_recv()
+
+            @pl.when(jnp.logical_not(middle))
+            def _():
+                self.copy(0, self.got.at[1], 1, z).wait_recv()
+
+        def left(self):
+            for j in range(3):
+                self.copy(j, self.via, 3, z).wait_send()
+
+    out_blocks = Scatter(g.sblk, g.rblk, g.via, 0)
+    in_blocks = Scatter(g.sblk2, g.rblk2, g.via2, 4)
+
+    @pl.when(middle)
+    def _():
+        g.rblk[1] = jnp.zeros((ROWS, BLOCK), BF)
+        g.rblk2[1] = jnp.zeros((ROWS, BLOCK), BF)
+
+    @pl.when(jnp.logical_not(middle))
+    def _():
+        g.via[...] = jnp.zeros((ROWS, BLOCK), BF)
+        g.via2[...] = jnp.zeros((ROWS, BLOCK), BF)
+
+    def out_block(k):
+        return mul(g.gn[...], g.wo[:, cut(k * BLOCK, BLOCK, 128)])
+
+    out_blocks.block(0, out_block(dests[0]))
+    out_blocks.block(1, out_block(dests[1]))
+    t_z.s1()
     g.own[...] = mul(g.gn[...], g.wo[:, own])
-    t_z.s1()
-
-    def inside_back(q):
+
+    def inside_back(q, first, count):
         rows = cut(q * SPAN, SPAN, 256)
         seg = g.segc[cut(HALO + q * SPAN, SPAN, 16), 0:1]
         segr = g.segr[0:1, cut(q * SPAN, SPAN, 256)]
-        scores = mul(g.b[rows, :], g.c[rows, :], NT)
         mask = (tri_i <= tri_j) & (seg == segr)
-        g.scores[...] = jnp.where(mask, scores, 0.0)
-        g.gscores[...] = jnp.zeros((SPAN, SPAN), F32)
-
-        def pair(p):
+        if first == 0:
+            g.scores[...] = jnp.where(mask, mul(g.b[rows, :], g.c[rows, :], NT), 0.0)
+            g.gscores[...] = jnp.zeros((SPAN, SPAN), F32)
+
+        def pair(t):
+            p = first + t
             cols = head_cols(g.cum, rows, p)
             at = cut(p * 128, 128, 128)
             steps = head_cols(g.step, rows, p)
@@ -1080,34 +1234,27 @@
                 g.gscores[...] += mul(vals, gm, NT) * fall
             g.z[rows, at] = jnp.where(left, outs[0], outs[1])
 
-        loop(6, pair)
+        loop(count, pair)
+        if first + count < 6:
+            return
         gs = jnp.where(mask, g.gscores[...], 0.0)
         hi, lo = parts(gs, 2)
         g.gb[rows, :] = mul(hi, g.c[rows, :]) + mul(lo, g.c[rows, :])
         g.gc[rows, :] = mul(hi, g.b[rows, :], TN) + mul(lo, g.b[rows, :], TN)
 
-    inside_back(1)
+    inside_back(1, 0, 6)
+    arrive(both_down, -1)
+    behind.meet(g.boths[1, 0:1, :])
+    out_blocks.block(2, out_block(dests[2]))
+    inside_back(0, 0, 3)
     t_out.s2()
-    inside_back(0)
-    t_z.s2()
-
-    for j in range(1, HOPS + 1):
-        @pl.when(s + j < SEQ)
-        def _():
-            back[j - 1].wait_recv()
-
-    for j in range(1, HOPS):
-        d = remote(g.decay.at[0], g.decay.at[2 + j], g.st_send.at[4 + j], g.st_recv.at[4 + j], {ALONG: s - j})
-
-        @pl.when(s + j < SEQ)
-        def _():
-            d.wait_recv()
-
-    got = [g.gstates[j].astype(F32) for j in range(HOPS)]
-    beyond = got[0] + g.decay[3][0:1] * (got[1] + g.decay[4][0:1] * got[2])
+    inside_back(0, 3, 3)
+
+    behind.end()
+    from_chips = g.chain_b[...]
+    beyond = jnp.where(core == 1, from_chips, g.other_b[...] + g.decay[1, 0:1] * from_chips)
     g.gloc[1] = beyond
     g.gloc[0] = g.local[1] + c1 * beyond
-    t_out.s3()
     ends = []
     for q in range(2):
         rows = pl.ds(q * SPAN, SPAN)
@@ -1130,20 +1277,22 @@
         gcum = gcum + jnp.where(is_last, end, 0.0)
         glog = sum(mul(g.tri[...], p, TN) for p in parts(gcum, 3))
         gstep = jnp.where(step > 1e-30, q1 / jnp.maximum(step, 1e-30), 0.0) + q2 * g.tail[rows, :]
-        gpre = (gstep - rates * glog) * jax.nn.sigmoid(g.spre[rows, :])
+        gpre = (gstep - rates * glog) * jax.nn.sigmoid(
+            g.acc[rows, WIDE + CHANNELS :] + g.params[3:4, 0:128]
+        )
         g.gsr[rows, :] = gpre.astype(BF)
         ends.append((rows_sum(gpre), rows_sum(glog * (-rates * step))))
         g.z[rows, :] = zed + loade * bg + skip * gm
         g.gb[rows, :] += sum(mul(p, glow, NT) for p in parts(vals * loade, 2))
         g.gc[rows, :] += sum(mul(p, g.slow[q], NT) for p in parts(gm * spread(g.lead[rows, :]), 2))
+        if q == 0:
+            t_z.s2()
     g.pack[16:24, 0:128] = jnp.broadcast_to(
         jnp.sum(ends[0][0] + ends[1][0], axis=0, keepdims=True), (8, 128)
     )
     g.pack[16:24, 128:256] = jnp.broadcast_to(
         jnp.sum(ends[0][1] + ends[1][1], axis=0, keepdims=True), (8, 128)
     )
-    t_z.s3()
-
     def grads_of(at, n):
         cols = pl.ds(n * 256, 256)
         if n < 3:
@@ -1159,10 +1308,6 @@
 
     g.gconv[ROWS : ROWS + 16, :] = jnp.zeros((16, WIDE), F32)
     loop(ROWS // 64, slopes)
-
-    def same_ahead(first, count, shift):
-        sv = g.segc[cut(first + HALO, count + 8, 8), :] if count else None
-        return sv
 
     v = g.gconv[0:8, :]
     sv = g.segc[HALO - 8 : HALO + 8, :]
@@ -1185,6 +1330,7 @@
         g.ret_in[...] = jnp.zeros((8, WIDE), F32)
 
     g.wacc[...] = jnp.zeros(g.wacc.shape, F32)
+    t_out.s3()
 
     def convolve_back(i):
         first = i * 64
@@ -1218,7 +1364,7 @@
             g.wacc[4, :, cols] += rows_sum(here)
 
     loop(ROWS // 64, convolve_back)
-    t_out.s4()
+    t_z.s3()
 
     @pl.when(s < SEQ - 1)
     def _():
@@ -1232,11 +1378,16 @@
     def bc_block(at):
         return sum(mul(g.xn[:, at], g.gbc[k], TN) for k in range(2))
 
+    for k in range(5):
+        row = jnp.sum(g.wacc[k], axis=0, keepdims=True)
+        g.pack[k : k + 1, :] = row[:, 0:CHANNELS]
+        g.bcv[z, k : k + 1, :] = row[:, CHANNELS:WIDE]
+    bcv = [send(g.bcv.at[z], g.bcv.at[z], g.bcvsem, i, p) for i, p in enumerate(zpeers)]
     bcs = []
-    for i, p in enumerate(zpeers):
-        k = lax.rem(z + 1 + i, LINE)
-        g.sbc[i] = bc_block(cut(k * BLOCK, BLOCK, 128)).astype(BF)
-        bcs.append(send(g.sbc.at[i], g.rbc.at[i], g.bcsem, i, p))
+    for k in range(LINE):
+        g.sbc[k] = bc_block(pl.ds(BLOCK * k, BLOCK)).astype(BF)
+    mine, other = cut(core * 192, 192, 16), cut((1 - core) * 192, 192, 16)
+    halves = send(g.sbc.at[:, other], g.hbc, g.bcsem, 3, partner)
 
     def grad_x(n):
         at = cut(n * 256, 256, 256)
@@ -1244,77 +1395,69 @@
 
     loop(6, grad_x)
     t_x.s0()
-    t_z.s4()
+    halves.wait_recv()
+    bc_rows = cut(core * 320, 192, 16)
+    g.p_rest[bc_rows, :] = g.sbc[z, mine, :].astype(F32) + g.hbc[z].astype(F32)
+    for i, p in enumerate(zpeers):
+        k = lax.rem(z + 1 + i, LINE)
+        g.sbc[k, mine, :] = (g.sbc[k, mine, :].astype(F32) + g.hbc[k].astype(F32)).astype(BF)
+        bcs.append(send(g.sbc.at[k, mine], g.rbc.at[i], g.bcsem, i, p))
 
     def back_block(k):
         at = cut(k * BLOCK, BLOCK, 16)
         v = mul(g.gx[...], g.wx[at, :], NT) + mul(g.gz[...], g.wz[at, :], NT)
-        return v + mul(g.gsr[...], g.wd[at, :], NT) + mul(g.gbc[0], g.wbc[k], NT) + mul(g.gbc[1], g.wbc[k], NT)
-
-    for d in outs:
-        d.wait_recv()
-        d.wait_send()
-        pending[:] = [q for q in pending if q is not d]
+        return v + mul(g.gsr[...], g.wd[:, cut(k * BLOCK, BLOCK, 128)]) + mul(g.gbc[0], g.wbc[k], NT) + mul(g.gbc[1], g.wbc[k], NT)
+
+    out_blocks.arrived()
+    out_blocks.left()
     out_sum = g.own[...]
     for i in range(3):
         out_sum = out_sum + g.rblk[i].astype(F32)
     g.layer_out[...] = (g.x[...].astype(F32) + out_sum).astype(BF)
-    ins = []
-    for i, p in enumerate(zpeers):
-        k = lax.rem(z + 1 + i, LINE)
-        g.sblk2[i] = back_block(k).astype(BF)
-        ins.append(send(g.sblk2.at[i], g.rblk2.at[i], g.block, 3 + i, p))
-        if i == 0:
-            t_x.s1()
-            t_out.s5()
+    in_blocks.block(0, back_block(dests[0]))
+    t_x.s1()
+    t_out.s4()
+    in_blocks.block(1, back_block(dests[1]))
     g.own[...] = back_block(z)
-
-    for k in range(5):
-        row = jnp.sum(g.wacc[k], axis=0, keepdims=True)
-        g.pack[k : k + 1, :] = row[:, 0:CHANNELS]
-        g.pack[8 + k : 9 + k, 0:256] = row[:, CHANNELS:WIDE]
+    in_blocks.block(2, back_block(dests[2]))
+    t_x.s2()
+    t_z.s4()
+
+    for d in bcs + bcv:
+        d.wait_recv()
+    g.pack[8:16, 0:256] = g.bcv[0] + g.bcv[1] + g.bcv[2] + g.bcv[3]
     g.pack[5:6, :] = jnp.sum(g.vacc[0], axis=0, keepdims=True)
-    g.pack[6:7, :] = jnp.sum(g.vacc[1], axis=0, keepdims=True)
-    g.dt_out[...] = mul(g.gsr[...], g.xn[...], TN)[0:16].astype(BF)
-    packs = []
-    for i, p in enumerate(speers):
-        packs.append(send(g.pack, g.packs.at[i], g.packsem, i, p))
-        packs.append(send(g.dt_out, g.dts.at[i], g.packsem, 7 + i, p))
-    bc = bc_block(own)
-    for d in bcs:
-        d.wait_recv()
+    skips = head_sum(jnp.broadcast_to(jnp.sum(g.vacc[1], axis=0, keepdims=True), (8, CHANNELS)))
+    g.pack[16:24, 256:384] = skips
+    bc = g.p_rest[bc_rows, :]
     for i in range(3):
         bc = bc + g.rbc[i].astype(F32)
-    g.p_bc[...] = bc
-    t_bc.s0()
+    g.p_rest[bc_rows, :] = bc
+    g.p_rest[cut((1 - core) * 320, 192, 16), :] = jnp.zeros((192, 256), F32)
+    for n in range(6):
+        cols = pl.ds(256 * n, 256)
+        g.p_rest[192 + 16 * n : 208 + 16 * n, :] = mul(g.gsr[...], g.xn[:, cols], TN)[0:16]
+    g.p_rest[288:320, :] = jnp.zeros((32, 256), F32)
+    for n in range(3):
+        g.p_rest[512 + 24 * n : 536 + 24 * n, :] = g.pack[:, 256 * n : 256 * n + 256]
+    g.p_rest[584:640, :] = jnp.zeros((56, 256), F32)
+    t_rest.s0()
+    t_x.s3()
+    t_rest.s1()
+    t_out.s5()
+    t_rest.s2()
+    t_x.s4()
     t_z.s5()
+    t_rest.s3()
     t_out.s6()
     store = [pltpu.make_async_copy(g.p_out, g.grad_out, g.load_sem.at[5])]
     store[0].start()
-    t_x.s2()
-    t_bc.s1()
+    t_rest.s4()
     t_z.s6()
     store.append(pltpu.make_async_copy(g.p_z, g.grad_z, g.load_sem.at[6]))
     store[1].start()
-    for d in packs:
-        d.wait_recv()
-    vec = g.pack[...]
-    dts = g.dt_out[...].astype(F32)
-    for i in range(7):
-        vec = vec + g.packs[i]
-        dts = dts + g.dts[i].astype(F32)
-    g.vec[...] = vec
-    g.grad_dt[...] = dts
-    g.bcv[z] = vec[8:16, 0:256]
-    bcv = [send(g.bcv.at[z], g.bcv.at[z], g.bcvsem, i, p) for i, p in enumerate(zpeers)]
-    t_x.s3()
-    t_bc.s2()
-    t_bc.s3()
-    t_x.s4()
-    t_bc.s4()
-
-    for d in ins:
-        d.wait_recv()
+
+    in_blocks.arrived()
     g.nacc[...] = jnp.zeros(g.nacc.shape, F32)
 
     def finish(i):
@@ -1333,7 +1476,7 @@
     g.ngain[0] = jnp.broadcast_to(jnp.sum(g.nacc[...], axis=0, keepdims=True), (8, BLOCK))
     ngs = [send(g.ngain.at[0], g.ngain.at[1 + i], g.nsem, 3 + i, p) for i, p in enumerate(speers)]
     t_x.s5()
-    t_bc.s5()
+    t_rest.s5()
     for d in nst:
         d.wait_recv()
     rows = (g.nstat[0] + g.nstat[1] + g.nstat[2] + g.nstat[3])[0:1]
@@ -1356,11 +1499,8 @@
     for i in range(7):
         total = total + g.ngain[1 + i]
     g.grad_gain[...] = total
-    for d in bcv:
-        d.wait_recv()
-    g.vec[8:16, 0:256] = g.bcv[0] + g.bcv[1] + g.bcv[2] + g.bcv[3]
-    t_bc.s6()
-    g.grad_bc[...] = g.p_bc[...]
+    t_rest.s6()
+    g.rest[...] = g.p_rest[...]
     t_x.s6()
     store.append(pltpu.make_async_copy(g.p_x, g.grad_x, g.load_sem.at[7]))
     store[2].start()
@@ -1375,30 +1515,65 @@
     def _():
         ret.wait_send()
 
-    for j in range(1, HOPS + 1):
-        d = remote(g.state_out, g.states.at[j - 1], g.st_send.at[j - 1], g.st_recv.at[j - 1], {ALONG: s + j})
-
-        @pl.when(s + j < SEQ)
+    for inside_it, d in later:
+        @pl.when(inside_it)
         def _():
             d.wait_send()
 
-        @pl.when(s - j >= 0)
-        def _():
-            back[j - 1].wait_send()
-
-    for j in range(1, HOPS):
-        up = remote(g.decay.at[0], g.decay.at[j], g.st_send.at[2 + j], g.st_recv.at[2 + j], {ALONG: s + j})
-        down_copy = remote(g.decay.at[0], g.decay.at[2 + j], g.st_send.at[4 + j], g.st_recv.at[4 + j], {ALONG: s - j})
-
-        @pl.when(s + j < SEQ)
-        def _():
-            up.wait_send()
-
-        @pl.when(s - j >= 0)
-        def _():
-            down_copy.wait_send()
-
+    in_blocks.left()
     for d in store:
+        d.wait()
+
+
+def unpack_kernel(
+    layer_hbm, in_hbm, out_low, z_low, x_low, rest, gain_sum,
+    layer_out, grad_in, gain, w_z, w_x, w_bc, w_dt, conv_x_w, conv_x_b, conv_bc_w, conv_bc_b, dt_bias, a_log, d_skip, gate_gain, w_out,
+    low_a, low_b, low_c, full_a, full_b, full_c, keep_a, keep_b, in_sem, out_sem,
+):
+    steps = 6
+    mats = [(out_low, low_a, full_a, w_out), (z_low, low_b, full_b, w_z), (x_low, low_c, full_c, w_x)]
+    loads, stores = [], []
+    for m, (src, low, _, _) in enumerate(mats):
+        n = low.shape[0] // steps
+        for i in range(steps):
+            at = pl.ds(i * n, n)
+            loads.append(pltpu.make_async_copy(src.at[at], low.at[at], in_sem.at[steps * m + i]))
+    for i, (src, dst) in enumerate([(layer_hbm, keep_a), (in_hbm, keep_b)]):
+        loads.append(pltpu.make_async_copy(src, dst, in_sem.at[18 + i]))
+    for d in loads:
+        d.start()
+    for n in range(3):
+        gain[n : n + 1, :] = gain_sum[0:1, 128 * n : 128 * n + 128]
+    w_bc[0:192, :] = rest[0:192, :]
+    w_bc[192:BLOCK, :] = rest[320:512, :]
+    for n in range(6):
+        w_dt[:, 256 * n : 256 * n + 256] = rest[192 + 16 * n : 204 + 16 * n, :]
+    for n in range(3):
+        at, base = pl.ds(256 * n, 256), 512 + 24 * n
+        conv_x_w[:, at] = rest[base : base + 4, :]
+        for e in range(2):
+            lanes, to = pl.ds(128 * e, 128), pl.ds(2 * n + e, 1)
+            conv_x_b[to, :] = rest[base + 4 : base + 5, lanes]
+            gate_gain[to, :] = rest[base + 5 : base + 6, lanes]
+    conv_bc_w[...] = rest[520:524, :]
+    for e in range(2):
+        conv_bc_b[e : e + 1, :] = rest[524:525, 128 * e : 128 * e + 128]
+    dt_bias[...] = rest[528:529, 0:12]
+    a_log[...] = rest[528:529, 128:140]
+    d_skip[...] = rest[552:553, 0:12]
+    for m, (_, low, full, dst) in enumerate(mats):
+        n = low.shape[0] // steps
+        for i in range(steps):
+            loads[steps * m + i].wait()
+            at = pl.ds(i * n, n)
+            full[at, :] = low[at, :].astype(F32)
+            stores.append(pltpu.make_async_copy(full.at[at], dst.at[at], out_sem.at[steps * m + i]))
+            stores[-1].start()
+    for i, (src, dst) in enumerate([(keep_a, layer_out), (keep_b, grad_in)]):
+        loads[18 + i].wait()
+        stores.append(pltpu.make_async_copy(src, dst, out_sem.at[18 + i]))
+        stores[-1].start()
+    for d in stores:
         d.wait()
 
 
@@ -1406,14 +1581,15 @@
     hidden_in, seq_lengths, norm_gain, w_z, w_x, w_bc, w_dt, conv_x_w, conv_x_b, conv_bc_w,
     conv_bc_b, dt_bias, a_log, d_skip, gate_gain, w_out, cotangent,
 ):
-    vectors = (norm_gain, conv_x_b, conv_bc_b, dt_bias, a_log, d_skip, gate_gain)
-    params = jnp.stack([jnp.pad(v, (0, CHANNELS - v.shape[0])) for v in vectors] + [jnp.zeros((CHANNELS,), F32)])
+    row = lambda v: v.reshape(-1, min(128, v.shape[0]))
     vm = pl.BlockSpec(memory_space=pltpu.VMEM)
-    hbm = pl.BlockSpec(memory_space=pl.ANY)
+    hbm = pl.BlockSpec(memory_space=pltpu.HBM)
     sm = pl.BlockSpec(memory_space=pltpu.SMEM)
     ins = dict(
         x_hbm=(hidden_in, hbm), cot_hbm=(cotangent, hbm), w_x=(w_x, hbm), w_z=(w_z, hbm), w_out=(w_out, hbm),
-        lengths=(seq_lengths, sm), params=(params, vm), w_bc=(w_bc, vm), w_dt=(w_dt, vm),
+        lengths=(seq_lengths, sm), norm_gain=(row(norm_gain), vm), conv_x_b=(row(conv_x_b), vm),
+        conv_bc_b=(row(conv_bc_b), vm), dt_bias=(row(dt_bias), vm), a_log=(row(a_log), vm), d_skip=(row(d_skip), vm),
+        gate_gain=(row(gate_gain), vm), w_bc=(w_bc, vm), w_dt=(w_dt.T, vm),
         conv_x_w=(conv_x_w, vm), conv_bc_w=(conv_bc_w, vm),
     )
     outs = dict(
@@ -1422,9 +1598,7 @@
         grad_out=((CHANNELS, D), BF, hbm),
         grad_z=((D, CHANNELS), BF, hbm),
         grad_x=((D, CHANNELS), BF, hbm),
-        grad_bc=((BLOCK, 256), F32, vm),
-        grad_dt=((16, D), F32, vm),
-        vec=((24, CHANNELS), F32, vm),
+        rest=((640, 256), F32, vm),
         grad_gain=((8, BLOCK), F32, vm),
     )
     V = pltpu.VMEM
@@ -1440,7 +1614,8 @@
         ssq=V((LINE, 8, ROWS), F32),
         gains=V((LINE, 8, BLOCK), F32),
         wbc=V((LINE, BLOCK, 256), BF),
-        wd=V((D, 128), BF),
+        wd=V((128, D), BF),
+        params=V((8, CHANNELS), F32),
         taps=V((8, WIDE), F32),
         spread=V((256, CHANNELS), BF),
         segc=V((ROWS + HALO, 128), F32),
@@ -1452,7 +1627,6 @@
         edge=V((HALO, WIDE), BF),
         halo=V((HALO, WIDE), BF),
         cf=V((ROWS + HALO, WIDE), F32),
-        spre=V((ROWS, 128), F32),
         step=V((ROWS, 128), F32),
         cum=V((ROWS, 128), F32),
         cumt=V((2, 16, SPAN), F32),
@@ -1461,7 +1635,7 @@
         lead=V((ROWS, 128), F32),
         carry=V((2, 8, 128), F32),
         carrye=V((2, 8, CHANNELS), F32),
-        decay=V((5, 8, CHANNELS), F32),
+        decay=V((2, 8, CHANNELS), F32),
         slope=V((ROWS + 16, WIDE), F32),
         inner=V((ROWS, CHANNELS), BF),
         b=V((ROWS, 128), BF),
@@ -1472,8 +1646,18 @@
         leadt=V((2, 16, SPAN), F32),
         stept=V((2, 16, SPAN), F32),
         local=V((2, STATE, CHANNELS), F32),
-        state_out=V((STATE, CHANNELS), F32),
-        states=V((HOPS, STATE, CHANNELS), F32),
+        mine=V((STATE, CHANNELS), F32),
+        other=V((STATE, CHANNELS), F32),
+        joined=V((STATE, BLOCK), F32),
+        got=V((2, STATE, BLOCK), F32),
+        chain=V((STATE, CHANNELS), F32),
+        mine_b=V((STATE, CHANNELS), F32),
+        other_b=V((STATE, CHANNELS), F32),
+        joined_b=V((STATE, BLOCK), F32),
+        got_b=V((2, STATE, BLOCK), F32),
+        chain_b=V((STATE, CHANNELS), F32),
+        both=V((8, BLOCK), F32),
+        boths=V((2, 8, BLOCK), F32),
         scores=V((SPAN, SPAN), F32),
         gscores=V((SPAN, SPAN), F32),
         out=V((ROWS, CHANNELS), F32),
@@ -1481,27 +1665,25 @@
         slow=V((2, STATE, CHANNELS), BF),
         gated=V((ROWS, CHANNELS), F32),
         part=V((2, ROWS, 128), F32),
-        stats=V((LINE, 16, ROWS), F32),
+        stats=V((LINE, 8, ROWS), F32),
         vacc=V((2, 8, CHANNELS), F32),
         gm=V((ROWS, CHANNELS), BF),
-        sent_grad=V((STATE, CHANNELS), F32),
-        gstates=V((HOPS, STATE, CHANNELS), F32),
         gloc=V((2, STATE, CHANNELS), F32),
         sblk=V((3, ROWS, BLOCK), BF),
         rblk=V((3, ROWS, BLOCK), BF),
         rblk2=V((3, ROWS, BLOCK), BF),
         gsr=V((ROWS, 128), BF),
         pack=V((24, CHANNELS), F32),
-        packs=V((7, 24, CHANNELS), F32),
         ret_out=V((8, WIDE), F32),
         ret_in=V((8, WIDE), F32),
         wacc=V((5, 8, WIDE), F32),
         gbc=V((2, ROWS, 256), BF),
         tail_rows=V((16, WIDE), F32),
-        sbc=V((3, BLOCK, 256), BF),
-        rbc=V((3, BLOCK, 256), BF),
-        dt_out=V((16, D), BF),
-        dts=V((7, 16, D), BF),
+        sbc=V((LINE, BLOCK, 256), BF),
+        hbc=V((LINE, 192, 256), BF),
+        rbc=V((3, 192, 256), BF),
+        via=V((ROWS, BLOCK), BF),
+        via2=V((ROWS, BLOCK), BF),
         bcv=V((LINE, 8, 256), F32),
         nacc=V((8, BLOCK), F32),
         nstat=V((LINE, 8, ROWS), F32),
@@ -1509,29 +1691,28 @@
         p_out=V((CHANNELS, D), BF),
         p_z=V((D, CHANNELS), BF),
         p_x=V((D, CHANNELS), BF),
-        p_bc=V((BLOCK, 256), F32),
+        p_rest=V((640, 256), F32),
         load_sem=S((8,)),
         edge_sem=S((4,)),
-        st_send=S((7,)),
-        st_recv=S((7,)),
-        gs_send=S((3,)),
-        gs_recv=S((3,)),
+        gather_s=S((8,)),
+        gather_r=S((8,)),
+        block_s=S((8,)),
+        block_r=S((8,)),
+        st_send=S((11,)),
+        st_recv=S((11,)),
         tot_send=S((40,)),
         tot_recv=S((40,)),
         freed=pltpu.SemaphoreType.REGULAR((12,)),
     )
     pairs = dict(
         small=9,
-        gather=6,
         wide=7,
         stat=3,
-        block=6,
-        bcsem=3,
-        packsem=14,
+        bcsem=4,
         bcvsem=3,
         nsem=10,
     )
-    sums = [(CHANNELS, D, BF), (D, CHANNELS, BF), (D, CHANNELS, BF), (BLOCK, 256, F32)]
+    sums = [(CHANNELS, D, BF), (D, CHANNELS, BF), (D, CHANNELS, BF), (640, 256, F32)]
     bufs = [b for spec in sums for b in total_bufs(*spec)]
     sems = [S((k,)) for k in pairs.values() for _ in range(2)]
     names = [*ins, *outs, *scr]
@@ -1553,12 +1734,28 @@
         compiler_params=pltpu.CompilerParams(collective_id=0, has_side_effects=True, vmem_limit_bytes=66 * 2**20 - 2**21),
         name="layer",
     )(*[a for a, _ in ins.values()])
-    layer_out, grad_in, grad_out, grad_z, grad_x, grad_bc, grad_dt, vec, grad_gain = res
-    return (
-        layer_out, grad_in, grad_gain[0], grad_z.astype(F32), grad_x.astype(F32), grad_bc,
-        grad_dt[0:12].T, vec[0:4], vec[4], vec[8:12, 0:256], vec[12, 0:256], vec[16, 0:12], vec[16, 128:140],
-        jnp.sum(vec[6].reshape(12, HEAD_DIM), axis=1), vec[5], grad_out.astype(F32),
-    )
+    layer_out, grad_in, grad_out, grad_z, grad_x, rest, grad_gain = res
+    shapes = dict(
+        layer_out=((ROWS, BLOCK), BF, hbm), grad_in=((ROWS, BLOCK), F32, hbm), gain=((3, 128), F32, vm), w_z=((D, CHANNELS), F32, hbm),
+        w_x=((D, CHANNELS), F32, hbm), w_bc=((BLOCK, 256), F32, vm), w_dt=((12, D), F32, vm), conv_x_w=((4, CHANNELS), F32, vm),
+        conv_x_b=((6, 128), F32, vm), conv_bc_w=((4, 256), F32, vm), conv_bc_b=((2, 128), F32, vm), dt_bias=((1, 12), F32, vm),
+        a_log=((1, 12), F32, vm), d_skip=((1, 12), F32, vm), gate_gain=((6, 128), F32, vm), w_out=((CHANNELS, D), F32, hbm),
+    )
+    final = pl.pallas_call(
+        unpack_kernel,
+        out_shape=[jax.ShapeDtypeStruct(sh, dt) for sh, dt, _ in shapes.values()],
+        in_specs=[hbm] * 5 + [vm] * 2,
+        out_specs=[sp for _, _, sp in shapes.values()],
+        scratch_shapes=[
+            V((CHANNELS, D), BF), V((D, CHANNELS), BF), V((D, CHANNELS), BF),
+            V((CHANNELS, D), F32), V((D, CHANNELS), F32), V((D, CHANNELS), F32),
+            V((ROWS, BLOCK), BF), V((ROWS, BLOCK), F32), S((20,)), S((20,)),
+        ],
+        compiler_params=pltpu.CompilerParams(vmem_limit_bytes=63 * 2**20),
+    )(layer_out, grad_in, grad_out, grad_z, grad_x, rest, grad_gain)
+    flat = [v.reshape(v.size) if v.shape[1] <= 128 else v for v in final]
+    flat[6] = flat[6].T
+    return tuple(flat)
 
 
 def solution(mesh):

time: 255 us -> 184 us (0.72)
  Pallas kernels: 224 us -> 182 us
  local copies, waits for them, and re-layouts: 19 us -> 0 us
  other arithmetic: 10.4 us -> 0 us
    pallas_call x1, Pallas kernels: 224 us -> 172 us  [fast_layer(): pl.pallas_call(kernel, out_shape=[jax.ShapeDtypeStruct(sh, dt) for sh, dt...]
    pallas_call x0 -> x1, Pallas kernels: none -> 9.82 us  [fast_layer(): pl.pallas_call(unpack_kernel, out_shape=[jax.ShapeDtypeStruct(sh, dt) for...]
    convert_element_type x3 -> x0, other arithmetic: 9.73 us -> none  [the longest x1 4.36 us: fast_layer(): grad_z.astype(F32)]
    slice x5 -> x0, local copies, waits for them, and re-layouts: 6.66 us -> none  [the longest x1 1.47 us: fast_layer(): vec[5]]
    unnamed x14 -> x0, local copies, waits for them, and re-layouts: 4.15 us -> none
    pad x5 -> x0, local copies, waits for them, and re-layouts: 3.34 us -> none  [fast_layer(): jnp.pad(v, (0, CHANNELS - v.shape[0]))]
where the time goes in v2:
time: 184 us; the launch traced here: 183 us
  Pallas kernels  182 us (99%)
    pallas_call x1, Pallas kernels, fast_layer(): pl.pallas_call(kernel, out_shape=[jax.ShapeDtypeStruct(sh, dt) for sh, dt...  172 us
    pallas_call x1, Pallas kernels, fast_layer(): pl.pallas_call(unpack_kernel, out_shape=[jax.ShapeDtypeStruct(sh, dt) for...  9.82 us

profile of v2, /device:TPU:0, one launch (start us, length us, event | category | flops | bytes accessed | tf_op | source)
XLA Modules:
  0.0 182.6 jit_solution(16858602033379970884)
XLA Ops:
  0.7 172.0 %layer.1 = (bf16[512,384]{1,0:T(8,128)(2,1)}, f32[512,384]{1,0:T(8,128)}, bf16[768,1536]{1,0:T(8,128)(2,1)}, bf16[1536,768]{1,0:T(8,128)(2,1)}, bf16[1536,768]{1...) custom-call(bf16[512,384]{1,0:T(8,128)(2,1)} %refs_0_.1, bf16[512,384]{1,0:T(8,128)(2,1)} %refs_1_.1, ...), custom_call_target="tpu_custom_call" | custom-call | tf_op jit(solution)/shard_map/layer/pallas_call | solution.py:1728
  172.6 9.8 %shard_map.288 = (bf16[512,384]{1,0:T(8,128)(2,1)}, f32[512,384]{1,0:T(8,128)}, f32[3,128]{1,0:T(4,128)}, f32[1536,768]{1,0:T(8,128)}, f32[1536,768]{1,0:T(8,128...) custom-call(bf16[512,384]{1,0:T(8,128)(2,1)} %get-tuple-element.39.l, ...), custom_call_target="tpu_custom_call" | custom-call | tf_op jit(solution)/shard_map/pallas_call | solution.py:1744

commit v3 on v2

--- a/solution.py
+++ b/solution.py
@@ -619,7 +619,7 @@
     g.gz = g.xg.at[:, pl.ds(CHANNELS, CHANNELS)]
     g.gconv = g.slope
     g.gx = g.gm
-    g.sblk2 = g.sblk
+    g.own_in = g.acc.at[:, pl.ds(0, BLOCK)]
     g.own = g.gated.at[:, pl.ds(0, BLOCK)]
     g.gb = g.gated.at[:, pl.ds(BLOCK, 128)]
     g.gc = g.gated.at[:, pl.ds(BLOCK + 128, 128)]
@@ -660,9 +660,12 @@
     loads[3].wait()
     gain = g.params[0:1, 0:BLOCK]
     xv = g.x[...].astype(F32)
-    g.ssq[z] = jnp.broadcast_to(to_row(lanes_sum(xv * xv)), (8, ROWS))
-    g.gains[z] = jnp.broadcast_to(gain, (8, BLOCK))
-    piece = cut(48 * s, 48, 16)
+    g.ssq[z] = to_row(lanes_sum(xv * xv))
+    g.gains[z] = gain
+    core, chip = me[0], s // 2
+    partner = {ALONG: s + 1 - 2 * core}
+    chips = [{ALONG: lax.rem(s + 2 * d, SEQ)} for d in range(1, 4)]
+    piece = cut(48 * (4 * core + chip), 48, 16)
     own = cut(z * BLOCK, BLOCK, 128)
     g.wbc[z, piece, :] = g.w_bc[piece, :]
     small = []
@@ -699,7 +702,15 @@
         def _():
             block_copy(part, whole, base, 2, near[0], near[1]).start()
 
-    x_third = gather(g.x, g.xg, 0)
+    x_own = [block_copy(g.x, g.xg, 0, j, z, near[j]) for j in range(2)]
+    x_on = [block_copy(g.xg.at[:, cut(near[j] * BLOCK, BLOCK, 128)], g.xg, 0, 2 + j, near[j], near[1 - j % 2]) for j in range(2)]
+    x_on.append(block_copy(g.xg.at[:, cut(near[2] * BLOCK, BLOCK, 128)], g.xg, 0, 4, near[2], near[1]))
+    x_own[0].start()
+
+    @pl.when(middle)
+    def _():
+        x_own[1].start()
+
 
     g.wd[...] = jnp.zeros(g.wd.shape, BF)
     g.wd[0:12, :] = g.w_dt[...]
@@ -746,13 +757,13 @@
     for d in small:
         d.wait_recv()
     wide = [
-        send(g.wbc.at[:, piece], g.wbc.at[:, piece], g.wide, i, p) for i, p in enumerate(speers)
+        send(g.wbc.at[:, piece], g.wbc.at[:, piece], g.wide, i, p) for i, p in enumerate(chips)
     ]
     total = g.ssq[0] + g.ssq[1] + g.ssq[2] + g.ssq[3]
-    g.xscale[...] = to_col(lax.rsqrt(total[0:1] / D + epsilon))
+    g.xscale[...] = to_col(lax.rsqrt(total / D + epsilon))
 
     def normalise(k, src):
-        gk = g.gains[k][0:1]
+        gk = g.gains[k]
         cols = cut(k * BLOCK, BLOCK, 128)
 
         def body(i):
@@ -790,11 +801,31 @@
     project(z, g.wz, CHANNELS, WIDE, True)
     project_dt(z, True)
     for i, k in enumerate(near):
-        gathered(g.x, g.xg, 0, i)
+        if i != 1:
+            gathered(g.x, g.xg, 0, i)
+        else:
+            @pl.when(jnp.logical_not(middle))
+            def _():
+                gathered(g.x, g.xg, 0, 1)
+
+        if i == 2:
+            @pl.when(middle)
+            def _():
+                x_on[2].start()
+
         if i == 0:
-            relay(g.xg, 0)
+            @pl.when(middle)
+            def _():
+                x_on[0].start()
+                gathered(g.x, g.xg, 0, 1)
+                x_on[1].start()
+
+            for d in wide:
+                d.wait_recv()
+            share = g.wbc.at[:, cut(192 * core, 192, 16)]
+            wide = [send(share, share, g.wide, 3, partner)]
         if i == 2:
-            pending.append(gather(g.cotg.at[:, own], g.cotg, 4))
+            pending.append(gather(g.cotg.at[:, own], g.cotg, 5))
         normalise(k, lambda at, cols: g.xg[at, cols])
         project(k, g.wx, CHANNELS, 0, False)
         if i < 2:
@@ -905,9 +936,7 @@
 
     outer(g.bt, g.loadt, g.inner)
     c0, c1 = g.carrye[0][0:1], g.carrye[1][0:1]
-    core, chip = me[0], s // 2
     half, rest = cut(core * BLOCK, BLOCK, 128), cut((1 - core) * BLOCK, BLOCK, 128)
-    partner = {ALONG: s + 1 - 2 * core}
     later = []
 
     class Chain:
@@ -1015,11 +1044,29 @@
             g.boths[i] = jnp.zeros((8, BLOCK), F32)
 
     inside(0, 3, 3)
-    gathered(g.cotg.at[:, own], g.cotg, 4, 0)
-    relay(g.cotg, 4)
+    gathered(g.cotg.at[:, own], g.cotg, 5, 0)
+    relay(g.cotg, 5)
     inside(1, 0, 6)
 
     arrive(both_up, 1)
+    loads[4].wait()
+    gate_gain = g.params[6:7, :]
+
+    def down(k, first):
+        at = cut(k * BLOCK, BLOCK, 128)
+
+        def body(n):
+            cols = cut(n * 256, 256, 256)
+            p = mul(g.cotg[:, at], g.wo[cols, at], NT)
+            if first:
+                g.ggn[:, cols] = p
+            else:
+                g.ggn[:, cols] += p
+
+        loop(3, body)
+
+    down(z, True)
+    down(near[0], False)
     ahead.meet(g.boths[0, 0:1, :])
 
     def act(i):
@@ -1057,36 +1104,18 @@
         g.part[0, at, :] = lanes_sum(gated * gated)
 
     loop(ROWS // 64, gate)
-
-    loads[4].wait()
-    gate_gain = g.params[6:7, :]
-
-    def down(k, first):
-        at = cut(k * BLOCK, BLOCK, 128)
-
-        def body(n):
-            cols = cut(n * 256, 256, 256)
-            p = mul(g.cotg[:, at], g.wo[cols, at], NT)
-            if first:
-                g.ggn[:, cols] = p
-            else:
-                g.ggn[:, cols] += p
-
-        loop(3, body)
-
-    down(z, True)
-    for i, k in enumerate(near):
-        if i > 0:
-            gathered(g.cotg.at[:, own], g.cotg, 4, i)
-        down(k, False)
+    g.stats[z, 0:1, :] = to_row(g.part[0])
+
+    for i in (1, 2):
+        gathered(g.cotg.at[:, own], g.cotg, 5, i)
+        down(near[i], False)
 
     def inner_part(i):
         at = cut(i * 64, 64, 16)
         g.part[1, at, :] = lanes_sum(g.ggn[at, :] * gate_gain * g.gated[at, :])
 
     loop(ROWS // 64, inner_part)
-    which = lax.broadcasted_iota(jnp.int32, (8, ROWS), 0)
-    g.stats[z] = jnp.where(which == 0, to_row(g.part[0]), to_row(g.part[1]))
+    g.stats[z, 1:2, :] = to_row(g.part[1])
     stat = [send(g.stats.at[z], g.stats.at[z], g.stat, i, p) for i, p in enumerate(zpeers)]
     for d in stat:
         d.wait_recv()
@@ -1094,7 +1123,11 @@
     gscale = lax.rsqrt(sums[0:1] / INNER + epsilon)
     g.part[0] = to_col(gscale)
     g.part[1] = to_col(gscale * gscale * gscale * sums[1:2] / INNER)
-    x_third.wait_send()
+    @pl.when(middle)
+    def _():
+        for d in x_on:
+            d.wait_send()
+
     g.vacc[...] = jnp.zeros(g.vacc.shape, F32)
     g.pack[...] = jnp.zeros(g.pack.shape, F32)
     g.bcv[z] = jnp.zeros((8, 256), F32)
@@ -1122,9 +1155,9 @@
     behind = Chain(g.mine_b, g.other_b, g.joined_b, g.got_b, g.chain_b, 4, -1)
     behind.share()
 
-    t_out, t_z, t_x, t_rest = [
+    t_out, t_z, t_xa, t_xb = [
         Total(ref, sum_bufs[5 * i : 5 * i + 5], g.tot_send, g.tot_recv, g.freed, 10 * i, me)
-        for i, ref in enumerate((g.p_out, g.p_z, g.p_x, g.p_rest))
+        for i, ref in enumerate((g.p_out, g.p_z, g.p_xa, g.p_xb))
     ]
 
     def grad_out(n):
@@ -1150,7 +1183,7 @@
             self.sent, self.got, self.via, self.base = sent, got, via, base
 
         def copy(self, j, dst, i, to):
-            return remote(self.sent.at[j], dst, g.block_s.at[self.base + j], g.block_r.at[self.base + i], {ACROSS: to})
+            return remote(self.sent[j], dst, g.block_s.at[self.base + j], g.block_r.at[self.base + i], {ACROSS: to})
 
         def direct(self, j):
             slot = lax.rem(z - dests[j] + 7, 4)
@@ -1164,7 +1197,7 @@
                     self.copy(0, self.via, 3, z).wait_recv()
 
                 v = v + self.via[...].astype(F32)
-            self.sent[j] = v.astype(BF)
+            self.sent[j][...] = v.astype(BF)
             if j == 0:
                 @pl.when(middle)
                 def _():
@@ -1188,8 +1221,11 @@
             for j in range(3):
                 self.copy(j, self.via, 3, z).wait_send()
 
-    out_blocks = Scatter(g.sblk, g.rblk, g.via, 0)
-    in_blocks = Scatter(g.sblk2, g.rblk2, g.via2, 4)
+    blocks = [pl.ds(0, BLOCK), pl.ds(BLOCK, BLOCK)]
+    out_blocks = Scatter([g.sblk.at[j] for j in range(3)], g.rblk, g.via, 0)
+    in_blocks = Scatter(
+        [g.gn.at[:, blocks[0]], g.gn.at[:, blocks[1]], g.inner.at[:, blocks[0]]], g.rblk2, g.via2, 4
+    )
 
     @pl.when(middle)
     def _():
@@ -1245,9 +1281,7 @@
     inside_back(1, 0, 6)
     arrive(both_down, -1)
     behind.meet(g.boths[1, 0:1, :])
-    out_blocks.block(2, out_block(dests[2]))
     inside_back(0, 0, 3)
-    t_out.s2()
     inside_back(0, 3, 3)
 
     behind.end()
@@ -1286,7 +1320,8 @@
         g.gb[rows, :] += sum(mul(p, glow, NT) for p in parts(vals * loade, 2))
         g.gc[rows, :] += sum(mul(p, g.slow[q], NT) for p in parts(gm * spread(g.lead[rows, :]), 2))
         if q == 0:
-            t_z.s2()
+            t_out.s2()
+            out_blocks.block(2, out_block(dests[2]))
     g.pack[16:24, 0:128] = jnp.broadcast_to(
         jnp.sum(ends[0][0] + ends[1][0], axis=0, keepdims=True), (8, 128)
     )
@@ -1330,7 +1365,7 @@
         g.ret_in[...] = jnp.zeros((8, WIDE), F32)
 
     g.wacc[...] = jnp.zeros(g.wacc.shape, F32)
-    t_out.s3()
+    t_z.s2()
 
     def convolve_back(i):
         first = i * 64
@@ -1364,7 +1399,7 @@
             g.wacc[4, :, cols] += rows_sum(here)
 
     loop(ROWS // 64, convolve_back)
-    t_z.s3()
+    t_out.s3()
 
     @pl.when(s < SEQ - 1)
     def _():
@@ -1389,15 +1424,19 @@
     mine, other = cut(core * 192, 192, 16), cut((1 - core) * 192, 192, 16)
     halves = send(g.sbc.at[:, other], g.hbc, g.bcsem, 3, partner)
 
-    def grad_x(n):
-        at = cut(n * 256, 256, 256)
-        g.p_x[at, :] = mul(g.xn[:, at], g.gx[...], TN).astype(BF)
-
-    loop(6, grad_x)
-    t_x.s0()
+    def grad_x(ref, first):
+        def body(n):
+            at = cut(n * 256, 256, 256)
+            ref[at, :] = mul(g.xn[:, cut(first + n * 256, 256, 256)], g.gx[...], TN).astype(BF)
+
+        loop(3, body)
+
+    grad_x(g.p_xa, 0)
+    t_xa.s0()
+    grad_x(g.p_xb, CHANNELS)
+    t_xb.s0()
     halves.wait_recv()
-    bc_rows = cut(core * 320, 192, 16)
-    g.p_rest[bc_rows, :] = g.sbc[z, mine, :].astype(F32) + g.hbc[z].astype(F32)
+    g.bcsum[...] = g.sbc[z, mine, :].astype(F32) + g.hbc[z].astype(F32)
     for i, p in enumerate(zpeers):
         k = lax.rem(z + 1 + i, LINE)
         g.sbc[k, mine, :] = (g.sbc[k, mine, :].astype(F32) + g.hbc[k].astype(F32)).astype(BF)
@@ -1408,20 +1447,14 @@
         v = mul(g.gx[...], g.wx[at, :], NT) + mul(g.gz[...], g.wz[at, :], NT)
         return v + mul(g.gsr[...], g.wd[:, cut(k * BLOCK, BLOCK, 128)]) + mul(g.gbc[0], g.wbc[k], NT) + mul(g.gbc[1], g.wbc[k], NT)
 
-    out_blocks.arrived()
-    out_blocks.left()
-    out_sum = g.own[...]
-    for i in range(3):
-        out_sum = out_sum + g.rblk[i].astype(F32)
-    g.layer_out[...] = (g.x[...].astype(F32) + out_sum).astype(BF)
     in_blocks.block(0, back_block(dests[0]))
-    t_x.s1()
-    t_out.s4()
+    t_xa.s1()
+    t_xb.s1()
     in_blocks.block(1, back_block(dests[1]))
-    g.own[...] = back_block(z)
-    in_blocks.block(2, back_block(dests[2]))
-    t_x.s2()
-    t_z.s4()
+    g.own_in[...] = back_block(z)
+    t_z.s3()
+    t_xa.s2()
+    t_xb.s2()
 
     for d in bcs + bcv:
         d.wait_recv()
@@ -1429,57 +1462,71 @@
     g.pack[5:6, :] = jnp.sum(g.vacc[0], axis=0, keepdims=True)
     skips = head_sum(jnp.broadcast_to(jnp.sum(g.vacc[1], axis=0, keepdims=True), (8, CHANNELS)))
     g.pack[16:24, 256:384] = skips
-    bc = g.p_rest[bc_rows, :]
+    bc = g.bcsum[...]
     for i in range(3):
         bc = bc + g.rbc[i].astype(F32)
-    g.p_rest[bc_rows, :] = bc
-    g.p_rest[cut((1 - core) * 320, 192, 16), :] = jnp.zeros((192, 256), F32)
+    g.q_out[0:192, :] = bc.astype(BF)
     for n in range(6):
         cols = pl.ds(256 * n, 256)
-        g.p_rest[192 + 16 * n : 208 + 16 * n, :] = mul(g.gsr[...], g.xn[:, cols], TN)[0:16]
-    g.p_rest[288:320, :] = jnp.zeros((32, 256), F32)
+        g.few[16 * n : 16 * n + 16, :] = mul(g.gsr[...], g.xn[:, cols], TN)[0:16]
     for n in range(3):
-        g.p_rest[512 + 24 * n : 536 + 24 * n, :] = g.pack[:, 256 * n : 256 * n + 256]
-    g.p_rest[584:640, :] = jnp.zeros((56, 256), F32)
-    t_rest.s0()
-    t_x.s3()
-    t_rest.s1()
+        g.few[96 + 24 * n : 120 + 24 * n, :] = g.pack[:, 256 * n : 256 * n + 256]
+    g.few[168:192, :] = jnp.zeros((24, 256), F32)
+    few = send(g.few, g.few_in, g.restsem, 0, partner)
+    in_blocks.block(2, back_block(dests[2]))
+    t_out.s4()
+    t_xa.s3()
+    few.wait_recv()
+    few_half = cut(96 * core, 96, 8)
+    g.q_out[192:288, :] = (g.few[few_half, :] + g.few_in[few_half, :]).astype(BF)
+    across_x = send(g.q_out, g.q_in.at[0], g.restsem, 1, {ALONG: s + 2 - 4 * me[1]})
+    t_xb.s3()
+    t_z.s4()
+    out_blocks.arrived()
+    out_sum = g.own[...]
+    for i in range(3):
+        out_sum = out_sum + g.rblk[i].astype(F32)
+    g.layer_out[...] = (g.x[...].astype(F32) + out_sum).astype(BF)
+
+    in_blocks.arrived()
+    g.nacc[...] = jnp.zeros(g.nacc.shape, F32)
+
+    def finish(i):
+        at = cut(i * 64, 64, 16)
+        v = g.own_in[at, :]
+        for k in range(3):
+            v = v + g.rblk2[k, at, :].astype(F32)
+        g.own_in[at, :] = v
+        x = g.x[at, :].astype(F32)
+        g.part[0, at, :] = lanes_sum(v * gain * x)
+        g.nacc[...] += rows_sum(v * x * wide_of(g.xscale[at, :], 3))
+
+    loop(ROWS // 64, finish)
+    g.nstat[z] = to_row(g.part[0])
+    nst = [send(g.nstat.at[z], g.nstat.at[z], g.nsem, i, p) for i, p in enumerate(zpeers)]
+    g.ngain[0] = jnp.sum(g.nacc[...], axis=0, keepdims=True)
+    ngs = [send(g.ngain.at[0], g.ngain.at[1 + i], g.nsem, 3 + i, p) for i, p in enumerate(speers)]
+    t_xa.s4()
+    across_x.wait_recv()
+    g.q_mid[...] = (g.q_out[...].astype(F32) + g.q_in[0].astype(F32)).astype(BF)
+    across_y = send(g.q_mid, g.q_in.at[1], g.restsem, 2, {ALONG: s + 4 - 8 * me[2]})
+    t_xb.s4()
     t_out.s5()
-    t_rest.s2()
-    t_x.s4()
+    t_xa.s5()
     t_z.s5()
-    t_rest.s3()
+    t_xb.s5()
+    across_y.wait_recv()
+    g.rest[core] = g.q_mid[...].astype(F32) + g.q_in[1].astype(F32)
+    q_last = send(g.rest.at[core], g.rest.at[core], g.restsem, 3, partner)
     t_out.s6()
     store = [pltpu.make_async_copy(g.p_out, g.grad_out, g.load_sem.at[5])]
     store[0].start()
-    t_rest.s4()
     t_z.s6()
     store.append(pltpu.make_async_copy(g.p_z, g.grad_z, g.load_sem.at[6]))
     store[1].start()
-
-    in_blocks.arrived()
-    g.nacc[...] = jnp.zeros(g.nacc.shape, F32)
-
-    def finish(i):
-        at = cut(i * 64, 64, 16)
-        v = g.own[at, :]
-        for k in range(3):
-            v = v + g.rblk2[k, at, :].astype(F32)
-        g.own[at, :] = v
-        x = g.x[at, :].astype(F32)
-        g.part[0, at, :] = lanes_sum(v * gain * x)
-        g.nacc[...] += rows_sum(v * x * wide_of(g.xscale[at, :], 3))
-
-    loop(ROWS // 64, finish)
-    g.nstat[z] = jnp.broadcast_to(to_row(g.part[0]), (8, ROWS))
-    nst = [send(g.nstat.at[z], g.nstat.at[z], g.nsem, i, p) for i, p in enumerate(zpeers)]
-    g.ngain[0] = jnp.broadcast_to(jnp.sum(g.nacc[...], axis=0, keepdims=True), (8, BLOCK))
-    ngs = [send(g.ngain.at[0], g.ngain.at[1 + i], g.nsem, 3 + i, p) for i, p in enumerate(speers)]
-    t_x.s5()
-    t_rest.s5()
     for d in nst:
         d.wait_recv()
-    rows = (g.nstat[0] + g.nstat[1] + g.nstat[2] + g.nstat[3])[0:1]
+    rows = g.nstat[0] + g.nstat[1] + g.nstat[2] + g.nstat[3]
     g.part[0] = to_col(rows / D)
 
     def last(i):
@@ -1488,7 +1535,7 @@
         x = g.x[at, :].astype(F32)
         g.grad_in[at, :] = (
             g.cotg[at, own].astype(F32)
-            + sc * (g.own[at, :] * gain)
+            + sc * (g.own_in[at, :] * gain)
             - x * (sc * sc * sc * wide_of(g.part[0, at, :], 3))
         )
 
@@ -1498,12 +1545,13 @@
     total = g.ngain[0]
     for i in range(7):
         total = total + g.ngain[1 + i]
-    g.grad_gain[...] = total
-    t_rest.s6()
-    g.rest[...] = g.p_rest[...]
-    t_x.s6()
-    store.append(pltpu.make_async_copy(g.p_x, g.grad_x, g.load_sem.at[7]))
-    store[2].start()
+    g.grad_gain[...] = jnp.broadcast_to(total, (8, BLOCK))
+    q_last.wait_recv()
+    for i, (t, ref) in enumerate(((t_xa, g.p_xa), (t_xb, g.p_xb))):
+        t.s6()
+        rows_of = pl.ds(CHANNELS * i, CHANNELS)
+        store.append(pltpu.make_async_copy(ref, g.grad_x.at[rows_of], g.load_sem.at[7 + i]))
+        store[-1].start()
     for d in pending:
         d.wait_send()
 
@@ -1514,12 +1562,19 @@
     @pl.when(s > 0)
     def _():
         ret.wait_send()
+
+    x_own[0].wait_send()
+
+    @pl.when(middle)
+    def _():
+        x_own[1].wait_send()
 
     for inside_it, d in later:
         @pl.when(inside_it)
         def _():
             d.wait_send()
 
+    out_blocks.left()
     in_blocks.left()
     for d in store:
         d.wait()
@@ -1544,23 +1599,23 @@
         d.start()
     for n in range(3):
         gain[n : n + 1, :] = gain_sum[0:1, 128 * n : 128 * n + 128]
-    w_bc[0:192, :] = rest[0:192, :]
-    w_bc[192:BLOCK, :] = rest[320:512, :]
+    w_bc[0:192, :] = rest[0, 0:192, :]
+    w_bc[192:BLOCK, :] = rest[1, 0:192, :]
     for n in range(6):
-        w_dt[:, 256 * n : 256 * n + 256] = rest[192 + 16 * n : 204 + 16 * n, :]
+        w_dt[:, 256 * n : 256 * n + 256] = rest[0, 192 + 16 * n : 204 + 16 * n, :]
     for n in range(3):
-        at, base = pl.ds(256 * n, 256), 512 + 24 * n
-        conv_x_w[:, at] = rest[base : base + 4, :]
+        at, base = pl.ds(256 * n, 256), 192 + 24 * n
+        conv_x_w[:, at] = rest[1, base : base + 4, :]
         for e in range(2):
             lanes, to = pl.ds(128 * e, 128), pl.ds(2 * n + e, 1)
-            conv_x_b[to, :] = rest[base + 4 : base + 5, lanes]
-            gate_gain[to, :] = rest[base + 5 : base + 6, lanes]
-    conv_bc_w[...] = rest[520:524, :]
+            conv_x_b[to, :] = rest[1, base + 4 : base + 5, lanes]
+            gate_gain[to, :] = rest[1, base + 5 : base + 6, lanes]
+    conv_bc_w[...] = rest[1, 200:204, :]
     for e in range(2):
-        conv_bc_b[e : e + 1, :] = rest[524:525, 128 * e : 128 * e + 128]
-    dt_bias[...] = rest[528:529, 0:12]
-    a_log[...] = rest[528:529, 128:140]
-    d_skip[...] = rest[552:553, 0:12]
+        conv_bc_b[e : e + 1, :] = rest[1, 204:205, 128 * e : 128 * e + 128]
+    dt_bias[...] = rest[1, 208:209, 0:12]
+    a_log[...] = rest[1, 208:209, 128:140]
+    d_skip[...] = rest[1, 232:233, 0:12]
     for m, (_, low, full, dst) in enumerate(mats):
         n = low.shape[0] // steps
         for i in range(steps):
@@ -1598,7 +1653,7 @@
         grad_out=((CHANNELS, D), BF, hbm),
         grad_z=((D, CHANNELS), BF, hbm),
         grad_x=((D, CHANNELS), BF, hbm),
-        rest=((640, 256), F32, vm),
+        rest=((2, 288, 256), F32, vm),
         grad_gain=((8, BLOCK), F32, vm),
     )
     V = pltpu.VMEM
@@ -1611,8 +1666,8 @@
         xg=V((ROWS, D), BF),
         xn=V((ROWS, D), BF),
         cotg=V((ROWS, D), BF),
-        ssq=V((LINE, 8, ROWS), F32),
-        gains=V((LINE, 8, BLOCK), F32),
+        ssq=V((LINE, 1, ROWS), F32),
+        gains=V((LINE, 1, BLOCK), F32),
         wbc=V((LINE, BLOCK, 256), BF),
         wd=V((128, D), BF),
         params=V((8, CHANNELS), F32),
@@ -1665,7 +1720,7 @@
         slow=V((2, STATE, CHANNELS), BF),
         gated=V((ROWS, CHANNELS), F32),
         part=V((2, ROWS, 128), F32),
-        stats=V((LINE, 8, ROWS), F32),
+        stats=V((LINE, 2, ROWS), F32),
         vacc=V((2, 8, CHANNELS), F32),
         gm=V((ROWS, CHANNELS), BF),
         gloc=V((2, STATE, CHANNELS), F32),
@@ -1686,16 +1741,22 @@
         via2=V((ROWS, BLOCK), BF),
         bcv=V((LINE, 8, 256), F32),
         nacc=V((8, BLOCK), F32),
-        nstat=V((LINE, 8, ROWS), F32),
-        ngain=V((8, 8, BLOCK), F32),
+        nstat=V((LINE, 1, ROWS), F32),
+        ngain=V((8, 1, BLOCK), F32),
         p_out=V((CHANNELS, D), BF),
         p_z=V((D, CHANNELS), BF),
-        p_x=V((D, CHANNELS), BF),
-        p_rest=V((640, 256), F32),
-        load_sem=S((8,)),
+        p_xa=V((CHANNELS, CHANNELS), BF),
+        p_xb=V((CHANNELS, CHANNELS), BF),
+        bcsum=V((192, 256), F32),
+        few=V((192, 256), F32),
+        few_in=V((192, 256), F32),
+        q_out=V((288, 256), BF),
+        q_mid=V((288, 256), BF),
+        q_in=V((2, 288, 256), BF),
+        load_sem=S((9,)),
         edge_sem=S((4,)),
         gather_s=S((8,)),
-        gather_r=S((8,)),
+        gather_r=S((9,)),
         block_s=S((8,)),
         block_r=S((8,)),
         st_send=S((11,)),
@@ -1706,13 +1767,14 @@
     )
     pairs = dict(
         small=9,
-        wide=7,
+        wide=4,
         stat=3,
         bcsem=4,
+        restsem=4,
         bcvsem=3,
         nsem=10,
     )
-    sums = [(CHANNELS, D, BF), (D, CHANNELS, BF), (D, CHANNELS, BF), (640, 256, F32)]
+    sums = [(CHANNELS, D, BF), (D, CHANNELS, BF), (CHANNELS, CHANNELS, BF), (CHANNELS, CHANNELS, BF)]
     bufs = [b for spec in sums for b in total_bufs(*spec)]
     sems = [S((k,)) for k in pairs.values() for _ in range(2)]
     names = [*ins, *outs, *scr]

time: 184 us -> 173 us (0.940)
  Pallas kernels: 182 us -> 170 us
    pallas_call x1, Pallas kernels: 172 us -> 160 us  [fast_layer(): pl.pallas_call(kernel, out_shape=[jax.ShapeDtypeStruct(sh, dt) for sh, dt...]
where the time goes in v3:
time: 173 us; the launch traced here: 171 us
  Pallas kernels  170 us (98%)
    pallas_call x1, Pallas kernels, fast_layer(): pl.pallas_call(kernel, out_shape=[jax.ShapeDtypeStruct(sh, dt) for sh, dt...  160 us
    pallas_call x1, Pallas kernels, fast_layer(): pl.pallas_call(unpack_kernel, out_shape=[jax.ShapeDtypeStruct(sh, dt) for...  9.8 us

profile of v3, /device:TPU:0, one launch (start us, length us, event | category | flops | bytes accessed | tf_op | source)
XLA Modules:
  0.0 171.1 jit_solution(7267091529188593404)
XLA Ops:
  0.7 160.4 %layer.1 = (bf16[512,384]{1,0:T(8,128)(2,1)}, f32[512,384]{1,0:T(8,128)}, bf16[768,1536]{1,0:T(8,128)(2,1)}, bf16[1536,768]{1,0:T(8,128)(2,1)}, bf16[1536,768]{1...) custom-call(bf16[512,384]{1,0:T(8,128)(2,1)} %refs_0_.1, bf16[512,384]{1,0:T(8,128)(2,1)} %refs_1_.1, ...), custom_call_target="tpu_custom_call" | custom-call | tf_op jit(solution)/shard_map/layer/pallas_call | solution.py:1790
  161.1 9.8 %shard_map.288 = (bf16[512,384]{1,0:T(8,128)(2,1)}, f32[512,384]{1,0:T(8,128)}, f32[3,128]{1,0:T(4,128)}, f32[1536,768]{1,0:T(8,128)}, f32[1536,768]{1,0:T(8,128...) custom-call(bf16[512,384]{1,0:T(8,128)(2,1)} %get-tuple-element.39.l, ...), custom_call_target="tpu_custom_call" | custom-call | tf_op jit(solution)/shard_map/pallas_call | solution.py:1806

commit v4 on v3

--- a/solution.py
+++ b/solution.py
@@ -1117,6 +1117,70 @@
     loop(ROWS // 64, inner_part)
     g.stats[z, 1:2, :] = to_row(g.part[1])
     stat = [send(g.stats.at[z], g.stats.at[z], g.stat, i, p) for i, p in enumerate(zpeers)]
+    dests = [along_line(z, a, b) for a, b in ((2, 3), (3, 0), (1, 2))]
+
+    class Scatter:
+        def __init__(self, sent, got, via, base):
+            self.sent, self.got, self.via, self.base = sent, got, via, base
+
+        def copy(self, j, dst, i, to):
+            return remote(self.sent[j], dst, g.block_s.at[self.base + j], g.block_r.at[self.base + i], {ACROSS: to})
+
+        def direct(self, j):
+            slot = lax.rem(z - dests[j] + 7, 4)
+            return self.copy(j, self.got.at[slot], slot, dests[j])
+
+        def block(self, j, value):
+            v = value
+            if j == 2:
+                @pl.when(middle)
+                def _():
+                    self.copy(0, self.via, 3, z).wait_recv()
+
+                v = v + self.via[...].astype(F32)
+            self.sent[j][...] = v.astype(BF)
+            if j == 0:
+                @pl.when(middle)
+                def _():
+                    self.direct(0).start()
+
+                @pl.when(jnp.logical_not(middle))
+                def _():
+                    self.copy(0, self.via, 3, dests[2]).start()
+            else:
+                self.direct(j).start()
+
+        def arrived(self):
+            for i in (0, 2):
+                self.copy(0, self.got.at[i], i, z).wait_recv()
+
+            @pl.when(jnp.logical_not(middle))
+            def _():
+                self.copy(0, self.got.at[1], 1, z).wait_recv()
+
+        def left(self):
+            for j in range(3):
+                self.copy(j, self.via, 3, z).wait_send()
+
+    blocks = [pl.ds(0, BLOCK), pl.ds(BLOCK, BLOCK)]
+    out_blocks = Scatter([g.sblk.at[j] for j in range(3)], g.rblk, g.via, 0)
+    in_blocks = Scatter(
+        [g.gn.at[:, blocks[0]], g.gn.at[:, blocks[1]], g.inner.at[:, blocks[0]]], g.rblk2, g.via2, 4
+    )
+
+    @pl.when(middle)
+    def _():
+        g.rblk[1] = jnp.zeros((ROWS, BLOCK), BF)
+        g.rblk2[1] = jnp.zeros((ROWS, BLOCK), BF)
+
+    @pl.when(jnp.logical_not(middle))
+    def _():
+        g.via[...] = jnp.zeros((ROWS, BLOCK), BF)
+        g.via2[...] = jnp.zeros((ROWS, BLOCK), BF)
+
+    def out_block(k):
+        return mul(g.gn[...], g.wo[:, cut(k * BLOCK, BLOCK, 128)])
+
     for d in stat:
         d.wait_recv()
     sums = g.stats[0] + g.stats[1] + g.stats[2] + g.stats[3]
@@ -1149,6 +1213,8 @@
         g.vacc[1] += rows_sum(gm.astype(F32) * vals)
 
     loop(ROWS // 64, ungate)
+    out_blocks.block(0, out_block(dests[0]))
+    out_blocks.block(1, out_block(dests[1]))
 
     outer(g.ct, g.leadt, g.gm)
     g.mine_b[...] = g.local[0] + c0 * g.local[1]
@@ -1176,72 +1242,6 @@
     t_z.s0()
     t_out.s1()
 
-    dests = [along_line(z, a, b) for a, b in ((2, 3), (3, 0), (1, 2))]
-
-    class Scatter:
-        def __init__(self, sent, got, via, base):
-            self.sent, self.got, self.via, self.base = sent, got, via, base
-
-        def copy(self, j, dst, i, to):
-            return remote(self.sent[j], dst, g.block_s.at[self.base + j], g.block_r.at[self.base + i], {ACROSS: to})
-
-        def direct(self, j):
-            slot = lax.rem(z - dests[j] + 7, 4)
-            return self.copy(j, self.got.at[slot], slot, dests[j])
-
-        def block(self, j, value):
-            v = value
-            if j == 2:
-                @pl.when(middle)
-                def _():
-                    self.copy(0, self.via, 3, z).wait_recv()
-
-                v = v + self.via[...].astype(F32)
-            self.sent[j][...] = v.astype(BF)
-            if j == 0:
-                @pl.when(middle)
-                def _():
-                    self.direct(0).start()
-
-                @pl.when(jnp.logical_not(middle))
-                def _():
-                    self.copy(0, self.via, 3, dests[2]).start()
-            else:
-                self.direct(j).start()
-
-        def arrived(self):
-            for i in (0, 2):
-                self.copy(0, self.got.at[i], i, z).wait_recv()
-
-            @pl.when(jnp.logical_not(middle))
-            def _():
-                self.copy(0, self.got.at[1], 1, z).wait_recv()
-
-        def left(self):
-            for j in range(3):
-                self.copy(j, self.via, 3, z).wait_send()
-
-    blocks = [pl.ds(0, BLOCK), pl.ds(BLOCK, BLOCK)]
-    out_blocks = Scatter([g.sblk.at[j] for j in range(3)], g.rblk, g.via, 0)
-    in_blocks = Scatter(
-        [g.gn.at[:, blocks[0]], g.gn.at[:, blocks[1]], g.inner.at[:, blocks[0]]], g.rblk2, g.via2, 4
-    )
-
-    @pl.when(middle)
-    def _():
-        g.rblk[1] = jnp.zeros((ROWS, BLOCK), BF)
-        g.rblk2[1] = jnp.zeros((ROWS, BLOCK), BF)
-
-    @pl.when(jnp.logical_not(middle))
-    def _():
-        g.via[...] = jnp.zeros((ROWS, BLOCK), BF)
-        g.via2[...] = jnp.zeros((ROWS, BLOCK), BF)
-
-    def out_block(k):
-        return mul(g.gn[...], g.wo[:, cut(k * BLOCK, BLOCK, 128)])
-
-    out_blocks.block(0, out_block(dests[0]))
-    out_blocks.block(1, out_block(dests[1]))
     t_z.s1()
     g.own[...] = mul(g.gn[...], g.wo[:, own])
 
@@ -1419,10 +1419,13 @@
         g.bcv[z, k : k + 1, :] = row[:, CHANNELS:WIDE]
     bcv = [send(g.bcv.at[z], g.bcv.at[z], g.bcvsem, i, p) for i, p in enumerate(zpeers)]
     bcs = []
-    for k in range(LINE):
-        g.sbc[k] = bc_block(pl.ds(BLOCK * k, BLOCK)).astype(BF)
+    bc_parts = [g.acc.at[pl.ds(0, BLOCK), pl.ds(WIDE + 256 * i, 256)] for i in range(3)]
+    bc_parts.append(g.acc.at[pl.ds(0, BLOCK), pl.ds(BLOCK, 256)])
     mine, other = cut(core * 192, 192, 16), cut((1 - core) * 192, 192, 16)
-    halves = send(g.sbc.at[:, other], g.hbc, g.bcsem, 3, partner)
+    halves = []
+    for i in range(LINE):
+        bc_parts[i][...] = bc_block(cut(lax.rem(z + 1 + i, LINE) * BLOCK, BLOCK, 128))
+        halves.append(send(bc_parts[i].at[other], g.hbc.at[i], g.bcsem, 3 + i, partner))
 
     def grad_x(ref, first):
         def body(n):
@@ -1431,16 +1434,17 @@
 
         loop(3, body)
 
+    t_z.s3()
     grad_x(g.p_xa, 0)
     t_xa.s0()
     grad_x(g.p_xb, CHANNELS)
     t_xb.s0()
-    halves.wait_recv()
-    g.bcsum[...] = g.sbc[z, mine, :].astype(F32) + g.hbc[z].astype(F32)
+    for d in halves:
+        d.wait_recv()
+    g.bcsum[...] = bc_parts[3][mine, :] + g.hbc[3]
     for i, p in enumerate(zpeers):
-        k = lax.rem(z + 1 + i, LINE)
-        g.sbc[k, mine, :] = (g.sbc[k, mine, :].astype(F32) + g.hbc[k].astype(F32)).astype(BF)
-        bcs.append(send(g.sbc.at[k, mine], g.rbc.at[i], g.bcsem, i, p))
+        g.tbc[i] = (bc_parts[i][mine, :] + g.hbc[i]).astype(BF)
+        bcs.append(send(g.tbc.at[i], g.rbc.at[i], g.bcsem, i, p))
 
     def back_block(k):
         at = cut(k * BLOCK, BLOCK, 16)
@@ -1450,10 +1454,11 @@
     in_blocks.block(0, back_block(dests[0]))
     t_xa.s1()
     t_xb.s1()
+    t_out.s4()
     in_blocks.block(1, back_block(dests[1]))
     g.own_in[...] = back_block(z)
-    t_z.s3()
     t_xa.s2()
+    t_z.s4()
     t_xb.s2()
 
     for d in bcs + bcv:
@@ -1474,14 +1479,18 @@
     g.few[168:192, :] = jnp.zeros((24, 256), F32)
     few = send(g.few, g.few_in, g.restsem, 0, partner)
     in_blocks.block(2, back_block(dests[2]))
-    t_out.s4()
     t_xa.s3()
     few.wait_recv()
     few_half = cut(96 * core, 96, 8)
     g.q_out[192:288, :] = (g.few[few_half, :] + g.few_in[few_half, :]).astype(BF)
     across_x = send(g.q_out, g.q_in.at[0], g.restsem, 1, {ALONG: s + 2 - 4 * me[1]})
     t_xb.s3()
-    t_z.s4()
+    t_xa.s4()
+    across_x.wait_recv()
+    g.q_mid[...] = (g.q_out[...].astype(F32) + g.q_in[0].astype(F32)).astype(BF)
+    across_y = send(g.q_mid, g.q_in.at[1], g.restsem, 2, {ALONG: s + 4 - 8 * me[2]})
+    t_xb.s4()
+    t_out.s5()
     out_blocks.arrived()
     out_sum = g.own[...]
     for i in range(3):
@@ -1506,14 +1515,8 @@
     nst = [send(g.nstat.at[z], g.nstat.at[z], g.nsem, i, p) for i, p in enumerate(zpeers)]
     g.ngain[0] = jnp.sum(g.nacc[...], axis=0, keepdims=True)
     ngs = [send(g.ngain.at[0], g.ngain.at[1 + i], g.nsem, 3 + i, p) for i, p in enumerate(speers)]
-    t_xa.s4()
-    across_x.wait_recv()
-    g.q_mid[...] = (g.q_out[...].astype(F32) + g.q_in[0].astype(F32)).astype(BF)
-    across_y = send(g.q_mid, g.q_in.at[1], g.restsem, 2, {ALONG: s + 4 - 8 * me[2]})
-    t_xb.s4()
-    t_out.s5()
+    t_z.s5()
     t_xa.s5()
-    t_z.s5()
     t_xb.s5()
     across_y.wait_recv()
     g.rest[core] = g.q_mid[...].astype(F32) + g.q_in[1].astype(F32)
@@ -1734,8 +1737,8 @@
         wacc=V((5, 8, WIDE), F32),
         gbc=V((2, ROWS, 256), BF),
         tail_rows=V((16, WIDE), F32),
-        sbc=V((LINE, BLOCK, 256), BF),
-        hbc=V((LINE, 192, 256), BF),
+        hbc=V((LINE, 192, 256), F32),
+        tbc=V((3, 192, 256), BF),
         rbc=V((3, 192, 256), BF),
         via=V((ROWS, BLOCK), BF),
         via2=V((ROWS, BLOCK), BF),
@@ -1769,7 +1772,7 @@
         small=9,
         wide=4,
         stat=3,
-        bcsem=4,
+        bcsem=7,
         restsem=4,
         bcvsem=3,
         nsem=10,

time: 173 us -> 167 us (0.965)
  Pallas kernels: 170 us -> 166 us
    pallas_call x1, Pallas kernels: 160 us -> 156 us  [fast_layer(): pl.pallas_call(kernel, out_shape=[jax.ShapeDtypeStruct(sh, dt) for sh, dt...]
where the time goes in v4:
time: 167 us; the launch traced here: 166 us
  Pallas kernels  166 us (99%)
    pallas_call x1, Pallas kernels, fast_layer(): pl.pallas_call(kernel, out_shape=[jax.ShapeDtypeStruct(sh, dt) for sh, dt...  156 us
    pallas_call x1, Pallas kernels, fast_layer(): pl.pallas_call(unpack_kernel, out_shape=[jax.ShapeDtypeStruct(sh, dt) for...  9.8 us

profile of v4, /device:TPU:0, one launch (start us, length us, event | category | flops | bytes accessed | tf_op | source)
XLA Modules:
  0.0 166.4 jit_solution(6751886466652362410)
XLA Ops:
  0.7 155.7 %layer.1 = (bf16[512,384]{1,0:T(8,128)(2,1)}, f32[512,384]{1,0:T(8,128)}, bf16[768,1536]{1,0:T(8,128)(2,1)}, bf16[1536,768]{1,0:T(8,128)(2,1)}, bf16[1536,768]{1...) custom-call(bf16[512,384]{1,0:T(8,128)(2,1)} %refs_0_.1, bf16[512,384]{1,0:T(8,128)(2,1)} %refs_1_.1, ...), custom_call_target="tpu_custom_call" | custom-call | tf_op jit(solution)/shard_map/layer/pallas_call | solution.py:1793
  156.4 9.8 %shard_map.288 = (bf16[512,384]{1,0:T(8,128)(2,1)}, f32[512,384]{1,0:T(8,128)}, f32[3,128]{1,0:T(4,128)}, f32[1536,768]{1,0:T(8,128)}, f32[1536,768]{1,0:T(8,128...) custom-call(bf16[512,384]{1,0:T(8,128)(2,1)} %get-tuple-element.39.l, ...), custom_call_target="tpu_custom_call" | custom-call | tf_op jit(solution)/shard_map/pallas_call | solution.py:1809

commit v5 on v4

--- a/solution.py
+++ b/solution.py
@@ -1104,7 +1104,8 @@
         g.part[0, at, :] = lanes_sum(gated * gated)
 
     loop(ROWS // 64, gate)
-    g.stats[z, 0:1, :] = to_row(g.part[0])
+    g.sqs[z] = to_row(g.part[0])
+    squares = [send(g.sqs.at[z], g.sqs.at[z], g.sqsem, i, p) for i, p in enumerate(zpeers)]
 
     for i in (1, 2):
         gathered(g.cotg.at[:, own], g.cotg, 5, i)
@@ -1115,7 +1116,7 @@
         g.part[1, at, :] = lanes_sum(g.ggn[at, :] * gate_gain * g.gated[at, :])
 
     loop(ROWS // 64, inner_part)
-    g.stats[z, 1:2, :] = to_row(g.part[1])
+    g.stats[z] = to_row(g.part[1])
     stat = [send(g.stats.at[z], g.stats.at[z], g.stat, i, p) for i, p in enumerate(zpeers)]
     dests = [along_line(z, a, b) for a, b in ((2, 3), (3, 0), (1, 2))]
 
@@ -1181,17 +1182,39 @@
     def out_block(k):
         return mul(g.gn[...], g.wo[:, cut(k * BLOCK, BLOCK, 128)])
 
-    for d in stat:
+    for d in squares:
         d.wait_recv()
-    sums = g.stats[0] + g.stats[1] + g.stats[2] + g.stats[3]
-    gscale = lax.rsqrt(sums[0:1] / INNER + epsilon)
+    gscale = lax.rsqrt((g.sqs[0] + g.sqs[1] + g.sqs[2] + g.sqs[3]) / INNER + epsilon)
     g.part[0] = to_col(gscale)
-    g.part[1] = to_col(gscale * gscale * gscale * sums[1:2] / INNER)
+
     @pl.when(middle)
     def _():
         for d in x_on:
             d.wait_send()
 
+    def norm_gate(i):
+        at = cut(i * 64, 64, 16)
+        g.gn[at, :] = (g.gated[at, :] * wide_of(g.part[0, at, :], 6) * gate_gain).astype(BF)
+
+    loop(ROWS // 64, norm_gate)
+    out_blocks.block(0, out_block(dests[0]))
+    out_blocks.block(1, out_block(dests[1]))
+    t_out, t_z, t_xa, t_xb = [
+        Total(ref, sum_bufs[5 * i : 5 * i + 5], g.tot_send, g.tot_recv, g.freed, 10 * i, me)
+        for i, ref in enumerate((g.p_out, g.p_z, g.p_xa, g.p_xb))
+    ]
+
+    def grad_out(n):
+        at = cut(n * 256, 256, 256)
+        g.p_out[at, :] = mul(g.gn[:, at], g.cotg[...], TN).astype(BF)
+
+    loop(3, grad_out)
+    t_out.s0()
+
+    for d in stat:
+        d.wait_recv()
+    sums = g.stats[0] + g.stats[1] + g.stats[2] + g.stats[3]
+    g.part[1] = to_col(gscale * gscale * gscale * sums / INNER)
     g.vacc[...] = jnp.zeros(g.vacc.shape, F32)
     g.pack[...] = jnp.zeros(g.pack.shape, F32)
     g.bcv[z] = jnp.zeros((8, 256), F32)
@@ -1203,7 +1226,6 @@
         vals = g.inner[at, :].astype(F32)
         mixed = g.out[at, :] + vals * skip
         gated, ggn = g.gated[at, :], g.ggn[at, :]
-        g.gn[at, :] = (gated * a * gate_gain).astype(BF)
         gg = a * (ggn * gate_gain) - gated * wide_of(g.part[1, at, :], 6)
         sig = jax.nn.sigmoid(pre)
         gm = (gg * (pre * sig)).astype(BF)
@@ -1213,36 +1235,20 @@
         g.vacc[1] += rows_sum(gm.astype(F32) * vals)
 
     loop(ROWS // 64, ungate)
-    out_blocks.block(0, out_block(dests[0]))
-    out_blocks.block(1, out_block(dests[1]))
+    t_out.s1()
 
     outer(g.ct, g.leadt, g.gm)
     g.mine_b[...] = g.local[0] + c0 * g.local[1]
     behind = Chain(g.mine_b, g.other_b, g.joined_b, g.got_b, g.chain_b, 4, -1)
     behind.share()
 
-    t_out, t_z, t_xa, t_xb = [
-        Total(ref, sum_bufs[5 * i : 5 * i + 5], g.tot_send, g.tot_recv, g.freed, 10 * i, me)
-        for i, ref in enumerate((g.p_out, g.p_z, g.p_xa, g.p_xb))
-    ]
-
-    def grad_out(n):
-        at = cut(n * 256, 256, 256)
-        g.p_out[at, :] = mul(g.gn[:, at], g.cotg[...], TN).astype(BF)
-
-    loop(3, grad_out)
-    behind.join()
-    t_out.s0()
-
     def grad_z(n):
         at = cut(n * 256, 256, 256)
         g.p_z[at, :] = mul(g.xn[:, at], g.gz[...], TN).astype(BF)
 
     loop(6, grad_z)
+    behind.join()
     t_z.s0()
-    t_out.s1()
-
-    t_z.s1()
     g.own[...] = mul(g.gn[...], g.wo[:, own])
 
     def inside_back(q, first, count):
@@ -1278,11 +1284,14 @@
         g.gb[rows, :] = mul(hi, g.c[rows, :]) + mul(lo, g.c[rows, :])
         g.gc[rows, :] = mul(hi, g.b[rows, :], TN) + mul(lo, g.b[rows, :], TN)
 
-    inside_back(1, 0, 6)
+    inside_back(1, 0, 3)
+    t_z.s1()
+    inside_back(1, 3, 3)
+    inside_back(0, 0, 6)
     arrive(both_down, -1)
     behind.meet(g.boths[1, 0:1, :])
-    inside_back(0, 0, 3)
-    inside_back(0, 3, 3)
+    out_blocks.block(2, out_block(dests[2]))
+    t_out.s2()
 
     behind.end()
     from_chips = g.chain_b[...]
@@ -1319,9 +1328,6 @@
         g.z[rows, :] = zed + loade * bg + skip * gm
         g.gb[rows, :] += sum(mul(p, glow, NT) for p in parts(vals * loade, 2))
         g.gc[rows, :] += sum(mul(p, g.slow[q], NT) for p in parts(gm * spread(g.lead[rows, :]), 2))
-        if q == 0:
-            t_out.s2()
-            out_blocks.block(2, out_block(dests[2]))
     g.pack[16:24, 0:128] = jnp.broadcast_to(
         jnp.sum(ends[0][0] + ends[1][0], axis=0, keepdims=True), (8, 128)
     )
@@ -1365,7 +1371,6 @@
         g.ret_in[...] = jnp.zeros((8, WIDE), F32)
 
     g.wacc[...] = jnp.zeros(g.wacc.shape, F32)
-    t_z.s2()
 
     def convolve_back(i):
         first = i * 64
@@ -1399,7 +1404,7 @@
             g.wacc[4, :, cols] += rows_sum(here)
 
     loop(ROWS // 64, convolve_back)
-    t_out.s3()
+    t_z.s2()
 
     @pl.when(s < SEQ - 1)
     def _():
@@ -1411,13 +1416,26 @@
         g.gbc[k, ROWS - 16 : ROWS, :] = v
 
     def bc_block(at):
-        return sum(mul(g.xn[:, at], g.gbc[k], TN) for k in range(2))
+        both = mul(g.xn[:, at], jnp.concatenate([g.gbc[0], g.gbc[1]], axis=1), TN)
+        return both[:, 0:256] + both[:, 256:512]
 
     for k in range(5):
         row = jnp.sum(g.wacc[k], axis=0, keepdims=True)
         g.pack[k : k + 1, :] = row[:, 0:CHANNELS]
         g.bcv[z, k : k + 1, :] = row[:, CHANNELS:WIDE]
     bcv = [send(g.bcv.at[z], g.bcv.at[z], g.bcvsem, i, p) for i, p in enumerate(zpeers)]
+    def grad_x(ref, first):
+        def body(n):
+            at = cut(n * 256, 256, 256)
+            ref[at, :] = mul(g.xn[:, cut(first + n * 256, 256, 256)], g.gx[...], TN).astype(BF)
+
+        loop(3, body)
+
+    grad_x(g.p_xa, 0)
+    t_xa.s0()
+    grad_x(g.p_xb, CHANNELS)
+    t_xb.s0()
+    t_out.s3()
     bcs = []
     bc_parts = [g.acc.at[pl.ds(0, BLOCK), pl.ds(WIDE + 256 * i, 256)] for i in range(3)]
     bc_parts.append(g.acc.at[pl.ds(0, BLOCK), pl.ds(BLOCK, 256)])
@@ -1426,19 +1444,8 @@
     for i in range(LINE):
         bc_parts[i][...] = bc_block(cut(lax.rem(z + 1 + i, LINE) * BLOCK, BLOCK, 128))
         halves.append(send(bc_parts[i].at[other], g.hbc.at[i], g.bcsem, 3 + i, partner))
-
-    def grad_x(ref, first):
-        def body(n):
-            at = cut(n * 256, 256, 256)
-            ref[at, :] = mul(g.xn[:, cut(first + n * 256, 256, 256)], g.gx[...], TN).astype(BF)
-
-        loop(3, body)
-
-    t_z.s3()
-    grad_x(g.p_xa, 0)
-    t_xa.s0()
-    grad_x(g.p_xb, CHANNELS)
-    t_xb.s0()
+    t_xa.s1()
+    t_xb.s1()
     for d in halves:
         d.wait_recv()
     g.bcsum[...] = bc_parts[3][mine, :] + g.hbc[3]
@@ -1452,14 +1459,13 @@
         return v + mul(g.gsr[...], g.wd[:, cut(k * BLOCK, BLOCK, 128)]) + mul(g.gbc[0], g.wbc[k], NT) + mul(g.gbc[1], g.wbc[k], NT)
 
     in_blocks.block(0, back_block(dests[0]))
-    t_xa.s1()
-    t_xb.s1()
+    t_z.s3()
+    in_blocks.block(1, back_block(dests[1]))
     t_out.s4()
-    in_blocks.block(1, back_block(dests[1]))
     g.own_in[...] = back_block(z)
     t_xa.s2()
+    t_xb.s2()
     t_z.s4()
-    t_xb.s2()
 
     for d in bcs + bcv:
         d.wait_recv()
@@ -1584,9 +1590,9 @@
 
 
 def unpack_kernel(
-    layer_hbm, in_hbm, out_low, z_low, x_low, rest, gain_sum,
+    layer_hbm, in_hbm, out_low, z_low, x_low, rest_hbm, gain_sum,
     layer_out, grad_in, gain, w_z, w_x, w_bc, w_dt, conv_x_w, conv_x_b, conv_bc_w, conv_bc_b, dt_bias, a_log, d_skip, gate_gain, w_out,
-    low_a, low_b, low_c, full_a, full_b, full_c, keep_a, keep_b, in_sem, out_sem,
+    low_a, low_b, low_c, full_a, full_b, full_c, keep_a, keep_b, rest, bc_rows, in_sem, out_sem,
 ):
     steps = 6
     mats = [(out_low, low_a, full_a, w_out), (z_low, low_b, full_b, w_z), (x_low, low_c, full_c, w_x)]
@@ -1596,14 +1602,29 @@
         for i in range(steps):
             at = pl.ds(i * n, n)
             loads.append(pltpu.make_async_copy(src.at[at], low.at[at], in_sem.at[steps * m + i]))
-    for i, (src, dst) in enumerate([(layer_hbm, keep_a), (in_hbm, keep_b)]):
+    for i, (src, dst) in enumerate([(layer_hbm, keep_a), (in_hbm, keep_b), (rest_hbm, rest)]):
         loads.append(pltpu.make_async_copy(src, dst, in_sem.at[18 + i]))
     for d in loads:
         d.start()
+    for m, (_, low, full, dst) in enumerate(mats):
+        n = low.shape[0] // steps
+        for i in range(steps):
+            loads[steps * m + i].wait()
+            at = pl.ds(i * n, n)
+            full[at, :] = low[at, :].astype(F32)
+            stores.append(pltpu.make_async_copy(full.at[at], dst.at[at], out_sem.at[steps * m + i]))
+            stores[-1].start()
+    for i, (src, dst) in enumerate([(keep_a, layer_out), (keep_b, grad_in)]):
+        loads[18 + i].wait()
+        stores.append(pltpu.make_async_copy(src, dst, out_sem.at[18 + i]))
+        stores[-1].start()
+    loads[20].wait()
     for n in range(3):
         gain[n : n + 1, :] = gain_sum[0:1, 128 * n : 128 * n + 128]
-    w_bc[0:192, :] = rest[0, 0:192, :]
-    w_bc[192:BLOCK, :] = rest[1, 0:192, :]
+    bc_rows[0:192, :] = rest[0, 0:192, :]
+    bc_rows[192:BLOCK, :] = rest[1, 0:192, :]
+    stores.append(pltpu.make_async_copy(bc_rows, w_bc, out_sem.at[20]))
+    stores[-1].start()
     for n in range(6):
         w_dt[:, 256 * n : 256 * n + 256] = rest[0, 192 + 16 * n : 204 + 16 * n, :]
     for n in range(3):
@@ -1619,18 +1640,6 @@
     dt_bias[...] = rest[1, 208:209, 0:12]
     a_log[...] = rest[1, 208:209, 128:140]
     d_skip[...] = rest[1, 232:233, 0:12]
-    for m, (_, low, full, dst) in enumerate(mats):
-        n = low.shape[0] // steps
-        for i in range(steps):
-            loads[steps * m + i].wait()
-            at = pl.ds(i * n, n)
-            full[at, :] = low[at, :].astype(F32)
-            stores.append(pltpu.make_async_copy(full.at[at], dst.at[at], out_sem.at[steps * m + i]))
-            stores[-1].start()
-    for i, (src, dst) in enumerate([(keep_a, layer_out), (keep_b, grad_in)]):
-        loads[18 + i].wait()
-        stores.append(pltpu.make_async_copy(src, dst, out_sem.at[18 + i]))
-        stores[-1].start()
     for d in stores:
         d.wait()
 
@@ -1723,7 +1732,8 @@
         slow=V((2, STATE, CHANNELS), BF),
         gated=V((ROWS, CHANNELS), F32),
         part=V((2, ROWS, 128), F32),
-        stats=V((LINE, 2, ROWS), F32),
+        stats=V((LINE, 1, ROWS), F32),
+        sqs=V((LINE, 1, ROWS), F32),
         vacc=V((2, 8, CHANNELS), F32),
         gm=V((ROWS, CHANNELS), BF),
         gloc=V((2, STATE, CHANNELS), F32),
@@ -1772,6 +1782,7 @@
         small=9,
         wide=4,
         stat=3,
+        sqsem=3,
         bcsem=7,
         restsem=4,
         bcvsem=3,
@@ -1802,19 +1813,19 @@
     layer_out, grad_in, grad_out, grad_z, grad_x, rest, grad_gain = res
     shapes = dict(
         layer_out=((ROWS, BLOCK), BF, hbm), grad_in=((ROWS, BLOCK), F32, hbm), gain=((3, 128), F32, vm), w_z=((D, CHANNELS), F32, hbm),
-        w_x=((D, CHANNELS), F32, hbm), w_bc=((BLOCK, 256), F32, vm), w_dt=((12, D), F32, vm), conv_x_w=((4, CHANNELS), F32, vm),
+        w_x=((D, CHANNELS), F32, hbm), w_bc=((BLOCK, 256), F32, hbm), w_dt=((12, D), F32, vm), conv_x_w=((4, CHANNELS), F32, vm),
         conv_x_b=((6, 128), F32, vm), conv_bc_w=((4, 256), F32, vm), conv_bc_b=((2, 128), F32, vm), dt_bias=((1, 12), F32, vm),
         a_log=((1, 12), F32, vm), d_skip=((1, 12), F32, vm), gate_gain=((6, 128), F32, vm), w_out=((CHANNELS, D), F32, hbm),
     )
     final = pl.pallas_call(
         unpack_kernel,
         out_shape=[jax.ShapeDtypeStruct(sh, dt) for sh, dt, _ in shapes.values()],
-        in_specs=[hbm] * 5 + [vm] * 2,
+        in_specs=[hbm] * 6 + [vm],
         out_specs=[sp for _, _, sp in shapes.values()],
         scratch_shapes=[
             V((CHANNELS, D), BF), V((D, CHANNELS), BF), V((D, CHANNELS), BF),
             V((CHANNELS, D), F32), V((D, CHANNELS), F32), V((D, CHANNELS), F32),
-            V((ROWS, BLOCK), BF), V((ROWS, BLOCK), F32), S((20,)), S((20,)),
+            V((ROWS, BLOCK), BF), V((ROWS, BLOCK), F32), V((2, 288, 256), F32), V((BLOCK, 256), F32), S((21,)), S((21,)),
         ],
         compiler_params=pltpu.CompilerParams(vmem_limit_bytes=63 * 2**20),
     )(layer_out, grad_in, grad_out, grad_z, grad_x, rest, grad_gain)

time: 167 us -> 165 us (0.988)
  Pallas kernels: 166 us -> 164 us
where the time goes in v5:
time: 165 us
  Pallas kernels  164 us (99%)
    pallas_call x1, Pallas kernels, fast_layer(): pl.pallas_call(kernel, out_shape=[jax.ShapeDtypeStruct(sh, dt) for sh, dt...  154 us
    pallas_call x1, Pallas kernels, fast_layer(): pl.pallas_call(unpack_kernel, out_shape=[jax.ShapeDtypeStruct(sh, dt) for...  9.72 us

profile of v5, /device:TPU:0, one launch (start us, length us, event | category | flops | bytes accessed | tf_op | source)
XLA Modules:
  0.0 164.8 jit_solution(12727579745562879555)
XLA Ops:
  0.7 154.3 %layer.1 = (bf16[512,384]{1,0:T(8,128)(2,1)}, f32[512,384]{1,0:T(8,128)}, bf16[768,1536]{1,0:T(8,128)(2,1)}, bf16[1536,768]{1,0:T(8,128)(2,1)}, bf16[1536,768]{1...) custom-call(bf16[512,384]{1,0:T(8,128)(2,1)} %refs_0_.1, bf16[512,384]{1,0:T(8,128)(2,1)} %refs_1_.1, ...), custom_call_target="tpu_custom_call" | custom-call | tf_op jit(solution)/shard_map/layer/pallas_call | solution.py:1804
  154.9 9.7 %shard_map.288 = (bf16[512,384]{1,0:T(8,128)(2,1)}, f32[512,384]{1,0:T(8,128)}, f32[3,128]{1,0:T(4,128)}, f32[1536,768]{1,0:T(8,128)}, f32[1536,768]{1,0:T(8,128...) custom-call(bf16[512,384]{1,0:T(8,128)(2,1)} %get-tuple-element.39.l, ...), custom_call_target="tpu_custom_call" | custom-call | tf_op jit(solution)/shard_map/pallas_call | solution.py:1820

commit v6 on v5

--- a/solution.py
+++ b/solution.py
@@ -940,11 +940,12 @@
     later = []
 
     class Chain:
-        def __init__(self, mine, other, joined, got, result, base, way):
+        def __init__(self, mine, other, joined, far, got, result, base, way):
             self.mine, self.other, self.joined, self.got, self.result = mine, other, joined, got, result
             self.base, self.way = base, way
-            self.near = self.link(joined, got.at[0], 1, way)
-            self.far = self.link(joined, got.at[1], 2, 2 * way)
+            self.near = self.link(joined, got, 1, way)
+            self.far_from, self.far_to = far
+            self.far = self.link(self.far_from, self.far_to, 2, 2 * way)
 
         def link(self, src, dst, i, hop):
             to = {ALONG: s + 2 * hop}
@@ -961,19 +962,21 @@
                 self.joined[...] = odd_decay() * even + odd
             else:
                 self.joined[...] = even + even_decay() * odd
+            if self.far_from is not self.joined:
+                self.far_from[...] = self.joined[...].astype(BF)
             for d, hop in ((self.near, 1), (self.far, 2)):
                 pass_on(d, hop * self.way)
-            for i, hop in ((0, 1), (1, 2)):
+            for to, hop in ((self.got, 1), (self.far_to, 2)):
                 outside = chip - hop * self.way
 
                 @pl.when((outside < 0) | (outside > 3))
                 def _():
-                    self.got[i] = jnp.zeros((STATE, BLOCK), F32)
+                    to[...] = jnp.zeros((STATE, BLOCK), to.dtype)
 
         def meet(self, decay):
             for d, hop in ((self.near, 1), (self.far, 2)):
                 arrive(d, hop * self.way)
-            self.result[:, half] = self.got[0] + decay * self.got[1]
+            self.result[:, half] = self.got[...] + decay * self.far_to[...].astype(F32)
             p = self.result.at[:, half]
             self.last = send(p, p, (g.st_send, g.st_recv), self.base + 3, partner)
 
@@ -1001,7 +1004,7 @@
         return jnp.where(core == 0, g.decay[0, 0:1, half], g.decay[1, 0:1, half])
 
     g.mine[...] = c1 * g.local[0] + g.local[1]
-    ahead = Chain(g.mine, g.other, g.joined, g.got, g.chain, 0, 1)
+    ahead = Chain(g.mine, g.other, g.joined, (g.joined, g.got.at[1]), g.got.at[0], g.chain, 0, 1)
     ahead.share()
     dec = send(g.decay.at[0], g.decay.at[1], (g.st_send, g.st_recv), 8, partner)
     both_up = remote(g.both, g.boths.at[0], g.st_send.at[9], g.st_recv.at[9], {ALONG: s + 2})
@@ -1239,7 +1242,7 @@
 
     outer(g.ct, g.leadt, g.gm)
     g.mine_b[...] = g.local[0] + c0 * g.local[1]
-    behind = Chain(g.mine_b, g.other_b, g.joined_b, g.got_b, g.chain_b, 4, -1)
+    behind = Chain(g.mine_b, g.other_b, g.joined_b, (g.low_b, g.far_b), g.got_b, g.chain_b, 4, -1)
     behind.share()
 
     def grad_z(n):
@@ -1284,10 +1287,9 @@
         g.gb[rows, :] = mul(hi, g.c[rows, :]) + mul(lo, g.c[rows, :])
         g.gc[rows, :] = mul(hi, g.b[rows, :], TN) + mul(lo, g.b[rows, :], TN)
 
-    inside_back(1, 0, 3)
+    inside_back(1, 0, 6)
+    inside_back(0, 0, 6)
     t_z.s1()
-    inside_back(1, 3, 3)
-    inside_back(0, 0, 6)
     arrive(both_down, -1)
     behind.meet(g.boths[1, 0:1, :])
     out_blocks.block(2, out_block(dests[2]))
@@ -1594,7 +1596,7 @@
     layer_out, grad_in, gain, w_z, w_x, w_bc, w_dt, conv_x_w, conv_x_b, conv_bc_w, conv_bc_b, dt_bias, a_log, d_skip, gate_gain, w_out,
     low_a, low_b, low_c, full_a, full_b, full_c, keep_a, keep_b, rest, bc_rows, in_sem, out_sem,
 ):
-    steps = 6
+    steps = 3
     mats = [(out_low, low_a, full_a, w_out), (z_low, low_b, full_b, w_z), (x_low, low_c, full_c, w_x)]
     loads, stores = [], []
     for m, (src, low, _, _) in enumerate(mats):
@@ -1603,7 +1605,7 @@
             at = pl.ds(i * n, n)
             loads.append(pltpu.make_async_copy(src.at[at], low.at[at], in_sem.at[steps * m + i]))
     for i, (src, dst) in enumerate([(layer_hbm, keep_a), (in_hbm, keep_b), (rest_hbm, rest)]):
-        loads.append(pltpu.make_async_copy(src, dst, in_sem.at[18 + i]))
+        loads.append(pltpu.make_async_copy(src, dst, in_sem.at[9 + i]))
     for d in loads:
         d.start()
     for m, (_, low, full, dst) in enumerate(mats):
@@ -1615,15 +1617,15 @@
             stores.append(pltpu.make_async_copy(full.at[at], dst.at[at], out_sem.at[steps * m + i]))
             stores[-1].start()
     for i, (src, dst) in enumerate([(keep_a, layer_out), (keep_b, grad_in)]):
-        loads[18 + i].wait()
-        stores.append(pltpu.make_async_copy(src, dst, out_sem.at[18 + i]))
+        loads[9 + i].wait()
+        stores.append(pltpu.make_async_copy(src, dst, out_sem.at[9 + i]))
         stores[-1].start()
-    loads[20].wait()
+    loads[11].wait()
     for n in range(3):
         gain[n : n + 1, :] = gain_sum[0:1, 128 * n : 128 * n + 128]
     bc_rows[0:192, :] = rest[0, 0:192, :]
     bc_rows[192:BLOCK, :] = rest[1, 0:192, :]
-    stores.append(pltpu.make_async_copy(bc_rows, w_bc, out_sem.at[20]))
+    stores.append(pltpu.make_async_copy(bc_rows, w_bc, out_sem.at[11]))
     stores[-1].start()
     for n in range(6):
         w_dt[:, 256 * n : 256 * n + 256] = rest[0, 192 + 16 * n : 204 + 16 * n, :]
@@ -1721,7 +1723,9 @@
         mine_b=V((STATE, CHANNELS), F32),
         other_b=V((STATE, CHANNELS), F32),
         joined_b=V((STATE, BLOCK), F32),
-        got_b=V((2, STATE, BLOCK), F32),
+        got_b=V((STATE, BLOCK), F32),
+        low_b=V((STATE, BLOCK), BF),
+        far_b=V((STATE, BLOCK), BF),
         chain_b=V((STATE, CHANNELS), F32),
         both=V((8, BLOCK), F32),
         boths=V((2, 8, BLOCK), F32),
@@ -1825,7 +1829,7 @@
         scratch_shapes=[
             V((CHANNELS, D), BF), V((D, CHANNELS), BF), V((D, CHANNELS), BF),
             V((CHANNELS, D), F32), V((D, CHANNELS), F32), V((D, CHANNELS), F32),
-            V((ROWS, BLOCK), BF), V((ROWS, BLOCK), F32), V((2, 288, 256), F32), V((BLOCK, 256), F32), S((21,)), S((21,)),
+            V((ROWS, BLOCK), BF), V((ROWS, BLOCK), F32), V((2, 288, 256), F32), V((BLOCK, 256), F32), S((12,)), S((12,)),
         ],
         compiler_params=pltpu.CompilerParams(vmem_limit_bytes=63 * 2**20),
     )(layer_out, grad_in, grad_out, grad_z, grad_x, rest, grad_gain)

time: 165 us -> 164 us (level)
  no operation moved by 1% of the time
where the time goes in v6:
time: 164 us
  Pallas kernels  163 us (99%)
    pallas_call x1, Pallas kernels, fast_layer(): pl.pallas_call(kernel, out_shape=[jax.ShapeDtypeStruct(sh, dt) for sh, dt...  154 us
    pallas_call x1, Pallas kernels, fast_layer(): pl.pallas_call(unpack_kernel, out_shape=[jax.ShapeDtypeStruct(sh, dt) for...  9.36 us

profile of v6, /device:TPU:0, one launch (start us, length us, event | category | flops | bytes accessed | tf_op | source)
XLA Modules:
  0.0 164.0 jit_solution(17363394201535455419)
XLA Ops:
  0.7 153.8 %layer.1 = (bf16[512,384]{1,0:T(8,128)(2,1)}, f32[512,384]{1,0:T(8,128)}, bf16[768,1536]{1,0:T(8,128)(2,1)}, bf16[1536,768]{1,0:T(8,128)(2,1)}, bf16[1536,768]{1...) custom-call(bf16[512,384]{1,0:T(8,128)(2,1)} %refs_0_.1, bf16[512,384]{1,0:T(8,128)(2,1)} %refs_1_.1, ...), custom_call_target="tpu_custom_call" | custom-call | tf_op jit(solution)/shard_map/layer/pallas_call | solution.py:1808
  154.4 9.4 %shard_map.288 = (bf16[512,384]{1,0:T(8,128)(2,1)}, f32[512,384]{1,0:T(8,128)}, f32[3,128]{1,0:T(4,128)}, f32[1536,768]{1,0:T(8,128)}, f32[1536,768]{1,0:T(8,128...) custom-call(bf16[512,384]{1,0:T(8,128)(2,1)} %get-tuple-element.39.l, ...), custom_call_target="tpu_custom_call" | custom-call | tf_op jit(solution)/shard_map/pallas_call | solution.py:1824
